TPU v7x, 512 devices: a whole 4x8x8 slice. The times are simulated.
512 devices in a mesh: frame: 16 (over z_hi, x), tile: 32 (over y, z_lo, core).
Axes of the slice: x: 4, y: 8, z: 8 (z_hi: 4, z_lo: 2; z = z_hi * 2 + z_lo), core: 2. Of those that a mesh axis runs over, the one named last changes fastest.
Arguments:
- saved_codes: bfloat16 [32, 128, 32, 128], P('frame', 'tile'), may hold values from -1 to 1
- saved_scales: float32 [32, 128, 32], P('frame', 'tile'), may hold values from 0.5 to 2.5
- kernels: bfloat16 [2, 27, 128, 128], replicated, may hold values from -0.109375 to 0.109375
- norm_gains: float32 [2, 128], replicated, may hold values from 0.25 to 1.75
- cotangent: bfloat16 [32, 128, 32, 128], P('frame', 'tile'), may hold values from -13 to 13
Outputs:
- input_grad: bfloat16 [32, 128, 32, 128], P('frame', 'tile')
- kernel_grads: float32 [54, 128, 128], P(None, 'tile', 'frame')
All inputs are finite; a program needn't handle non-finite values.
Results may differ from a plain program's by a relative error of at most 0.028.
Values may be sent and summed in bfloat16 or wider, within the bound.
No kernel may reach another device: no remote copies, remote signals or barrier semaphores. Data moves between devices by JAX's collectives and lax.ppermute only.
A program may use at most 64 MiB of HBM per device.

v0:
```python
import math

import jax
import jax.numpy as jnp
from jax import lax
from jax.sharding import PartitionSpec as P

EPS = 1e-06


def with_halo(cells, sides, width):
    for axis, dim in sides:
        count = lax.axis_size(axis)
        ends = count - 1
        head = lax.slice_in_dim(cells, 0, width, axis=dim)
        tail = lax.slice_in_dim(cells, cells.shape[dim] - width, cells.shape[dim], axis=dim)
        cells = jnp.concatenate(
            [
                lax.ppermute(tail, axis, [(i, (i + 1) % count) for i in range(ends)]),
                cells,
                lax.ppermute(head, axis, [((i + 1) % count, i) for i in range(ends)]),
            ],
            axis=dim,
        )
    return cells


def from_behind(value, axis, steps):
    count = lax.axis_size(axis)
    first, last = (max(0, -steps), min(count, count - steps))
    return lax.ppermute(value, axis, [(source, source + steps) for source in range(first, last)])


def split_up(shard, dim, size):
    lengths = shard.shape
    blocks = shard.reshape(*lengths[:dim], size, lengths[dim] // size, *lengths[dim + 1 :])
    return jnp.moveaxis(blocks, dim, 0)


def sent_and_summed(shard, axis, dim):
    blocks = split_up(shard, dim, lax.axis_size(axis))
    arrived = lax.all_to_all(blocks, axis, split_axis=0, concat_axis=0, tiled=True)
    return arrived.astype(jnp.float32).sum(axis=0)


def patches(extended, frames, rows, columns, offset, sign):
    pieces = []
    for depth in range(3):
        for down in range(3):
            for across in range(3):
                first_frame = offset + sign * depth
                first_row = 1 + sign * (down - 1) + (offset - 2 * (sign < 0) * 0) * 0
                first_col = 1 + sign * (across - 1)
                pieces.append(
                    extended[
                        first_frame : first_frame + frames,
                        first_row : first_row + rows,
                        first_col : first_col + columns,
                    ]
                )
    joined = jnp.concatenate(pieces, axis=-1)
    return joined.reshape(frames * rows * columns, joined.shape[-1])


def pad_columns(block):
    return jnp.pad(block, ((0, 0), (0, 0), (1, 1), (0, 0)))


def extend_input(layer_in):
    own_rows = with_halo(layer_in, (("tile", 1),), 1)
    earlier = from_behind(own_rows, "frame", 1)
    widened = jnp.concatenate([earlier, own_rows], axis=0)
    return pad_columns(widened)


def extend_cotangent(pre_grad):
    later = from_behind(pre_grad, "frame", -1)
    joined = jnp.concatenate([pre_grad, later], axis=0)
    widened = with_halo(joined, (("tile", 1),), 1)
    return pad_columns(widened)


def local(saved_codes, saved_scales, kernels, norm_gains, cotangent):
    frames, rows, columns, channels = saved_codes.shape
    layer_count = kernels.shape[0]
    cells = frames * rows * columns
    layer_in = (saved_codes.astype(jnp.float32) * saved_scales[..., None]).astype(jnp.bfloat16)
    extended_list = []
    states = []
    for layer in range(layer_count):
        extended = extend_input(layer_in)
        extended_list.append(extended)
        columns_in = patches(extended, frames, rows, columns, 0, 1)
        forward_kernel = kernels[layer].reshape(27 * channels, channels)
        pre_norm = jnp.dot(columns_in, forward_kernel, preferred_element_type=jnp.float32)
        inverse = lax.rsqrt(jnp.mean(pre_norm * pre_norm, axis=-1, keepdims=True) + EPS)
        normed = pre_norm * inverse * norm_gains[layer]
        states.append((pre_norm, inverse, normed))
        if layer + 1 < layer_count:
            layer_in = (
                jax.nn.silu(normed).astype(jnp.bfloat16).reshape(frames, rows, columns, channels)
            )
    upstream = cotangent.reshape(cells, channels)
    grads_list = [None] * layer_count
    for layer in reversed(range(layer_count)):
        pre_norm, inverse, normed = states[layer]
        sigma = jax.nn.sigmoid(normed)
        scaled = (
            norm_gains[layer]
            * upstream.astype(jnp.float32)
            * sigma
            * (1.0 + normed * (1.0 - sigma))
        )
        mixed = jnp.mean(pre_norm * scaled, axis=-1, keepdims=True)
        pre_grad = (inverse * scaled - pre_norm * inverse**3 * mixed).astype(jnp.bfloat16)
        columns_in = patches(extended_list[layer], frames, rows, columns, 0, 1)
        kernel_part = lax.dot_general(
            columns_in, pre_grad, (((0,), (0,)), ((), ())), preferred_element_type=jnp.float32
        )
        grads_list[layer] = kernel_part.reshape(27, channels, channels)
        spread_grad = extend_cotangent(pre_grad.reshape(frames, rows, columns, channels))
        columns_back = patches(spread_grad, frames, rows, columns, 2, -1)
        back_kernel = jnp.transpose(kernels[layer], (0, 2, 1)).reshape(27 * channels, channels)
        upstream = jnp.dot(columns_back, back_kernel, preferred_element_type=jnp.float32).astype(
            jnp.bfloat16
        )
    input_grad = upstream.reshape(frames, rows, columns, channels)
    stacked = jnp.concatenate(grads_list, axis=0)
    partial_sum = sent_and_summed(stacked.astype(jnp.bfloat16), "tile", 1)
    summed = sent_and_summed(partial_sum.astype(jnp.bfloat16), "frame", 2)
    total_cells = cells * lax.axis_size("frame") * lax.axis_size("tile")
    kernel_grads = summed / jnp.float32(math.sqrt(total_cells))
    return (input_grad, kernel_grads)


def solution(mesh):
    in_specs = (
        P("frame", "tile", None, None),
        P("frame", "tile", None),
        P(),
        P(),
        P("frame", "tile", None, None),
    )
    out_specs = (P("frame", "tile", None, None), P(None, "tile", "frame"))
    return jax.shard_map(local, mesh=mesh, in_specs=in_specs, out_specs=out_specs, check_vma=False)
```

profile of v0, /device:TPU:40, one launch (start us, length us, event | category | flops | bytes accessed | tf_op | source)
XLA Modules:
  0.0 178.6 jit_solution(5098679651175532246)
XLA Ops:
  0.6 0.9 multiply_convert_fusion.1
  1.6 1.9 %collective-permute-start = (bf16[2,1,32,128]{3,2,1,0:T(8,128)(2,1)S(1)}, bf16[2,1,32,128]{3,2,1,0:T(8,128)(2,1)S(1)}, u32[]{:S(2)}, u32[]{:S(2)}) collective-permute-start(bf16[2,1,32,128]{3,2,1,0:T(8,128)(2,1)S(1)} %get-tuple-element.90), channel_id=1, source_target_pairs={{0,1},{1,2},{2,3},{3,4},{4,5},{5,6},{6,7},{7,8},{8,9},{9,10},{10,1... | collective-permute-start | bytes 49160 | tf_op jit(solution)/shard_map/ppermute | solution.py:19
  3.5 4.5 %collective-permute-start.1 = (bf16[2,1,32,128]{3,2,1,0:T(8,128)(2,1)S(1)}, bf16[2,1,32,128]{3,2,1,0:T(8,128)(2,1)S(1)}, u32[]{:S(2)}, u32[]{:S(2)}) collective-permute-start(bf16[2,1,32,128]{3,2,1,0:T(8,128)(2,1)S(1)} %get-tuple-element.91), channel_id=1, source_target_pairs={{1,0},{2,1},{3,2},{4,3},{5,4},{6,5},{7,6},{8,7},{9,8},{10,9},{11,1... | collective-permute-start | bytes 49160 | tf_op jit(solution)/shard_map/ppermute | solution.py:21
  8.1 3.2 %slice_bitcast_fusion.3 = (bf16[27,128,128]{1,2,0:T(8,128)(2,1)S(1)}, bf16[27,128,128]{1,2,0:T(8,128)(2,1)S(1)}, bf16[1,27,128,128]{3,2,1,0:T(8,128)(2,1)}, bf16[1,27,128,128]{3,2,1,0:T(8,128)(2,1)S(1)}) fusion(bf16[2,27,128,128]{3,2,1,0:T(8,128)(2,1)} %param.7), kind=kLoop, calls=%fused_computation.216 | loop fusion | bytes 5308416 | tf_op jit(solution)/shard_map/transpose | solution.py:123
  11.3 3.4 %collective-permute-start.2 = (bf16[2,6,32,128]{3,2,1,0:T(8,128)(2,1)S(1)}, bf16[2,6,32,128]{3,2,1,0:T(8,128)(2,1)S(1)}, u32[]{:S(2)}, u32[]{:S(2)}) collective-permute-start(bf16[2,6,32,128]{3,2,1,0:T(8,128)(2,1)S(1)} %pad_maximum_fusion.2), channel_id=1, source_target_pairs={{0,32},{32,64},{64,96},{96,128},{128,160},{160,192},{192,224},{224... | collective-permute-start | bytes 294920 | tf_op jit(solution)/shard_map/ppermute | solution.py:31
  15.3 1.6 collective-permute-done.2
  18.2 0.7 multiply_reduce_fusion.3
  21.0 1.9 %collective-permute-start.3 = (bf16[2,1,32,128]{3,2,1,0:T(8,128)(2,1)}, bf16[2,1,32,128]{3,2,1,0:T(8,128)(2,1)S(1)}, u32[]{:S(2)}, u32[]{:S(2)}) collective-permute-start(bf16[2,1,32,128]{3,2,1,0:T(8,128)(2,1)} %get-tuple-element.88), channel_id=1, source_target_pairs={{0,1},{1,2},{2,3},{3,4},{4,5},{5,6},{6,7},{7,8},{8,9},{9,10},{10,1... | collective-permute-start | bytes 49160 | tf_op jit(solution)/shard_map/ppermute | solution.py:19
  22.9 4.5 %collective-permute-start.4 = (bf16[2,1,32,128]{3,2,1,0:T(8,128)(2,1)}, bf16[2,1,32,128]{3,2,1,0:T(8,128)(2,1)}, u32[]{:S(2)}, u32[]{:S(2)}) collective-permute-start(bf16[2,1,32,128]{3,2,1,0:T(8,128)(2,1)} %get-tuple-element.89), channel_id=1, source_target_pairs={{1,0},{2,1},{3,2},{4,3},{5,4},{6,5},{7,6},{8,7},{9,8},{10,9},{11,1... | collective-permute-start | bytes 49160 | tf_op jit(solution)/shard_map/ppermute | solution.py:21
  27.5 1.7 copy.21
  29.1 1.6 copy.20
  30.8 0.9 copy.22
  31.7 1.9 %dot_general.31 = bf16[27,32,4,256]{3,2,1,0:T(4,128)(2,1)} reshape(bf16[3456,256]{1,0:T(8,128)(2,1)S(1)} %bitcast.137) | data formatting | bytes 3538944 | tf_op jit(solution)/shard_map/dot_general | solution.py:117
  33.6 0.7 pad_maximum_fusion.3
  34.4 4.3 %collective-permute-start.5 = (bf16[2,6,32,128]{3,2,1,0:T(8,128)(2,1)S(1)}, bf16[2,6,32,128]{3,2,1,0:T(8,128)(2,1)S(1)}, u32[]{:S(2)}, u32[]{:S(2)}) collective-permute-start(bf16[2,6,32,128]{3,2,1,0:T(8,128)(2,1)S(1)} %pad_maximum_fusion.3), channel_id=1, source_target_pairs={{0,32},{32,64},{64,96},{96,128},{128,160},{160,192},{192,224},{224... | collective-permute-start | bytes 294920 | tf_op jit(solution)/shard_map/ppermute | solution.py:31
  38.7 0.7 pad_maximum_fusion.6
  39.4 1.5 collective-permute-done.5
  40.9 0.7 maximum_maximum_fusion.1
  43.2 1.3 multiply_reduce_fusion.2
  44.5 0.9 copy.24
  46.0 1.1 multiply_reduce_fusion.1
  47.2 1.1 subtract_convert_fusion.1
  48.2 1.3 collective-permute-start.6
  50.2 4.6 %collective-permute-done.6 = bf16[2,4,32,128]{3,2,1,0:T(8,128)(2,1)S(1)} collective-permute-done((bf16[2,4,32,128]{3,2,1,0:T(8,128)(2,1)S(1)}, bf16[2,4,32,128]{3,2,1,0:T(8,128)(2,1)S(1)}, u32[]{:S(2)}, u32[]{:S(2)}) %collective-permute-start.6) | collective-permute-done | bytes 65568 | tf_op jit(solution)/shard_map/ppermute | solution.py:31
  54.8 1.9 %collective-permute-start.7 = (bf16[4,1,32,128]{3,2,1,0:T(8,128)(2,1)S(1)}, bf16[4,1,32,128]{3,2,1,0:T(8,128)(2,1)S(1)}, u32[]{:S(2)}, u32[]{:S(2)}) collective-permute-start(bf16[4,1,32,128]{3,2,1,0:T(8,128)(2,1)S(1)} %get-tuple-element.81), channel_id=1, source_target_pairs={{0,1},{1,2},{2,3},{3,4},{4,5},{5,6},{6,7},{7,8},{8,9},{9,10},{10,1... | collective-permute-start | bytes 98312 | tf_op jit(solution)/shard_map/ppermute | solution.py:19
  56.7 4.5 %collective-permute-start.8 = (bf16[4,1,32,128]{3,2,1,0:T(8,128)(2,1)S(1)}, bf16[4,1,32,128]{3,2,1,0:T(8,128)(2,1)S(1)}, u32[]{:S(2)}, u32[]{:S(2)}) collective-permute-start(bf16[4,1,32,128]{3,2,1,0:T(8,128)(2,1)S(1)} %get-tuple-element.82), channel_id=1, source_target_pairs={{1,0},{2,1},{3,2},{4,3},{5,4},{6,5},{7,6},{8,7},{9,8},{10,9},{11,1... | collective-permute-start | bytes 98312 | tf_op jit(solution)/shard_map/ppermute | solution.py:21
  61.3 1.5 collective-permute-done.8
  64.5 0.7 multiply_reduce_fusion
  66.6 1.3 collective-permute-start.9
  68.0 2.2 %copy.26 = bf16[32,54,4,128]{3,2,1,0:T(4,128)(2,1)} copy(bf16[32,54,4,128]{3,0,2,1:T(8,128)(2,1)S(1)} %maximum_bitcast_fusion) | data formatting | bytes 3538944 | tf_op jit(solution)/shard_map/transpose | solution.py:37
  70.2 12.1 %all-to-all-start = ((bf16[32,54,4,128]{3,2,1,0:T(4,128)(2,1)}), bf16[32,54,4,128]{3,2,1,0:T(4,128)(2,1)S(1)}, u32[]{:S(2)}, u32[]{:S(2)}) async-start(bf16[32,54,4,128]{3,2,1,0:T(4,128)(2,1)} %copy.26), calls=%async_computation | async-start | bytes 3538944 | tf_op jit(solution)/shard_map/all_to_all | solution.py:42
  82.3 2.0 %collective-permute-start.10 = (bf16[4,1,32,128]{3,2,1,0:T(8,128)(2,1)S(1)}, bf16[4,1,32,128]{3,2,1,0:T(8,128)(2,1)S(1)}, u32[]{:S(2)}, u32[]{:S(2)}) collective-permute-start(bf16[4,1,32,128]{3,2,1,0:T(8,128)(2,1)S(1)} %get-tuple-element.77), channel_id=1, source_target_pairs={{0,1},{1,2},{2,3},{3,4},{4,5},{5,6},{6,7},{7,8},{8,9},{9,10},{10,1... | collective-permute-start | bytes 98312 | tf_op jit(solution)/shard_map/ppermute | solution.py:19
  84.4 4.6 %collective-permute-start.11 = (bf16[4,1,32,128]{3,2,1,0:T(8,128)(2,1)S(1)}, bf16[4,1,32,128]{3,2,1,0:T(8,128)(2,1)S(1)}, u32[]{:S(2)}, u32[]{:S(2)}) collective-permute-start(bf16[4,1,32,128]{3,2,1,0:T(8,128)(2,1)S(1)} %get-tuple-element.78), channel_id=1, source_target_pairs={{1,0},{2,1},{3,2},{4,3},{5,4},{6,5},{7,6},{8,7},{9,8},{10,9},{11,1... | collective-permute-start | bytes 98312 | tf_op jit(solution)/shard_map/ppermute | solution.py:21
  89.0 35.0 %collective-permute-done.10 = bf16[4,1,32,128]{3,2,1,0:T(8,128)(2,1)S(1)} collective-permute-done((bf16[4,1,32,128]{3,2,1,0:T(8,128)(2,1)S(1)}, bf16[4,1,32,128]{3,2,1,0:T(8,128)(2,1)S(1)}, u32[]{:S(2)}, u32[]{:S(2)}) %collective-permute-start.10) | collective-permute-done | bytes 32800 | tf_op jit(solution)/shard_map/ppermute | solution.py:19
  128.2 0.7 constant_dynamic-update-slice_fusion.101
  129.5 0.7 constant_dynamic-update-slice_fusion.99
  131.5 0.7 constant_dynamic-update-slice_fusion.96
  132.1 0.7 constant_dynamic-update-slice_fusion.95
  134.1 0.7 constant_dynamic-update-slice_fusion.92
  136.7 0.7 constant_dynamic-update-slice_fusion.88
  137.3 0.7 constant_dynamic-update-slice_fusion.87
  138.0 0.7 constant_dynamic-update-slice_fusion.86
  140.6 0.7 constant_dynamic-update-slice_fusion.82
  141.9 0.8 reduce_sum.61
  142.9 0.8 reshape.179
  143.7 23.9 %all-to-all-start.1 = ((bf16[16,2,864]{2,1,0:T(2,128)(2,1)}), bf16[16,2,864]{2,1,0:T(2,128)(2,1)S(1)}, u32[]{:S(2)}, u32[]{:S(2)}) async-start(bf16[16,2,864]{2,1,0:T(2,128)(2,1)} %reshape.179), calls=%async_computation.1 | async-start | bytes 114688 | tf_op jit(solution)/shard_map/all_to_all | solution.py:42
  167.7 2.7 %convolution_convert_fusion = bf16[256,128]{1,0:T(8,128)(2,1)} fusion(bf16[256,3456]{1,0:T(8,128)(2,1)} %constant_dynamic-update-slice_fusion.81, bf16[3456,128]{1,0:T(8,128)(2,1)S(1)} %bitcast.138), kind=kOutput, calls=%fused_computation.7 | convolution fusion | flops 226525184 | bytes 2719744 | tf_op jit(solution)/shard_map/dot_general | solution.py:124
  170.4 7.3 %all-to-all-done.1 = bf16[16,2,864]{2,1,0:T(2,128)(2,1)S(1)} async-done(((bf16[16,2,864]{2,1,0:T(2,128)(2,1)}), bf16[16,2,864]{2,1,0:T(2,128)(2,1)S(1)}, u32[]{:S(2)}, u32[]{:S(2)}) %all-to-all-start.1) | async-done | bytes 55328 | tf_op jit(solution)/shard_map/all_to_all | solution.py:42
  (179 shorter events, 22.3 us)
Async XLA Ops:
  1.6 9.7 %collective-permute-start = (bf16[2,1,32,128]{3,2,1,0:T(8,128)(2,1)S(1)}, bf16[2,1,32,128]{3,2,1,0:T(8,128)(2,1)S(1)}, u32[]{:S(2)}, u32[]{:S(2)}) collective-permute-start(bf16[2,1,32,128]{3,2,1,0:T(8,128)(2,1)S(1)} %get-tuple-element.90), channel_id=1, source_target_pairs={{0,1},{1,2},{2,3},{3,4},{4,5},{5,6},{6,7},{7,8},{8,9},{9,10},{10,1... | collective-permute-start | bytes 49160 | tf_op jit(solution)/shard_map/ppermute | solution.py:19
  3.5 11.2 %copy-start.17 = (f32[2,128]{1,0:T(2,128)S(1)}, f32[2,128]{1,0:T(2,128)}, u32[]{:S(2)}) copy-start(f32[2,128]{1,0:T(2,128)} %param.8) | copy-start | bytes 3076
  3.5 7.8 %collective-permute-start.1 = (bf16[2,1,32,128]{3,2,1,0:T(8,128)(2,1)S(1)}, bf16[2,1,32,128]{3,2,1,0:T(8,128)(2,1)S(1)}, u32[]{:S(2)}, u32[]{:S(2)}) collective-permute-start(bf16[2,1,32,128]{3,2,1,0:T(8,128)(2,1)S(1)} %get-tuple-element.91), channel_id=1, source_target_pairs={{1,0},{2,1},{3,2},{4,3},{5,4},{6,5},{7,6},{8,7},{9,8},{10,9},{11,1... | collective-permute-start | bytes 49160 | tf_op jit(solution)/shard_map/ppermute | solution.py:21
  11.3 5.6 %collective-permute-start.2 = (bf16[2,6,32,128]{3,2,1,0:T(8,128)(2,1)S(1)}, bf16[2,6,32,128]{3,2,1,0:T(8,128)(2,1)S(1)}, u32[]{:S(2)}, u32[]{:S(2)}) collective-permute-start(bf16[2,6,32,128]{3,2,1,0:T(8,128)(2,1)S(1)} %pad_maximum_fusion.2), channel_id=1, source_target_pairs={{0,32},{32,64},{64,96},{96,128},{128,160},{160,192},{192,224},{224... | collective-permute-start | bytes 294920 | tf_op jit(solution)/shard_map/ppermute | solution.py:31
  15.3 4.3 %copy-start.13 = (f32[128]{0:T(128)}, f32[128]{0:T(128)S(1)}, u32[]{:S(2)}) copy-start(f32[128]{0:T(128)S(1)} %get-tuple-element.97) | copy-start | bytes 1540
  17.1 0.8 copy-start.9
  17.1 0.8 copy-start.12
  19.0 0.7 copy-start.2
  19.6 1.4 copy-start.10
  19.8 0.6 copy-start.6
  21.0 12.6 %collective-permute-start.3 = (bf16[2,1,32,128]{3,2,1,0:T(8,128)(2,1)}, bf16[2,1,32,128]{3,2,1,0:T(8,128)(2,1)S(1)}, u32[]{:S(2)}, u32[]{:S(2)}) collective-permute-start(bf16[2,1,32,128]{3,2,1,0:T(8,128)(2,1)} %get-tuple-element.88), channel_id=1, source_target_pairs={{0,1},{1,2},{2,3},{3,4},{4,5},{5,6},{6,7},{7,8},{8,9},{9,10},{10,1... | collective-permute-start | bytes 49160 | tf_op jit(solution)/shard_map/ppermute | solution.py:19
  22.9 10.7 %collective-permute-start.4 = (bf16[2,1,32,128]{3,2,1,0:T(8,128)(2,1)}, bf16[2,1,32,128]{3,2,1,0:T(8,128)(2,1)}, u32[]{:S(2)}, u32[]{:S(2)}) collective-permute-start(bf16[2,1,32,128]{3,2,1,0:T(8,128)(2,1)} %get-tuple-element.89), channel_id=1, source_target_pairs={{1,0},{2,1},{3,2},{4,3},{5,4},{6,5},{7,6},{8,7},{9,8},{10,9},{11,1... | collective-permute-start | bytes 49160 | tf_op jit(solution)/shard_map/ppermute | solution.py:21
  31.7 2.0 %copy-start.7 = (bf16[256,128]{1,0:T(8,128)(2,1)S(1)}, bf16[256,128]{1,0:T(8,128)(2,1)}, u32[]{:S(2)}) copy-start(bf16[256,128]{1,0:T(8,128)(2,1)} %copy-done.6) | copy-start | bytes 196612
  34.4 6.5 %collective-permute-start.5 = (bf16[2,6,32,128]{3,2,1,0:T(8,128)(2,1)S(1)}, bf16[2,6,32,128]{3,2,1,0:T(8,128)(2,1)S(1)}, u32[]{:S(2)}, u32[]{:S(2)}) collective-permute-start(bf16[2,6,32,128]{3,2,1,0:T(8,128)(2,1)S(1)} %pad_maximum_fusion.3), channel_id=1, source_target_pairs={{0,32},{32,64},{64,96},{96,128},{128,160},{160,192},{192,224},{224... | collective-permute-start | bytes 294920 | tf_op jit(solution)/shard_map/ppermute | solution.py:31
  41.9 0.9 copy-start.3
  41.9 0.9 copy-start.11
  41.9 0.9 copy-start.14
  42.0 1.2 copy-start.1
  45.4 0.7 copy-start.15
  48.2 6.5 %collective-permute-start.6 = (bf16[2,4,32,128]{3,2,1,0:T(8,128)(2,1)S(1)}, bf16[2,4,32,128]{3,2,1,0:T(8,128)(2,1)S(1)}, u32[]{:S(2)}, u32[]{:S(2)}) collective-permute-start(bf16[2,4,32,128]{3,2,1,0:T(8,128)(2,1)S(1)} %bitcast.146), channel_id=1, source_target_pairs={{32,0},{64,32},{96,64},{128,96},{160,128},{192,160},{224,192},{256... | collective-permute-start | bytes 196616 | tf_op jit(solution)/shard_map/ppermute | solution.py:31
  54.8 6.5 %collective-permute-start.7 = (bf16[4,1,32,128]{3,2,1,0:T(8,128)(2,1)S(1)}, bf16[4,1,32,128]{3,2,1,0:T(8,128)(2,1)S(1)}, u32[]{:S(2)}, u32[]{:S(2)}) collective-permute-start(bf16[4,1,32,128]{3,2,1,0:T(8,128)(2,1)S(1)} %get-tuple-element.81), channel_id=1, source_target_pairs={{0,1},{1,2},{2,3},{3,4},{4,5},{5,6},{6,7},{7,8},{8,9},{9,10},{10,1... | collective-permute-start | bytes 98312 | tf_op jit(solution)/shard_map/ppermute | solution.py:19
  56.7 6.1 %collective-permute-start.8 = (bf16[4,1,32,128]{3,2,1,0:T(8,128)(2,1)S(1)}, bf16[4,1,32,128]{3,2,1,0:T(8,128)(2,1)S(1)}, u32[]{:S(2)}, u32[]{:S(2)}) collective-permute-start(bf16[4,1,32,128]{3,2,1,0:T(8,128)(2,1)S(1)} %get-tuple-element.82), channel_id=1, source_target_pairs={{1,0},{2,1},{3,2},{4,3},{5,4},{6,5},{7,6},{8,7},{9,8},{10,9},{11,1... | collective-permute-start | bytes 98312 | tf_op jit(solution)/shard_map/ppermute | solution.py:21
  63.2 0.9 copy-start.4
  63.3 1.2 copy-start.8
  63.9 1.3 copy-start.16
  64.5 1.5 copy-start.5
  66.6 15.7 %collective-permute-start.9 = (bf16[2,4,32,128]{3,2,1,0:T(8,128)(2,1)S(1)}, bf16[2,4,32,128]{3,2,1,0:T(8,128)(2,1)S(1)}, u32[]{:S(2)}, u32[]{:S(2)}) collective-permute-start(bf16[2,4,32,128]{3,2,1,0:T(8,128)(2,1)S(1)} %bitcast.141), channel_id=1, source_target_pairs={{32,0},{64,32},{96,64},{128,96},{160,128},{192,160},{224,192},{256... | collective-permute-start | bytes 196616 | tf_op jit(solution)/shard_map/ppermute | solution.py:31
  70.2 71.7 %all-to-all-start = ((bf16[32,54,4,128]{3,2,1,0:T(4,128)(2,1)}), bf16[32,54,4,128]{3,2,1,0:T(4,128)(2,1)S(1)}, u32[]{:S(2)}, u32[]{:S(2)}) async-start(bf16[32,54,4,128]{3,2,1,0:T(4,128)(2,1)} %copy.26), calls=%async_computation | async-start | bytes 3538944 | tf_op jit(solution)/shard_map/all_to_all | solution.py:42
  82.3 41.7 %collective-permute-start.10 = (bf16[4,1,32,128]{3,2,1,0:T(8,128)(2,1)S(1)}, bf16[4,1,32,128]{3,2,1,0:T(8,128)(2,1)S(1)}, u32[]{:S(2)}, u32[]{:S(2)}) collective-permute-start(bf16[4,1,32,128]{3,2,1,0:T(8,128)(2,1)S(1)} %get-tuple-element.77), channel_id=1, source_target_pairs={{0,1},{1,2},{2,3},{3,4},{4,5},{5,6},{6,7},{7,8},{8,9},{9,10},{10,1... | collective-permute-start | bytes 98312 | tf_op jit(solution)/shard_map/ppermute | solution.py:19
  84.4 39.7 %collective-permute-start.11 = (bf16[4,1,32,128]{3,2,1,0:T(8,128)(2,1)S(1)}, bf16[4,1,32,128]{3,2,1,0:T(8,128)(2,1)S(1)}, u32[]{:S(2)}, u32[]{:S(2)}) collective-permute-start(bf16[4,1,32,128]{3,2,1,0:T(8,128)(2,1)S(1)} %get-tuple-element.78), channel_id=1, source_target_pairs={{1,0},{2,1},{3,2},{4,3},{5,4},{6,5},{7,6},{8,7},{9,8},{10,9},{11,1... | collective-permute-start | bytes 98312 | tf_op jit(solution)/shard_map/ppermute | solution.py:21
  137.3 30.3 %copy-start = (bf16[27,128,128]{2,1,0:T(8,128)(2,1)S(1)}, bf16[27,128,128]{2,1,0:T(8,128)(2,1)}, u32[]{:S(2)}) copy-start(bf16[27,128,128]{2,1,0:T(8,128)(2,1)} %copy.21) | copy-start | bytes 2654212
  143.7 34.0 %all-to-all-start.1 = ((bf16[16,2,864]{2,1,0:T(2,128)(2,1)}), bf16[16,2,864]{2,1,0:T(2,128)(2,1)S(1)}, u32[]{:S(2)}, u32[]{:S(2)}) async-start(bf16[16,2,864]{2,1,0:T(2,128)(2,1)} %reshape.179), calls=%async_computation.1 | async-start | bytes 114688 | tf_op jit(solution)/shard_map/all_to_all | solution.py:42
where the time goes:
time: 180 us; the launch traced here: 179 us
  starting transfers between devices  72.3 us (40%)
  waiting for transfers between devices  51.6 us (29%)
  local copies, waits for them, and re-layouts  37.9 us (21%)
  other arithmetic  8.47 us (5%)
  matrix products  6.65 us (4%)
    all_to_all x2, starting transfers between devices, sent_and_summed(): lax.all_to_all(blocks, axis, split_axis=0, concat_axis=0, tiled=True)  36 us
    ppermute x4, waiting for transfers between devices, with_halo(): lax.ppermute(tail, axis, [(i, (i + 1) % count) for i in range(ends)])  35 us
    unnamed x139, local copies, waits for them, and re-layouts  22.3 us
    ppermute x4, starting transfers between devices, with_halo(): lax.ppermute(head, axis, [((i + 1) % count, i) for i in range(ends)])  18.2 us
    ppermute x4, starting transfers between devices, from_behind(): lax.ppermute(value, axis, [(source, source + steps) for source in range(f...  10.3 us
    ppermute x4, starting transfers between devices, with_halo(): lax.ppermute(tail, axis, [(i, (i + 1) % count) for i in range(ends)])  7.78 us
    ppermute x4, waiting for transfers between devices, from_behind(): lax.ppermute(value, axis, [(source, source + steps) for source in range(f...  7.69 us
    all_to_all x2, waiting for transfers between devices, sent_and_summed(): lax.all_to_all(blocks, axis, split_axis=0, concat_axis=0, tiled=True)  7.33 us
  transfers between devices with their start and end apart: 14, of which 6 were waited for; matrix products, arithmetic and copies ran while one was open for 19% of the time, Pallas kernels for 0%

commit v1 on v0

--- a/solution.py
+++ b/solution.py
@@ -3,6 +3,8 @@
 import jax
 import jax.numpy as jnp
 from jax import lax
+from jax.experimental import pallas as pl
+from jax.experimental.pallas import tpu as pltpu
 from jax.sharding import PartitionSpec as P
 
 EPS = 1e-06
@@ -31,16 +33,46 @@
     return lax.ppermute(value, axis, [(source, source + steps) for source in range(first, last)])
 
 
-def split_up(shard, dim, size):
-    lengths = shard.shape
-    blocks = shard.reshape(*lengths[:dim], size, lengths[dim] // size, *lengths[dim + 1 :])
-    return jnp.moveaxis(blocks, dim, 0)
+def parts_kernel(first_ref, second_ref, *part_refs):
+    taps = first_ref.shape[0]
+    for index, part_ref in enumerate(part_refs):
+        tap, half = divmod(index, 2)
+        source = first_ref if tap < taps else second_ref
+        rows = source.shape[1] // 2
+        block = source[tap % taps, half * rows : (half + 1) * rows]
+        part_ref[...] = block.reshape(part_ref.shape).astype(part_ref.dtype)
 
 
-def sent_and_summed(shard, axis, dim):
-    blocks = split_up(shard, dim, lax.axis_size(axis))
-    arrived = lax.all_to_all(blocks, axis, split_axis=0, concat_axis=0, tiled=True)
-    return arrived.astype(jnp.float32).sum(axis=0)
+def in_parts(first, second, pieces):
+    taps, rows, lanes = first.shape
+    shape = jax.ShapeDtypeStruct((pieces // 2, rows // pieces, lanes), jnp.bfloat16)
+    return pl.pallas_call(parts_kernel, out_shape=[shape] * (4 * taps))(first, second)
+
+
+def pick_kernel(scale, *refs):
+    *part_refs, out_ref, rows_ref = refs
+    position = lax.axis_index("tile")
+    blocks = part_refs[0].shape[0]
+    width = out_ref.shape[-1]
+    upper = position >= blocks
+    index = jnp.where(upper, position - blocks, position)
+    for tap in range(len(part_refs) // 2):
+        low = part_refs[2 * tap][index].astype(jnp.float32)
+        high = part_refs[2 * tap + 1][index].astype(jnp.float32)
+        rows_ref[tap] = jnp.where(upper, high, low) * scale
+    lanes = rows_ref.shape[-1]
+    shift = lanes - lax.axis_index("frame") * width
+    out_ref[...] = pltpu.roll(rows_ref[...], shift, 2)[:, :, :width]
+
+
+def picked(parts, width, scale):
+    taps = len(parts) // 2
+    _, rows, lanes = parts[0].shape
+    return pl.pallas_call(
+        lambda *refs: pick_kernel(scale, *refs),
+        out_shape=jax.ShapeDtypeStruct((taps, rows, width), jnp.float32),
+        scratch_shapes=[pltpu.VMEM((taps, rows, lanes), jnp.float32)],
+    )(*parts)
 
 
 def patches(extended, frames, rows, columns, offset, sign):
@@ -125,11 +157,10 @@
             jnp.bfloat16
         )
     input_grad = upstream.reshape(frames, rows, columns, channels)
-    stacked = jnp.concatenate(grads_list, axis=0)
-    partial_sum = sent_and_summed(stacked.astype(jnp.bfloat16), "tile", 1)
-    summed = sent_and_summed(partial_sum.astype(jnp.bfloat16), "frame", 2)
     total_cells = cells * lax.axis_size("frame") * lax.axis_size("tile")
-    kernel_grads = summed / jnp.float32(math.sqrt(total_cells))
+    parts = in_parts(grads_list[0], grads_list[1], lax.axis_size("tile"))
+    summed = lax.psum(parts, ("frame", "tile"))
+    kernel_grads = picked(summed, channels // lax.axis_size("frame"), 1.0 / math.sqrt(total_cells))
     return (input_grad, kernel_grads)
 
 

time: 180 us -> 218 us (1.21)
  the two profiles are of different devices: /device:TPU:40 before, /device:TPU:34 now
where the time goes in v1:
time: 218 us; the launch traced here: 217 us
  blocking collectives  119 us (55%)
  starting transfers between devices  34.2 us (16%)
  local copies, waits for them, and re-layouts  19.2 us (9%)
  waiting for transfers between devices  18.2 us (8%)
  other arithmetic  10.1 us (5%)
  matrix products  8.56 us (4%)
  Pallas kernels  5.79 us (3%)
    psum x1, blocking collectives, local(): summed = lax.psum(parts, ('frame', 'tile'))  119 us
    ppermute x4, starting transfers between devices, with_halo(): lax.ppermute(head, axis, [((i + 1) % count, i) for i in range(ends)])  15.9 us
    ppermute x4, waiting for transfers between devices, with_halo(): lax.ppermute(tail, axis, [(i, (i + 1) % count) for i in range(ends)])  13.4 us
    ppermute x4, starting transfers between devices, from_behind(): lax.ppermute(value, axis, [(source, source + steps) for source in range(f...  10.6 us
    ppermute x4, starting transfers between devices, with_halo(): lax.ppermute(tail, axis, [(i, (i + 1) % count) for i in range(ends)])  7.68 us
    unnamed x133, local copies, waits for them, and re-layouts  6.73 us
    transpose x3, local copies, waits for them, and re-layouts, local(): jnp.transpose(kernels[layer], (0, 2, 1)).reshape(27 * channels, channels)  6.53 us
    dot_general x2, matrix products, local(): lax.dot_general(columns_in, pre_grad, (((0,), (0,)), ((), ())), preferred...  5.17 us
  transfers between devices with their start and end apart: 12, of which 7 were waited for; matrix products, arithmetic and copies ran while one was open for 9% of the time, Pallas kernels for 3%

profile of v1, /device:TPU:34, one launch (start us, length us, event | category | flops | bytes accessed | tf_op | source)
XLA Modules:
  0.0 216.9 jit_solution(5504838331629686993)
XLA Ops:
  0.6 0.9 multiply_convert_fusion.1
  1.6 3.6 %collective-permute-start.1 = (bf16[2,1,32,128]{3,2,1,0:T(8,128)(2,1)S(1)}, bf16[2,1,32,128]{3,2,1,0:T(8,128)(2,1)S(1)}, u32[]{:S(2)}, u32[]{:S(2)}) collective-permute-start(bf16[2,1,32,128]{3,2,1,0:T(8,128)(2,1)S(1)} %get-tuple-element.421), channel_id=1, source_target_pairs={{1,0},{2,1},{3,2},{4,3},{5,4},{6,5},{7,6},{8,7},{9,8},{10,9},{11,1... | collective-permute-start | bytes 49160 | tf_op jit(solution)/shard_map/ppermute | solution.py:23
  5.2 1.9 collective-permute-start
  7.1 3.2 %slice_bitcast_fusion.3 = (bf16[27,128,128]{1,2,0:T(8,128)(2,1)S(1)}, bf16[27,128,128]{1,2,0:T(8,128)(2,1)S(1)}, bf16[1,27,128,128]{3,2,1,0:T(8,128)(2,1)}, bf16[1,27,128,128]{3,2,1,0:T(8,128)(2,1)S(1)}) fusion(bf16[2,27,128,128]{3,2,1,0:T(8,128)(2,1)} %param.7), kind=kLoop, calls=%fused_computation.209 | loop fusion | bytes 5308416 | tf_op jit(solution)/shard_map/transpose | solution.py:155
  10.4 2.0 collective-permute-done
  12.4 3.4 %collective-permute-start.2 = (bf16[2,6,32,128]{3,2,1,0:T(8,128)(2,1)S(1)}, bf16[2,6,32,128]{3,2,1,0:T(8,128)(2,1)S(1)}, u32[]{:S(2)}, u32[]{:S(2)}) collective-permute-start(bf16[2,6,32,128]{3,2,1,0:T(8,128)(2,1)S(1)} %pad_maximum_fusion.2), channel_id=1, source_target_pairs={{0,32},{32,64},{64,96},{96,128},{128,160},{160,192},{192,224},{224... | collective-permute-start | bytes 294920 | tf_op jit(solution)/shard_map/ppermute | solution.py:33
  15.8 0.6 slice_bitcast_fusion
  16.4 2.5 %collective-permute-done.2 = bf16[2,6,32,128]{3,2,1,0:T(8,128)(2,1)S(1)} collective-permute-done((bf16[2,6,32,128]{3,2,1,0:T(8,128)(2,1)S(1)}, bf16[2,6,32,128]{3,2,1,0:T(8,128)(2,1)S(1)}, u32[]{:S(2)}, u32[]{:S(2)}) %collective-permute-start.2) | collective-permute-done | bytes 98336 | tf_op jit(solution)/shard_map/ppermute | solution.py:33
  20.2 0.7 multiply_reduce_fusion.3
  21.0 0.6 multiply_multiply_fusion.1
  21.6 0.7 multiply_convert_fusion
  22.4 1.3 fusion.29
  23.7 2.6 %collective-permute-start.4 = (bf16[2,1,32,128]{3,2,1,0:T(8,128)(2,1)}, bf16[2,1,32,128]{3,2,1,0:T(8,128)(2,1)S(1)}, u32[]{:S(2)}, u32[]{:S(2)}) collective-permute-start(bf16[2,1,32,128]{3,2,1,0:T(8,128)(2,1)} %get-tuple-element.419), channel_id=1, source_target_pairs={{1,0},{2,1},{3,2},{4,3},{5,4},{6,5},{7,6},{8,7},{9,8},{10,9},{11,1... | collective-permute-start | bytes 49160 | tf_op jit(solution)/shard_map/ppermute | solution.py:23
  26.3 1.9 collective-permute-start.3
  28.2 1.7 copy.15
  29.9 1.6 copy.16
  31.5 0.9 copy.17
  32.5 1.3 collective-permute-done.3
  33.8 0.9 pad_maximum_fusion.3
  34.7 3.4 %collective-permute-start.5 = (bf16[2,6,32,128]{3,2,1,0:T(8,128)(2,1)S(1)}, bf16[2,6,32,128]{3,2,1,0:T(8,128)(2,1)S(1)}, u32[]{:S(2)}, u32[]{:S(2)}) collective-permute-start(bf16[2,6,32,128]{3,2,1,0:T(8,128)(2,1)S(1)} %pad_maximum_fusion.3), channel_id=1, source_target_pairs={{0,32},{32,64},{64,96},{96,128},{128,160},{160,192},{192,224},{224... | collective-permute-start | bytes 294920 | tf_op jit(solution)/shard_map/ppermute | solution.py:33
  38.1 0.9 pad_maximum_fusion.6
  39.0 2.2 %collective-permute-done.5 = bf16[2,6,32,128]{3,2,1,0:T(8,128)(2,1)S(1)} collective-permute-done((bf16[2,6,32,128]{3,2,1,0:T(8,128)(2,1)S(1)}, bf16[2,6,32,128]{3,2,1,0:T(8,128)(2,1)S(1)}, u32[]{:S(2)}, u32[]{:S(2)}) %collective-permute-start.5) | collective-permute-done | bytes 98336 | tf_op jit(solution)/shard_map/ppermute | solution.py:33
  41.2 0.9 maximum_maximum_fusion.1
  43.6 0.7 multiply_reduce_fusion.2
  44.5 0.8 subtract_convert_fusion.1
  45.4 1.9 collective-permute-start.6
  47.3 2.2 %copy.18 = bf16[3456,256]{1,0:T(8,128)(2,1)} copy(bf16[3456,256]{0,1:T(8,128)(2,1)S(1)} %bitcast.124) | data formatting | bytes 3538944 | tf_op jit(solution)/shard_map/dot_general | solution.py:149
  49.5 3.3 %fusion.17.second_ref = f32[27,128,128]{2,1,0:T(8,128)} fusion(bf16[27,128,256]{2,1,0:T(8,128)(2,1)} %bitcast.128, bf16[256,128]{1,0:T(8,128)(2,1)} %subtract_convert_fusion.1), kind=kOutput, calls=%fused_computation.192 | convolution fusion | flops 226492416 | bytes 3604480 | tf_op jit(solution)/shard_map/dot_general | solution.py:149
  53.0 0.8 pad_maximum_fusion.13
  53.8 3.1 %collective-permute-start.8 = (bf16[4,1,32,128]{3,2,1,0:T(8,128)(2,1)S(1)}, bf16[4,1,32,128]{3,2,1,0:T(8,128)(2,1)S(1)}, u32[]{:S(2)}, u32[]{:S(2)}) collective-permute-start(bf16[4,1,32,128]{3,2,1,0:T(8,128)(2,1)S(1)} %get-tuple-element.412), channel_id=1, source_target_pairs={{1,0},{2,1},{3,2},{4,3},{5,4},{6,5},{7,6},{8,7},{9,8},{10,9},{11,1... | collective-permute-start | bytes 98312 | tf_op jit(solution)/shard_map/ppermute | solution.py:23
  56.9 1.9 collective-permute-start.7
  58.8 0.8 pad_maximum_fusion.5
  59.6 4.6 %collective-permute-done.7 = bf16[4,1,32,128]{3,2,1,0:T(8,128)(2,1)S(1)} collective-permute-done((bf16[4,1,32,128]{3,2,1,0:T(8,128)(2,1)S(1)}, bf16[4,1,32,128]{3,2,1,0:T(8,128)(2,1)S(1)}, u32[]{:S(2)}, u32[]{:S(2)}) %collective-permute-start.7) | collective-permute-done | bytes 32800 | tf_op jit(solution)/shard_map/ppermute | solution.py:21
  64.3 1.0 fusion.12
  65.4 1.0 maximum_maximum_fusion.2
  66.6 0.9 constant_dynamic-update-slice_fusion.76
  67.9 0.9 constant_dynamic-update-slice_fusion.58
  68.9 0.7 multiply_reduce_fusion
  69.8 1.9 collective-permute-start.9
  71.8 1.8 fusion.19.first_ref
  73.6 3.5 %shard_map.68 = (bf16[16,4,128]{2,1,0:T(4,128)(2,1)}, bf16[16,4,128]{2,1,0:T(4,128)(2,1)}, bf16[16,4,128]{2,1,0:T(4,128)(2,1)}, bf16[16,4,128]{2,1,0:T(4,128)(2,...) custom-call(f32[27,128,128]{2,1,0:T(8,128)} %fusion.19.first_ref, ...), custom_call_target="tpu_custom_call" | custom-call | tf_op jit(solution)/shard_map/pallas_call | solution.py:49
  77.1 119.2 %all-reduce.6 = (bf16[16,4,128]{2,1,0:T(4,128)(2,1)}, bf16[16,4,128]{2,1,0:T(4,128)(2,1)}, bf16[16,4,128]{2,1,0:T(4,128)(2,1)}, bf16[16,4,128]{2,1,0:T(4,128)(2,...) all-reduce(bf16[16,4,128]{2,1,0:T(4,128)(2,1)} %get-tuple-element.1, ...), channel_id=1, replica_groups=mesh['frame'=16,'tile'=32] {'frame','tile'}, use_global_device_ids=true, to_apply=%region_4.5 | all-reduce | flops 884736 | bytes 3538944 | tf_op jit(solution)/shard_map/psum | solution.py:162
  196.3 2.3 %shard_map.69 = f32[54,4,8]{2,1,0:T(4,128)} custom-call(bf16[16,4,128]{2,1,0:T(4,128)(2,1)} %get-tuple-element.224.refs_0_, bf16[16,4,128]{2,1,0:T(4,128)(2,1)} %get-tuple-element.225.refs_1_, bf16[16,4,128]{2,1,0:T(4,128)(2,1)} %get-tuple-element.226.refs_2_, bf16[16,4,128]{2,1,0:T(4,128)(2,1)} %get-tuple-element.227.refs_3_, ...), custom_call_target="tpu_custom_call" | custom-call | tf_op jit(solution)/shard_map/pallas_call | solution.py:71
  198.6 1.6 copy.19
  200.2 6.5 %collective-permute-start.11 = (bf16[4,1,32,128]{3,2,1,0:T(8,128)(2,1)S(1)}, bf16[4,1,32,128]{3,2,1,0:T(8,128)(2,1)S(1)}, u32[]{:S(2)}, u32[]{:S(2)}) collective-permute-start(bf16[4,1,32,128]{3,2,1,0:T(8,128)(2,1)S(1)} %get-tuple-element.408), channel_id=1, source_target_pairs={{1,0},{2,1},{3,2},{4,3},{5,4},{6,5},{7,6},{8,7},{9,8},{10,9},{11,1... | collective-permute-start | bytes 98312 | tf_op jit(solution)/shard_map/ppermute | solution.py:23
  206.7 1.9 collective-permute-start.10
  208.7 5.4 %collective-permute-done.10 = bf16[4,1,32,128]{3,2,1,0:T(8,128)(2,1)S(1)} collective-permute-done((bf16[4,1,32,128]{3,2,1,0:T(8,128)(2,1)S(1)}, bf16[4,1,32,128]{3,2,1,0:T(8,128)(2,1)S(1)}, u32[]{:S(2)}, u32[]{:S(2)}) %collective-permute-start.10) | collective-permute-done | bytes 32800 | tf_op jit(solution)/shard_map/ppermute | solution.py:21
  215.7 1.2 convolution_convert_fusion
  (164 shorter events, 5.2 us)
Async XLA Ops:
  1.6 8.8 %collective-permute-start.1 = (bf16[2,1,32,128]{3,2,1,0:T(8,128)(2,1)S(1)}, bf16[2,1,32,128]{3,2,1,0:T(8,128)(2,1)S(1)}, u32[]{:S(2)}, u32[]{:S(2)}) collective-permute-start(bf16[2,1,32,128]{3,2,1,0:T(8,128)(2,1)S(1)} %get-tuple-element.421), channel_id=1, source_target_pairs={{1,0},{2,1},{3,2},{4,3},{5,4},{6,5},{7,6},{8,7},{9,8},{10,9},{11,1... | collective-permute-start | bytes 49160 | tf_op jit(solution)/shard_map/ppermute | solution.py:23
  5.2 10.6 %copy-start.15 = (f32[2,128]{1,0:T(2,128)S(1)}, f32[2,128]{1,0:T(2,128)}, u32[]{:S(2)}) copy-start(f32[2,128]{1,0:T(2,128)} %param.8) | copy-start | bytes 3076
  5.2 7.2 %collective-permute-start = (bf16[2,1,32,128]{3,2,1,0:T(8,128)(2,1)S(1)}, bf16[2,1,32,128]{3,2,1,0:T(8,128)(2,1)S(1)}, u32[]{:S(2)}, u32[]{:S(2)}) collective-permute-start(bf16[2,1,32,128]{3,2,1,0:T(8,128)(2,1)S(1)} %get-tuple-element.420), channel_id=1, source_target_pairs={{0,1},{1,2},{2,3},{3,4},{4,5},{5,6},{6,7},{7,8},{8,9},{9,10},{10,1... | collective-permute-start | bytes 49160 | tf_op jit(solution)/shard_map/ppermute | solution.py:21
  12.4 6.5 %collective-permute-start.2 = (bf16[2,6,32,128]{3,2,1,0:T(8,128)(2,1)S(1)}, bf16[2,6,32,128]{3,2,1,0:T(8,128)(2,1)S(1)}, u32[]{:S(2)}, u32[]{:S(2)}) collective-permute-start(bf16[2,6,32,128]{3,2,1,0:T(8,128)(2,1)S(1)} %pad_maximum_fusion.2), channel_id=1, source_target_pairs={{0,32},{32,64},{64,96},{96,128},{128,160},{160,192},{192,224},{224... | collective-permute-start | bytes 294920 | tf_op jit(solution)/shard_map/ppermute | solution.py:33
  16.4 5.2 %copy-start.11 = (f32[128]{0:T(128)}, f32[128]{0:T(128)S(1)}, u32[]{:S(2)}) copy-start(f32[128]{0:T(128)S(1)} %get-tuple-element.427) | copy-start | bytes 1540
  19.1 0.8 copy-start.6
  19.1 0.8 copy-start.10
  20.9 0.7 copy-start.2
  21.6 2.1 copy-start.8
  23.7 8.7 %collective-permute-start.4 = (bf16[2,1,32,128]{3,2,1,0:T(8,128)(2,1)}, bf16[2,1,32,128]{3,2,1,0:T(8,128)(2,1)S(1)}, u32[]{:S(2)}, u32[]{:S(2)}) collective-permute-start(bf16[2,1,32,128]{3,2,1,0:T(8,128)(2,1)} %get-tuple-element.419), channel_id=1, source_target_pairs={{1,0},{2,1},{3,2},{4,3},{5,4},{6,5},{7,6},{8,7},{9,8},{10,9},{11,1... | collective-permute-start | bytes 49160 | tf_op jit(solution)/shard_map/ppermute | solution.py:23
  26.3 7.5 %collective-permute-start.3 = (bf16[2,1,32,128]{3,2,1,0:T(8,128)(2,1)}, bf16[2,1,32,128]{3,2,1,0:T(8,128)(2,1)}, u32[]{:S(2)}, u32[]{:S(2)}) collective-permute-start(bf16[2,1,32,128]{3,2,1,0:T(8,128)(2,1)} %get-tuple-element.418), channel_id=1, source_target_pairs={{0,1},{1,2},{2,3},{3,4},{4,5},{5,6},{6,7},{7,8},{8,9},{9,10},{10,1... | collective-permute-start | bytes 49160 | tf_op jit(solution)/shard_map/ppermute | solution.py:21
  34.7 6.5 %collective-permute-start.5 = (bf16[2,6,32,128]{3,2,1,0:T(8,128)(2,1)S(1)}, bf16[2,6,32,128]{3,2,1,0:T(8,128)(2,1)S(1)}, u32[]{:S(2)}, u32[]{:S(2)}) collective-permute-start(bf16[2,6,32,128]{3,2,1,0:T(8,128)(2,1)S(1)} %pad_maximum_fusion.3), channel_id=1, source_target_pairs={{0,32},{32,64},{64,96},{96,128},{128,160},{160,192},{192,224},{224... | collective-permute-start | bytes 294920 | tf_op jit(solution)/shard_map/ppermute | solution.py:33
  42.3 0.9 copy-start.3
  42.3 0.9 copy-start.9
  42.3 0.9 copy-start.12
  42.4 1.2 copy-start.1
  43.2 1.1 copy-start.7
  43.2 1.1 copy-start.13
  45.4 7.6 %collective-permute-start.6 = (bf16[2,4,32,128]{3,2,1,0:T(8,128)(2,1)}, bf16[2,4,32,128]{3,2,1,0:T(8,128)(2,1)}, u32[]{:S(2)}, u32[]{:S(2)}) collective-permute-start(bf16[2,4,32,128]{3,2,1,0:T(8,128)(2,1)} %bitcast.33), channel_id=1, source_target_pairs={{32,0},{64,32},{96,64},{128,96},{160,128},{192,160},{224,192},{256... | collective-permute-start | bytes 196616 | tf_op jit(solution)/shard_map/ppermute | solution.py:33
  53.8 5.9 %collective-permute-start.8 = (bf16[4,1,32,128]{3,2,1,0:T(8,128)(2,1)S(1)}, bf16[4,1,32,128]{3,2,1,0:T(8,128)(2,1)S(1)}, u32[]{:S(2)}, u32[]{:S(2)}) collective-permute-start(bf16[4,1,32,128]{3,2,1,0:T(8,128)(2,1)S(1)} %get-tuple-element.412), channel_id=1, source_target_pairs={{1,0},{2,1},{3,2},{4,3},{5,4},{6,5},{7,6},{8,7},{9,8},{10,9},{11,1... | collective-permute-start | bytes 98312 | tf_op jit(solution)/shard_map/ppermute | solution.py:23
  56.9 7.3 %collective-permute-start.7 = (bf16[4,1,32,128]{3,2,1,0:T(8,128)(2,1)S(1)}, bf16[4,1,32,128]{3,2,1,0:T(8,128)(2,1)S(1)}, u32[]{:S(2)}, u32[]{:S(2)}) collective-permute-start(bf16[4,1,32,128]{3,2,1,0:T(8,128)(2,1)S(1)} %get-tuple-element.411), channel_id=1, source_target_pairs={{0,1},{1,2},{2,3},{3,4},{4,5},{5,6},{6,7},{7,8},{8,9},{9,10},{10,1... | collective-permute-start | bytes 98312 | tf_op jit(solution)/shard_map/ppermute | solution.py:21
  66.5 2.4 %copy-start.4 = (f32[256,128]{1,0:T(8,128)S(1)}, f32[256,128]{1,0:T(8,128)}, u32[]{:S(2)}) copy-start(f32[256,128]{1,0:T(8,128)} %copy-done.2) | copy-start | bytes 393220
  66.5 2.4 %copy-start.5 = (bf16[27,128,128]{2,1,0:T(8,128)(2,1)S(1)}, bf16[27,128,128]{2,1,0:T(8,128)(2,1)}, u32[]{:S(2)}) copy-start(bf16[27,128,128]{2,1,0:T(8,128)(2,1)} %copy.15) | copy-start | bytes 2654212
  68.9 0.8 copy-start.14
  69.8 130.3 %collective-permute-start.9 = (bf16[2,4,32,128]{3,2,1,0:T(8,128)(2,1)S(1)}, bf16[2,4,32,128]{3,2,1,0:T(8,128)(2,1)S(1)}, u32[]{:S(2)}, u32[]{:S(2)}) collective-permute-start(bf16[2,4,32,128]{3,2,1,0:T(8,128)(2,1)S(1)} %bitcast.132), channel_id=1, source_target_pairs={{32,0},{64,32},{96,64},{128,96},{160,128},{192,160},{224,192},{256... | collective-permute-start | bytes 196616 | tf_op jit(solution)/shard_map/ppermute | solution.py:33
  200.2 8.5 %collective-permute-start.11 = (bf16[4,1,32,128]{3,2,1,0:T(8,128)(2,1)S(1)}, bf16[4,1,32,128]{3,2,1,0:T(8,128)(2,1)S(1)}, u32[]{:S(2)}, u32[]{:S(2)}) collective-permute-start(bf16[4,1,32,128]{3,2,1,0:T(8,128)(2,1)S(1)} %get-tuple-element.408), channel_id=1, source_target_pairs={{1,0},{2,1},{3,2},{4,3},{5,4},{6,5},{7,6},{8,7},{9,8},{10,9},{11,1... | collective-permute-start | bytes 98312 | tf_op jit(solution)/shard_map/ppermute | solution.py:23
  206.7 7.3 %collective-permute-start.10 = (bf16[4,1,32,128]{3,2,1,0:T(8,128)(2,1)S(1)}, bf16[4,1,32,128]{3,2,1,0:T(8,128)(2,1)S(1)}, u32[]{:S(2)}, u32[]{:S(2)}) collective-permute-start(bf16[4,1,32,128]{3,2,1,0:T(8,128)(2,1)S(1)} %get-tuple-element.407), channel_id=1, source_target_pairs={{0,1},{1,2},{2,3},{3,4},{4,5},{5,6},{6,7},{7,8},{8,9},{9,10},{10,1... | collective-permute-start | bytes 98312 | tf_op jit(solution)/shard_map/ppermute | solution.py:21
  214.5 1.2 copy-start

commit v2 on v0

v2 whole, which is shorter than its diff:
```python
import math

import jax
import jax.numpy as jnp
from jax import lax
from jax.experimental import pallas as pl
from jax.experimental.pallas import tpu as pltpu
from jax.sharding import PartitionSpec as P

EPS = 1e-06
TAPS = 27
F32 = jnp.float32
BF16 = jnp.bfloat16


def call(kernel, out_shape, *operands, scratch=()):
    return pl.pallas_call(
        kernel,
        out_shape=out_shape,
        scratch_shapes=list(scratch),
        compiler_params=pltpu.CompilerParams(vmem_limit_bytes=48 * 2**20),
    )(*operands)


def shifted_columns(block):
    shape = block.shape
    columns = shape[-2]
    flat = block.astype(F32).reshape(-1, shape[-1])
    column = lax.broadcasted_iota(jnp.int32, flat.shape, 0) % columns
    before = jnp.where(column == 0, 0.0, pltpu.roll(flat, 1, 0))
    after = jnp.where(column == columns - 1, 0.0, pltpu.roll(flat, flat.shape[0] - 1, 0))
    return before.astype(BF16).reshape(shape), block, after.astype(BF16).reshape(shape)


def fill(patches, window, frames, rows, sign, seams):
    columns, channels = window[0][0][0].shape
    for row in range(rows):
        for frame in range(frames):
            first = (row * frames + frame) * columns
            for tap in range(TAPS):
                depth, down, across = tap // 9, tap // 3 % 3, tap % 3
                if sign > 0:
                    source = window[row + down][frame + depth][across]
                else:
                    source = window[row + 2 - down][frame + 2 - depth][2 - across]
                    down = 2 - down
                seam = seams.get((row, down))
                if seam is not None:
                    source = jnp.where(seam, jnp.zeros_like(source), source)
                patches[first : first + columns, tap * channels : (tap + 1) * channels] = source


def window_of(rows):
    return [[shifted_columns(block) for block in row] for row in rows]


def forward_rows(rows, frames, own_ref, earlier_ref):
    return [
        [earlier_ref[row, frame] for frame in range(frames)]
        + [own_ref[row, frame] for frame in range(frames)]
        for row in range(rows)
    ]


def silu_parts(pre_norm, gain):
    inverse = lax.rsqrt(jnp.mean(pre_norm * pre_norm, axis=-1, keepdims=True) + EPS)
    normed = pre_norm * inverse * gain
    return inverse, normed, 1.0 / (1.0 + jnp.exp(-normed))


def pre_norm_gradient(pre_norm, gain, upstream):
    inverse, normed, sigma = silu_parts(pre_norm, gain)
    scaled = gain * upstream * sigma * (1.0 + normed * (1.0 - sigma))
    mixed = jnp.mean(pre_norm * scaled, axis=-1, keepdims=True)
    return (inverse * scaled - pre_norm * inverse**3 * mixed).astype(BF16)


def at_last_tile():
    return lax.axis_index("tile") == lax.axis_size("tile") - 1


def first_rows(own_ref, earlier_ref, below_ref, frames, rows, total):
    result = []
    for row in range(total):
        if row < rows:
            result.append(
                [earlier_ref[frame, row] for frame in range(frames)]
                + [own_ref[frame, row] for frame in range(frames)]
            )
        else:
            result.append(
                [below_ref[frame * rows + row - rows] for frame in range(2 * frames)]
            )
    return result


def first_forward(own_ref, earlier_ref, below_ref, kernel_ref, gain_ref, next_ref, pre_ref, patches):
    frames, rows, columns, channels = own_ref.shape
    last = at_last_tile()
    window = window_of(first_rows(own_ref, earlier_ref, below_ref, frames, rows, 2 * rows))
    fill(patches, window, frames, 2 * rows - 2, 1, {(rows - 2, 2): last, (rows - 1, 0): last})
    pre_norm = jnp.dot(
        patches[...], kernel_ref[...].reshape(TAPS * channels, channels), preferred_element_type=F32
    )
    _, normed, sigma = silu_parts(pre_norm, gain_ref[0:1])
    next_ref[...] = (normed * sigma).astype(BF16).reshape(next_ref.shape)
    pre_ref[...] = pre_norm[: pre_ref.shape[0]]


def second_forward(own_ref, earlier_ref, top_ref, low_ref, kernel_ref, gain_ref, grad_ref, patches):
    total, frames, columns, channels = own_ref.shape
    rows = total - 2
    last = at_last_tile()
    window = window_of(forward_rows(total, frames, own_ref, earlier_ref))
    fill(patches, window, frames, rows, 1, {(rows - 3, 2): last, (rows - 2, 0): last})
    pre_norm = jnp.dot(
        patches[...], kernel_ref[...].reshape(TAPS * channels, channels), preferred_element_type=F32
    )
    spread = []
    for row in range(rows):
        for frame in range(frames):
            if row < rows - 2:
                spread.append(top_ref[frame, row + 2])
            else:
                spread.append(low_ref[frame * 2 + row - rows + 2])
    upstream = jnp.concatenate(spread, axis=0).astype(F32)
    grad_ref[...] = pre_norm_gradient(pre_norm, gain_ref[1:2], upstream).reshape(grad_ref.shape)


def backward_rows(own_ref, later_ref, above_ref, frames):
    rows = own_ref.shape[0]
    result = []
    for row in range(2):
        result.append([above_ref[row, frame] for frame in range(2 * frames)])
    for row in range(rows):
        result.append(
            [own_ref[row, frame] for frame in range(frames)]
            + [later_ref[row, frame] for frame in range(frames)]
        )
    return result


def back_product(patches, kernel_ref):
    turned = jnp.concatenate([kernel_ref[tap] for tap in range(TAPS)], axis=1)
    return lax.dot_general(
        patches[...], turned, (((1,), (1,)), ((), ())), preferred_element_type=F32
    )


def second_backward(
    own_ref, later_ref, above_ref, kernel_ref, gain_ref, pre_ref, grad_ref, patches
):
    rows, frames, columns, channels = own_ref.shape
    last = at_last_tile()
    window = window_of(backward_rows(own_ref, later_ref, above_ref, frames))
    fill(patches, window, frames, rows, -1, {(rows - 2, 2): last, (rows - 1, 0): last})
    upstream = back_product(patches, kernel_ref).astype(BF16).astype(F32)
    grad_ref[...] = pre_norm_gradient(pre_ref[...], gain_ref[0:1], upstream).reshape(grad_ref.shape)


def first_backward(own_ref, later_ref, above_ref, kernel_ref, out_ref, patches):
    rows, frames, columns, channels = own_ref.shape
    first, last = lax.axis_index("tile") == 0, at_last_tile()
    window = window_of(backward_rows(own_ref, later_ref, above_ref, frames))
    fill(patches, window, frames, rows, -1, {(0, 0): first, (rows - 1, 2): last})
    grad = back_product(patches, kernel_ref).astype(BF16)
    for row in range(rows):
        for frame in range(frames):
            cell = (row * frames + frame) * columns
            out_ref[frame, row] = grad[cell : cell + columns]


def split_gradient(patches, grad_ref, keep_ref, send_ref):
    chips, _, share, channels = keep_ref.shape
    odd = lax.axis_index("tile") % 2 == 1
    grad = grad_ref[...].reshape(-1, channels)
    for tap in range(TAPS):
        block = lax.dot_general(
            patches[:, tap * channels : (tap + 1) * channels],
            grad,
            (((0,), (0,)), ((), ())),
            preferred_element_type=F32,
        ).reshape(chips, 2, share, channels)
        even_part, odd_part = block[:, 0], block[:, 1]
        keep_ref[:, tap] = jnp.where(odd, odd_part, even_part).astype(BF16)
        send_ref[:, tap] = jnp.where(odd, even_part, odd_part).astype(BF16)


def second_kernel_gradient(own_ref, earlier_ref, grad_ref, keep_ref, send_ref, patches):
    total, frames, columns, channels = own_ref.shape
    rows = total - 2
    last = at_last_tile()
    window = window_of(forward_rows(total, frames, own_ref, earlier_ref))
    fill(patches, window, frames, rows, 1, {(rows - 3, 2): last, (rows - 2, 0): last})
    split_gradient(patches, grad_ref, keep_ref, send_ref)


def first_kernel_gradient(own_ref, earlier_ref, below_ref, grad_ref, keep_ref, send_ref, patches):
    frames, rows, columns, channels = own_ref.shape
    last = at_last_tile()
    window = window_of(first_rows(own_ref, earlier_ref, below_ref, frames, rows, rows + 2))
    fill(patches, window, frames, rows, 1, {(rows - 2, 2): last, (rows - 1, 0): last})
    split_gradient(patches, grad_ref, keep_ref, send_ref)


def add_pairs(keep_first, came_first, keep_second, came_second, out_ref):
    taps = keep_first.shape[1]
    out_ref[:, :taps] = (keep_first[...].astype(F32) + came_first[...].astype(F32)).astype(BF16)
    out_ref[:, taps:] = (keep_second[...].astype(F32) + came_second[...].astype(F32)).astype(BF16)


def sum_tiles(in_ref, out_ref, rows_ref):
    chips, taps, share, channels = in_ref.shape
    groups, width, _ = out_ref.shape
    total = in_ref[0].astype(F32)
    for chip in range(1, chips):
        total = total + in_ref[chip].astype(F32)
    rows_ref[...] = jnp.zeros_like(rows_ref)
    rows_ref[: taps * share] = total.reshape(taps * share, channels)
    out_ref[...] = rows_ref[...].T.reshape(groups, width, -1).astype(BF16)


def sum_frames(scale, in_ref, out_ref):
    groups = in_ref.shape[0]
    total = in_ref[0].astype(F32)
    for group in range(1, groups):
        total = total + in_ref[group].astype(F32)
    out_ref[...] = total.T[: out_ref.shape[0]] * scale


def shape_of(*dims, dtype=BF16):
    return jax.ShapeDtypeStruct(dims, dtype)


def local(saved_codes, saved_scales, kernels, norm_gains, cotangent):
    frames, rows, columns, channels = saved_codes.shape
    tiles, groups = lax.axis_size("tile"), lax.axis_size("frame")
    cells = frames * rows * columns
    block = (columns, channels)

    def patch_scratch(count):
        return (pltpu.VMEM((count, TAPS * channels), BF16),)

    def next_frames(value):
        return lax.ppermute(value, "frame", [(i, i + 1) for i in range(groups - 1)])

    def earlier_frames(value):
        return lax.ppermute(value, "frame", [(i + 1, i) for i in range(groups - 1)])

    def from_below(value):
        return lax.ppermute(value, "tile", [((i + 1) % tiles, i) for i in range(tiles)])

    def from_above(value):
        return lax.ppermute(value, "tile", [(i, (i + 1) % tiles) for i in range(tiles)])

    def partner(value):
        return lax.ppermute(value, "tile", [(i, i ^ 1) for i in range(tiles)])

    own_0 = (saved_codes.astype(F32) * saved_scales[..., None]).astype(BF16)
    earlier_0 = next_frames(own_0)
    sent = jnp.concatenate(
        [
            earlier_0.reshape(frames * rows, *block),
            own_0.reshape(frames * rows, *block),
            cotangent[:, :2].reshape(frames * 2, *block),
        ],
        axis=0,
    )
    below = from_below(sent)
    below_0, low = below[: 2 * frames * rows], below[2 * frames * rows :]
    wide = 2 * rows - 2
    own_1, pre_0 = call(
        first_forward,
        (shape_of(wide, frames, *block), shape_of(cells, channels, dtype=F32)),
        own_0,
        earlier_0,
        below_0,
        kernels[0],
        norm_gains,
        scratch=patch_scratch(wide * frames * columns),
    )
    earlier_1 = next_frames(own_1)
    grad_shape = shape_of(rows, frames, *block)
    grad_1 = call(
        second_forward,
        grad_shape,
        own_1,
        earlier_1,
        cotangent,
        low,
        kernels[1],
        norm_gains,
        scratch=patch_scratch(cells),
    )

    def with_neighbours(grad):
        later = earlier_frames(grad)
        above = from_above(jnp.concatenate([grad[rows - 2 :], later[rows - 2 :]], axis=1))
        return later, above

    share = channels // tiles
    part = shape_of(tiles // 2, TAPS, share, channels)
    later_1, above_1 = with_neighbours(grad_1)
    keep_1, send_1 = call(
        second_kernel_gradient, (part, part), own_1, earlier_1, grad_1, scratch=patch_scratch(cells)
    )
    came_1 = partner(send_1)
    grad_0 = call(
        second_backward,
        grad_shape,
        grad_1,
        later_1,
        above_1,
        kernels[1],
        norm_gains,
        pre_0,
        scratch=patch_scratch(cells),
    )
    keep_0, send_0 = call(
        first_kernel_gradient,
        (part, part),
        own_0,
        earlier_0,
        below_0,
        grad_0,
        scratch=patch_scratch(cells),
    )
    came_0 = partner(send_0)
    paired = call(
        add_pairs, shape_of(tiles // 2, 2 * TAPS, share, channels), keep_0, came_0, keep_1, came_1
    )
    by_core = [list(range(core, tiles, 2)) for core in range(2)]
    arrived = lax.all_to_all(
        paired, "tile", split_axis=0, concat_axis=0, tiled=True, axis_index_groups=by_core
    )
    later_0, above_0 = with_neighbours(grad_0)
    input_grad = call(
        first_backward,
        shape_of(frames, rows, *block),
        grad_0,
        later_0,
        above_0,
        kernels[0],
        scratch=patch_scratch(cells),
    )
    used = 2 * TAPS * share
    padded = -(-used // 128) * 128
    by_frame = call(
        sum_tiles,
        shape_of(groups, channels // groups, padded),
        arrived,
        scratch=(pltpu.VMEM((padded, channels), F32),),
    )
    spread = lax.all_to_all(by_frame, "frame", split_axis=0, concat_axis=0, tiled=True)
    scale = 1.0 / math.sqrt(cells * tiles * groups)
    summed = call(
        lambda *refs: sum_frames(scale, *refs),
        shape_of(used, channels // groups, dtype=F32),
        spread,
    )
    return (input_grad, summed.reshape(2 * TAPS, share, channels // groups))


def solution(mesh):
    in_specs = (
        P("frame", "tile", None, None),
        P("frame", "tile", None),
        P(),
        P(),
        P("frame", "tile", None, None),
    )
    out_specs = (P("frame", "tile", None, None), P(None, "tile", "frame"))
    return jax.shard_map(local, mesh=mesh, in_specs=in_specs, out_specs=out_specs, check_vma=False)
```

time: 180 us -> 109 us (0.61)
  the two profiles are of different devices: /device:TPU:40 before, /device:TPU:2 now
where the time goes in v2:
time: 109 us
  waiting for transfers between devices  49 us (45%)
  starting transfers between devices  46.5 us (43%)
  Pallas kernels  8.07 us (7%)
  local copies, waits for them, and re-layouts  3.1 us (3%)
    all_to_all x1, starting transfers between devices, local(): lax.all_to_all(by_frame, 'frame', split_axis=0, concat_axis=0, tiled=True)  20.5 us
    all_to_all x1, waiting for transfers between devices, local(): lax.all_to_all(paired, 'tile', split_axis=0, concat_axis=0, tiled=True, a...  15.7 us
    ppermute x2, waiting for transfers between devices, earlier_frames(): return lax.ppermute(value, 'frame', [(i + 1, i) for i in range(groups - 1)])  13.2 us
    ppermute x2, waiting for transfers between devices, from_above(): lax.ppermute(value, 'tile', [(i, (i + 1) % tiles) for i in range(tiles)])  8.81 us
    ppermute x2, waiting for transfers between devices, next_frames(): return lax.ppermute(value, 'frame', [(i, i + 1) for i in range(groups - 1)])  8.32 us
    pallas_call x9, Pallas kernels, call(): pl.pallas_call(kernel, out_shape=out_shape, scratch_shapes=list(scratch),...  8.07 us
    ppermute x2, starting transfers between devices, next_frames(): return lax.ppermute(value, 'frame', [(i, i + 1) for i in range(groups - 1)])  6.8 us
    all_to_all x1, starting transfers between devices, local(): lax.all_to_all(paired, 'tile', split_axis=0, concat_axis=0, tiled=True, a...  5.29 us
  transfers between devices with their start and end apart: 11, of which 9 were waited for; matrix products, arithmetic and copies ran while one was open for 2% of the time, Pallas kernels for 3%

profile of v2, /device:TPU:2, one launch (start us, length us, event | category | flops | bytes accessed | tf_op | source)
XLA Modules:
  0.0 108.5 jit_solution(1742417370129955308)
XLA Ops:
  0.6 0.9 multiply_convert_fusion.own_ref
  1.6 3.4 %collective-permute-start = (bf16[2,4,32,128]{3,2,1,0:T(8,128)(2,1)S(1)}, bf16[2,4,32,128]{3,2,1,0:T(8,128)(2,1)S(1)}, u32[]{:S(2)}, u32[]{:S(2)}) collective-permute-start(bf16[2,4,32,128]{3,2,1,0:T(8,128)(2,1)S(1)} %multiply_convert_fusion.own_ref), channel_id=1, source_target_pairs={{0,32},{32,64},{64,96},{96,128},{128,160},{160,192},{192,224},{224... | collective-permute-start | bytes 196616 | tf_op jit(solution)/shard_map/ppermute | solution.py:245
  5.0 0.8 slice.29
  5.7 5.2 %collective-permute-done.earlier_ref = bf16[2,4,32,128]{3,2,1,0:T(8,128)(2,1)S(1)} collective-permute-done((bf16[2,4,32,128]{3,2,1,0:T(8,128)(2,1)S(1)}, bf16[2,4,32,128]{3,2,1,0:T(8,128)(2,1)S(1)}, u32[]{:S(2)}, u32[]{:S(2)}) %collective-permute-start) | collective-permute-done | bytes 65568 | tf_op jit(solution)/shard_map/ppermute | solution.py:245
  11.0 0.0 copy-start.1
  11.0 0.0 copy-start
  11.0 2.4 %collective-permute-start.1 = (bf16[20,32,128]{2,1,0:T(8,128)(2,1)S(1)}, bf16[20,32,128]{2,1,0:T(8,128)(2,1)S(1)}, u32[]{:S(2)}, u32[]{:S(2)}) collective-permute-start(bf16[20,32,128]{2,1,0:T(8,128)(2,1)S(1)} %pad_maximum_fusion), channel_id=1, source_target_pairs={{1,0},{2,1},{3,2},{4,3},{5,4},{6,5},{7,6},{8,7},{9,8},{10,9},{11,1... | collective-permute-start | bytes 491528 | tf_op jit(solution)/shard_map/ppermute | solution.py:251
  13.4 1.6 %slice_bitcast_fusion = (bf16[27,128,128]{2,1,0:T(8,128)(2,1)S(1)}, bf16[27,128,128]{2,1,0:T(8,128)(2,1)S(1)}) fusion(bf16[2,27,128,128]{3,2,1,0:T(8,128)(2,1)} %param.7), kind=kLoop, calls=%fused_computation | loop fusion | bytes 3538944 | tf_op jit(solution)/shard_map/squeeze | solution.py:291
  15.0 1.2 %collective-permute-done.1 = bf16[20,32,128]{2,1,0:T(8,128)(2,1)S(1)} collective-permute-done((bf16[20,32,128]{2,1,0:T(8,128)(2,1)S(1)}, bf16[20,32,128]{2,1,0:T(8,128)(2,1)S(1)}, u32[]{:S(2)}, u32[]{:S(2)}) %collective-permute-start.1) | collective-permute-done | bytes 163872 | tf_op jit(solution)/shard_map/ppermute | solution.py:251
  16.2 0.0 copy-done.1
  16.2 1.1 shard_map.68
  17.3 3.4 %collective-permute-start.2 = (bf16[6,2,32,128]{3,2,1,0:T(8,128)(2,1)S(1)}, bf16[6,2,32,128]{3,2,1,0:T(8,128)(2,1)S(1)}, u32[]{:S(2)}, u32[]{:S(2)}) collective-permute-start(bf16[6,2,32,128]{3,2,1,0:T(8,128)(2,1)S(1)} %get-tuple-element.8.own_ref), channel_id=1, source_target_pairs={{0,32},{32,64},{64,96},{96,128},{128,160},{160,192},{192,224},{224... | collective-permute-start | bytes 294920 | tf_op jit(solution)/shard_map/ppermute | solution.py:245
  20.7 3.1 %collective-permute-done.2.earlier_ref = bf16[6,2,32,128]{3,2,1,0:T(8,128)(2,1)S(1)} collective-permute-done((bf16[6,2,32,128]{3,2,1,0:T(8,128)(2,1)S(1)}, bf16[6,2,32,128]{3,2,1,0:T(8,128)(2,1)S(1)}, u32[]{:S(2)}, u32[]{:S(2)}) %collective-permute-start.2) | collective-permute-done | bytes 98336 | tf_op jit(solution)/shard_map/ppermute | solution.py:245
  23.8 0.0 copy-done
  23.8 0.9 shard_map.69.own_ref.grad_ref
  24.7 1.9 %collective-permute-start.3 = (bf16[4,2,32,128]{3,2,1,0:T(8,128)(2,1)S(1)}, bf16[4,2,32,128]{3,2,1,0:T(8,128)(2,1)S(1)}, u32[]{:S(2)}, u32[]{:S(2)}) collective-permute-start(bf16[4,2,32,128]{3,2,1,0:T(8,128)(2,1)S(1)} %shard_map.69.own_ref.grad_ref), channel_id=1, source_target_pairs={{32,0},{64,32},{96,64},{128,96},{160,128},{192,160},{224,192},{256... | collective-permute-start | bytes 196616 | tf_op jit(solution)/shard_map/ppermute | solution.py:248
  26.6 5.2 %collective-permute-done.3.later_ref = bf16[4,2,32,128]{3,2,1,0:T(8,128)(2,1)S(1)} collective-permute-done((bf16[4,2,32,128]{3,2,1,0:T(8,128)(2,1)S(1)}, bf16[4,2,32,128]{3,2,1,0:T(8,128)(2,1)S(1)}, u32[]{:S(2)}, u32[]{:S(2)}) %collective-permute-start.3) | collective-permute-done | bytes 65568 | tf_op jit(solution)/shard_map/ppermute | solution.py:248
  31.9 1.9 %collective-permute-start.4 = (bf16[2,4,32,128]{3,2,1,0:T(8,128)(2,1)S(1)}, bf16[2,4,32,128]{3,2,1,0:T(8,128)(2,1)S(1)}, u32[]{:S(2)}, u32[]{:S(2)}) collective-permute-start(bf16[2,4,32,128]{3,2,1,0:T(8,128)(2,1)S(1)} %pad_maximum_fusion.1), channel_id=1, source_target_pairs={{0,1},{1,2},{2,3},{3,4},{4,5},{5,6},{6,7},{7,8},{8,9},{9,10},{10,1... | collective-permute-start | bytes 196616 | tf_op jit(solution)/shard_map/ppermute | solution.py:254
  33.8 0.8 shard_map.73
  34.6 1.9 %collective-permute-start.8 = (bf16[16,27,4,128]{3,2,1,0:T(4,128)(2,1)S(1)}, bf16[16,27,4,128]{3,2,1,0:T(4,128)(2,1)S(1)}, u32[]{:S(2)}, u32[]{:S(2)}) collective-permute-start(bf16[16,27,4,128]{3,2,1,0:T(4,128)(2,1)S(1)} %get-tuple-element.13), channel_id=1, source_target_pairs={{0,1},{1,0},{2,3},{3,2},{4,5},{5,4},{6,7},{7,6},{8,9},{9,8},{10,11... | collective-permute-start | bytes 1327112 | tf_op jit(solution)/shard_map/ppermute | solution.py:257
  36.5 3.0 %collective-permute-done.4.above_ref = bf16[2,4,32,128]{3,2,1,0:T(8,128)(2,1)S(1)} collective-permute-done((bf16[2,4,32,128]{3,2,1,0:T(8,128)(2,1)S(1)}, bf16[2,4,32,128]{3,2,1,0:T(8,128)(2,1)S(1)}, u32[]{:S(2)}, u32[]{:S(2)}) %collective-permute-start.4) | collective-permute-done | bytes 65568 | tf_op jit(solution)/shard_map/ppermute | solution.py:254
  39.6 0.8 shard_map.70.own_ref.grad_ref
  40.4 0.8 shard_map.72
  41.2 1.9 %collective-permute-start.7 = (bf16[16,27,4,128]{3,2,1,0:T(4,128)(2,1)S(1)}, bf16[16,27,4,128]{3,2,1,0:T(4,128)(2,1)S(1)}, u32[]{:S(2)}, u32[]{:S(2)}) collective-permute-start(bf16[16,27,4,128]{3,2,1,0:T(4,128)(2,1)S(1)} %get-tuple-element.11), channel_id=1, source_target_pairs={{0,1},{1,0},{2,3},{3,2},{4,5},{5,4},{6,7},{7,6},{8,9},{9,8},{10,11... | collective-permute-start | bytes 1327112 | tf_op jit(solution)/shard_map/ppermute | solution.py:257
  43.1 0.0 collective-permute-done.8.came_second
  43.1 1.7 %collective-permute-done.7.came_first = bf16[16,27,4,128]{3,2,1,0:T(4,128)(2,1)S(1)} collective-permute-done((bf16[16,27,4,128]{3,2,1,0:T(4,128)(2,1)S(1)}, bf16[16,27,4,128]{3,2,1,0:T(4,128)(2,1)S(1)}, u32[]{:S(2)}, u32[]{:S(2)}) %collective-permute-start.7) | collective-permute-done | bytes 442400 | tf_op jit(solution)/shard_map/ppermute | solution.py:257
  44.9 1.4 %shard_map.74 = bf16[16,54,4,128]{3,2,1,0:T(4,128)(2,1)} custom-call(bf16[16,27,4,128]{3,2,1,0:T(4,128)(2,1)S(1)} %get-tuple-element.10.keep_first, bf16[16,27,4,128]{3,2,1,0:T(4,128)(2,1)S(1)} %collective-permute-done.7.came_first, bf16[16,27,4,128]{3,2,1,0:T(4,128)(2,1)S(1)} %get-tuple-element.12.keep_second, ...), custom_call_target="tpu_custom_call" | custom-call | tf_op jit(solution)/shard_map/pallas_call | solution.py:17
  46.2 5.3 %all-to-all-start = ((bf16[16,54,4,128]{3,2,1,0:T(4,128)(2,1)}), bf16[16,54,4,128]{3,2,1,0:T(4,128)(2,1)S(1)}, u32[]{:S(2)}, u32[]{:S(2)}) async-start(bf16[16,54,4,128]{3,2,1,0:T(4,128)(2,1)} %shard_map.74), calls=%async_computation | async-start | bytes 1769472 | tf_op jit(solution)/shard_map/all_to_all | solution.py:333
  51.5 1.9 %collective-permute-start.5 = (bf16[4,2,32,128]{3,2,1,0:T(8,128)(2,1)S(1)}, bf16[4,2,32,128]{3,2,1,0:T(8,128)(2,1)S(1)}, u32[]{:S(2)}, u32[]{:S(2)}) collective-permute-start(bf16[4,2,32,128]{3,2,1,0:T(8,128)(2,1)S(1)} %shard_map.70.own_ref.grad_ref), channel_id=1, source_target_pairs={{32,0},{64,32},{96,64},{128,96},{160,128},{192,160},{224,192},{256... | collective-permute-start | bytes 196616 | tf_op jit(solution)/shard_map/ppermute | solution.py:248
  53.5 7.9 %collective-permute-done.5.later_ref = bf16[4,2,32,128]{3,2,1,0:T(8,128)(2,1)S(1)} collective-permute-done((bf16[4,2,32,128]{3,2,1,0:T(8,128)(2,1)S(1)}, bf16[4,2,32,128]{3,2,1,0:T(8,128)(2,1)S(1)}, u32[]{:S(2)}, u32[]{:S(2)}) %collective-permute-start.5) | collective-permute-done | bytes 65568 | tf_op jit(solution)/shard_map/ppermute | solution.py:248
  61.4 15.7 %all-to-all-done.in_ref = bf16[16,54,4,128]{3,2,1,0:T(4,128)(2,1)S(1)} async-done(((bf16[16,54,4,128]{3,2,1,0:T(4,128)(2,1)}), bf16[16,54,4,128]{3,2,1,0:T(4,128)(2,1)S(1)}, u32[]{:S(2)}, u32[]{:S(2)}) %all-to-all-start) | async-done | bytes 884768 | tf_op jit(solution)/shard_map/all_to_all | solution.py:333
  77.2 0.9 shard_map.75
  78.1 20.5 %all-to-all-start.1 = ((bf16[16,8,256]{2,1,0:T(8,128)(2,1)}), bf16[16,8,256]{2,1,0:T(8,128)(2,1)S(1)}, u32[]{:S(2)}, u32[]{:S(2)}) async-start(bf16[16,8,256]{2,1,0:T(8,128)(2,1)} %shard_map.75), calls=%async_computation.1 | async-start | bytes 131072 | tf_op jit(solution)/shard_map/all_to_all | solution.py:354
  98.7 1.9 %collective-permute-start.6 = (bf16[2,4,32,128]{3,2,1,0:T(8,128)(2,1)S(1)}, bf16[2,4,32,128]{3,2,1,0:T(8,128)(2,1)S(1)}, u32[]{:S(2)}, u32[]{:S(2)}) collective-permute-start(bf16[2,4,32,128]{3,2,1,0:T(8,128)(2,1)S(1)} %pad_maximum_fusion.2), channel_id=1, source_target_pairs={{0,1},{1,2},{2,3},{3,4},{4,5},{5,6},{6,7},{7,8},{8,9},{9,10},{10,1... | collective-permute-start | bytes 196616 | tf_op jit(solution)/shard_map/ppermute | solution.py:254
  100.6 5.8 %collective-permute-done.6.above_ref = bf16[2,4,32,128]{3,2,1,0:T(8,128)(2,1)S(1)} collective-permute-done((bf16[2,4,32,128]{3,2,1,0:T(8,128)(2,1)S(1)}, bf16[2,4,32,128]{3,2,1,0:T(8,128)(2,1)S(1)}, u32[]{:S(2)}, u32[]{:S(2)}) %collective-permute-start.6) | collective-permute-done | bytes 65568 | tf_op jit(solution)/shard_map/ppermute | solution.py:254
  106.3 1.3 %shard_map.71 = bf16[2,4,32,128]{3,2,1,0:T(8,128)(2,1)} custom-call(bf16[4,2,32,128]{3,2,1,0:T(8,128)(2,1)S(1)} %shard_map.70.own_ref.grad_ref, bf16[4,2,32,128]{3,2,1,0:T(8,128)(2,1)S(1)} %collective-permute-done.5.later_ref, bf16[2,4,32,128]{3,2,1,0:T(8,128)(2,1)S(1)} %collective-permute-done.6.above_ref, ...), custom_call_target="tpu_custom_call" | custom-call | tf_op jit(solution)/shard_map/pallas_call | solution.py:17
  107.7 0.0 all-to-all-done.1.refs_0_
  107.7 0.1 shard_map.76
  107.8 0.7 copy.7
  (9 shorter events, 0.1 us)
Async XLA Ops:
  1.6 9.4 %collective-permute-start = (bf16[2,4,32,128]{3,2,1,0:T(8,128)(2,1)S(1)}, bf16[2,4,32,128]{3,2,1,0:T(8,128)(2,1)S(1)}, u32[]{:S(2)}, u32[]{:S(2)}) collective-permute-start(bf16[2,4,32,128]{3,2,1,0:T(8,128)(2,1)S(1)} %multiply_convert_fusion.own_ref), channel_id=1, source_target_pairs={{0,32},{32,64},{64,96},{96,128},{128,160},{160,192},{192,224},{224... | collective-permute-start | bytes 196616 | tf_op jit(solution)/shard_map/ppermute | solution.py:245
  11.0 5.2 %copy-start.1 = (f32[2,128]{1,0:T(2,128)S(1)}, f32[2,128]{1,0:T(2,128)}, u32[]{:S(2)}) copy-start(f32[2,128]{1,0:T(2,128)} %gain_ref.5) | copy-start | bytes 3076
  11.0 12.8 %copy-start = (bf16[2,4,32,128]{3,2,1,0:T(8,128)(2,1)S(1)}, bf16[2,4,32,128]{3,2,1,0:T(8,128)(2,1)}, u32[]{:S(2)}) copy-start(bf16[2,4,32,128]{3,2,1,0:T(8,128)(2,1)} %top_ref.1) | copy-start | bytes 196612
  11.0 5.2 %collective-permute-start.1 = (bf16[20,32,128]{2,1,0:T(8,128)(2,1)S(1)}, bf16[20,32,128]{2,1,0:T(8,128)(2,1)S(1)}, u32[]{:S(2)}, u32[]{:S(2)}) collective-permute-start(bf16[20,32,128]{2,1,0:T(8,128)(2,1)S(1)} %pad_maximum_fusion), channel_id=1, source_target_pairs={{1,0},{2,1},{3,2},{4,3},{5,4},{6,5},{7,6},{8,7},{9,8},{10,9},{11,1... | collective-permute-start | bytes 491528 | tf_op jit(solution)/shard_map/ppermute | solution.py:251
  17.3 6.5 %collective-permute-start.2 = (bf16[6,2,32,128]{3,2,1,0:T(8,128)(2,1)S(1)}, bf16[6,2,32,128]{3,2,1,0:T(8,128)(2,1)S(1)}, u32[]{:S(2)}, u32[]{:S(2)}) collective-permute-start(bf16[6,2,32,128]{3,2,1,0:T(8,128)(2,1)S(1)} %get-tuple-element.8.own_ref), channel_id=1, source_target_pairs={{0,32},{32,64},{64,96},{96,128},{128,160},{160,192},{192,224},{224... | collective-permute-start | bytes 294920 | tf_op jit(solution)/shard_map/ppermute | solution.py:245
  24.7 7.2 %collective-permute-start.3 = (bf16[4,2,32,128]{3,2,1,0:T(8,128)(2,1)S(1)}, bf16[4,2,32,128]{3,2,1,0:T(8,128)(2,1)S(1)}, u32[]{:S(2)}, u32[]{:S(2)}) collective-permute-start(bf16[4,2,32,128]{3,2,1,0:T(8,128)(2,1)S(1)} %shard_map.69.own_ref.grad_ref), channel_id=1, source_target_pairs={{32,0},{64,32},{96,64},{128,96},{160,128},{192,160},{224,192},{256... | collective-permute-start | bytes 196616 | tf_op jit(solution)/shard_map/ppermute | solution.py:248
  31.9 7.7 %collective-permute-start.4 = (bf16[2,4,32,128]{3,2,1,0:T(8,128)(2,1)S(1)}, bf16[2,4,32,128]{3,2,1,0:T(8,128)(2,1)S(1)}, u32[]{:S(2)}, u32[]{:S(2)}) collective-permute-start(bf16[2,4,32,128]{3,2,1,0:T(8,128)(2,1)S(1)} %pad_maximum_fusion.1), channel_id=1, source_target_pairs={{0,1},{1,2},{2,3},{3,4},{4,5},{5,6},{6,7},{7,8},{8,9},{9,10},{10,1... | collective-permute-start | bytes 196616 | tf_op jit(solution)/shard_map/ppermute | solution.py:254
  34.6 8.5 %collective-permute-start.8 = (bf16[16,27,4,128]{3,2,1,0:T(4,128)(2,1)S(1)}, bf16[16,27,4,128]{3,2,1,0:T(4,128)(2,1)S(1)}, u32[]{:S(2)}, u32[]{:S(2)}) collective-permute-start(bf16[16,27,4,128]{3,2,1,0:T(4,128)(2,1)S(1)} %get-tuple-element.13), channel_id=1, source_target_pairs={{0,1},{1,0},{2,3},{3,2},{4,5},{5,4},{6,7},{7,6},{8,9},{9,8},{10,11... | collective-permute-start | bytes 1327112 | tf_op jit(solution)/shard_map/ppermute | solution.py:257
  41.2 3.7 %collective-permute-start.7 = (bf16[16,27,4,128]{3,2,1,0:T(4,128)(2,1)S(1)}, bf16[16,27,4,128]{3,2,1,0:T(4,128)(2,1)S(1)}, u32[]{:S(2)}, u32[]{:S(2)}) collective-permute-start(bf16[16,27,4,128]{3,2,1,0:T(4,128)(2,1)S(1)} %get-tuple-element.11), channel_id=1, source_target_pairs={{0,1},{1,0},{2,3},{3,2},{4,5},{5,4},{6,7},{7,6},{8,9},{9,8},{10,11... | collective-permute-start | bytes 1327112 | tf_op jit(solution)/shard_map/ppermute | solution.py:257
  46.2 30.9 %all-to-all-start = ((bf16[16,54,4,128]{3,2,1,0:T(4,128)(2,1)}), bf16[16,54,4,128]{3,2,1,0:T(4,128)(2,1)S(1)}, u32[]{:S(2)}, u32[]{:S(2)}) async-start(bf16[16,54,4,128]{3,2,1,0:T(4,128)(2,1)} %shard_map.74), calls=%async_computation | async-start | bytes 1769472 | tf_op jit(solution)/shard_map/all_to_all | solution.py:333
  51.5 9.9 %collective-permute-start.5 = (bf16[4,2,32,128]{3,2,1,0:T(8,128)(2,1)S(1)}, bf16[4,2,32,128]{3,2,1,0:T(8,128)(2,1)S(1)}, u32[]{:S(2)}, u32[]{:S(2)}) collective-permute-start(bf16[4,2,32,128]{3,2,1,0:T(8,128)(2,1)S(1)} %shard_map.70.own_ref.grad_ref), channel_id=1, source_target_pairs={{32,0},{64,32},{96,64},{128,96},{160,128},{192,160},{224,192},{256... | collective-permute-start | bytes 196616 | tf_op jit(solution)/shard_map/ppermute | solution.py:248
  78.1 29.6 %all-to-all-start.1 = ((bf16[16,8,256]{2,1,0:T(8,128)(2,1)}), bf16[16,8,256]{2,1,0:T(8,128)(2,1)S(1)}, u32[]{:S(2)}, u32[]{:S(2)}) async-start(bf16[16,8,256]{2,1,0:T(8,128)(2,1)} %shard_map.75), calls=%async_computation.1 | async-start | bytes 131072 | tf_op jit(solution)/shard_map/all_to_all | solution.py:354
  98.7 7.7 %collective-permute-start.6 = (bf16[2,4,32,128]{3,2,1,0:T(8,128)(2,1)S(1)}, bf16[2,4,32,128]{3,2,1,0:T(8,128)(2,1)S(1)}, u32[]{:S(2)}, u32[]{:S(2)}) collective-permute-start(bf16[2,4,32,128]{3,2,1,0:T(8,128)(2,1)S(1)} %pad_maximum_fusion.2), channel_id=1, source_target_pairs={{0,1},{1,2},{2,3},{3,4},{4,5},{5,6},{6,7},{7,8},{8,9},{9,10},{10,1... | collective-permute-start | bytes 196616 | tf_op jit(solution)/shard_map/ppermute | solution.py:254

commit v3 on v2

--- a/solution.py
+++ b/solution.py
@@ -54,12 +54,8 @@
     return [[shifted_columns(block) for block in row] for row in rows]
 
 
-def forward_rows(rows, frames, own_ref, earlier_ref):
-    return [
-        [earlier_ref[row, frame] for frame in range(frames)]
-        + [own_ref[row, frame] for frame in range(frames)]
-        for row in range(rows)
-    ]
+def block_rows(ref):
+    return [[ref[row, frame] for frame in range(ref.shape[1])] for row in range(ref.shape[0])]
 
 
 def silu_parts(pre_norm, gain):
@@ -79,42 +75,49 @@
     return lax.axis_index("tile") == lax.axis_size("tile") - 1
 
 
-def first_rows(own_ref, earlier_ref, below_ref, frames, rows, total):
+def first_rows(parts, below_ref, total):
+    frames, rows = parts[0].shape[:2]
+    skipped = (3 - len(parts)) * frames
     result = []
     for row in range(total):
         if row < rows:
-            result.append(
-                [earlier_ref[frame, row] for frame in range(frames)]
-                + [own_ref[frame, row] for frame in range(frames)]
-            )
+            result.append([part[frame, row] for part in parts for frame in range(frames)])
         else:
             result.append(
-                [below_ref[frame * rows + row - rows] for frame in range(2 * frames)]
+                [
+                    below_ref[(skipped + frame) * rows + row - rows]
+                    for frame in range(len(parts) * frames)
+                ]
             )
     return result
 
 
-def first_forward(own_ref, earlier_ref, below_ref, kernel_ref, gain_ref, next_ref, pre_ref, patches):
+def forward(
+    own_ref, earlier_ref, earliest_ref, below_ref, top_ref, first_kernel_ref, second_kernel_ref,
+    gain_ref, next_ref, pre_ref, grad_ref, wide_patches, patches,
+):
     frames, rows, columns, channels = own_ref.shape
     last = at_last_tile()
-    window = window_of(first_rows(own_ref, earlier_ref, below_ref, frames, rows, 2 * rows))
-    fill(patches, window, frames, 2 * rows - 2, 1, {(rows - 2, 2): last, (rows - 1, 0): last})
+    window = window_of(first_rows((earliest_ref, earlier_ref, own_ref), below_ref, 2 * rows))
+    wide, deep = 2 * rows - 2, 2 * frames
+    fill(wide_patches, window, deep, wide, 1, {(rows - 2, 2): last, (rows - 1, 0): last})
     pre_norm = jnp.dot(
-        patches[...], kernel_ref[...].reshape(TAPS * channels, channels), preferred_element_type=F32
+        wide_patches[...],
+        first_kernel_ref[...].reshape(TAPS * channels, channels),
+        preferred_element_type=F32,
     )
     _, normed, sigma = silu_parts(pre_norm, gain_ref[0:1])
     next_ref[...] = (normed * sigma).astype(BF16).reshape(next_ref.shape)
-    pre_ref[...] = pre_norm[: pre_ref.shape[0]]
-
-
-def second_forward(own_ref, earlier_ref, top_ref, low_ref, kernel_ref, gain_ref, grad_ref, patches):
-    total, frames, columns, channels = own_ref.shape
-    rows = total - 2
-    last = at_last_tile()
-    window = window_of(forward_rows(total, frames, own_ref, earlier_ref))
+    own_cells = frames * columns
+    for row in range(rows):
+        start = row * deep * columns + own_cells
+        pre_ref[row * own_cells : (row + 1) * own_cells] = pre_norm[start : start + own_cells]
+    window = window_of(block_rows(next_ref))
     fill(patches, window, frames, rows, 1, {(rows - 3, 2): last, (rows - 2, 0): last})
     pre_norm = jnp.dot(
-        patches[...], kernel_ref[...].reshape(TAPS * channels, channels), preferred_element_type=F32
+        patches[...],
+        second_kernel_ref[...].reshape(TAPS * channels, channels),
+        preferred_element_type=F32,
     )
     spread = []
     for row in range(rows):
@@ -122,7 +125,7 @@
             if row < rows - 2:
                 spread.append(top_ref[frame, row + 2])
             else:
-                spread.append(low_ref[frame * 2 + row - rows + 2])
+                spread.append(below_ref[3 * frames * rows + frame * 2 + row - rows + 2])
     upstream = jnp.concatenate(spread, axis=0).astype(F32)
     grad_ref[...] = pre_norm_gradient(pre_norm, gain_ref[1:2], upstream).reshape(grad_ref.shape)
 
@@ -158,7 +161,7 @@
     grad_ref[...] = pre_norm_gradient(pre_ref[...], gain_ref[0:1], upstream).reshape(grad_ref.shape)
 
 
-def first_backward(own_ref, later_ref, above_ref, kernel_ref, out_ref, patches):
+def first_backward(own_ref, later_ref, above_ref, kernel_ref, out_ref, token_ref, patches):
     rows, frames, columns, channels = own_ref.shape
     first, last = lax.axis_index("tile") == 0, at_last_tile()
     window = window_of(backward_rows(own_ref, later_ref, above_ref, frames))
@@ -168,6 +171,7 @@
         for frame in range(frames):
             cell = (row * frames + frame) * columns
             out_ref[frame, row] = grad[cell : cell + columns]
+    token_ref[...] = grad[: token_ref.shape[0]].astype(F32)
 
 
 def split_gradient(patches, grad_ref, keep_ref, send_ref):
@@ -186,11 +190,10 @@
         send_ref[:, tap] = jnp.where(odd, even_part, odd_part).astype(BF16)
 
 
-def second_kernel_gradient(own_ref, earlier_ref, grad_ref, keep_ref, send_ref, patches):
-    total, frames, columns, channels = own_ref.shape
-    rows = total - 2
+def second_kernel_gradient(next_ref, grad_ref, keep_ref, send_ref, patches):
+    rows, frames, _, _ = grad_ref.shape
     last = at_last_tile()
-    window = window_of(forward_rows(total, frames, own_ref, earlier_ref))
+    window = window_of(block_rows(next_ref))
     fill(patches, window, frames, rows, 1, {(rows - 3, 2): last, (rows - 2, 0): last})
     split_gradient(patches, grad_ref, keep_ref, send_ref)
 
@@ -198,7 +201,7 @@
 def first_kernel_gradient(own_ref, earlier_ref, below_ref, grad_ref, keep_ref, send_ref, patches):
     frames, rows, columns, channels = own_ref.shape
     last = at_last_tile()
-    window = window_of(first_rows(own_ref, earlier_ref, below_ref, frames, rows, rows + 2))
+    window = window_of(first_rows((earlier_ref, own_ref), below_ref, rows + 2))
     fill(patches, window, frames, rows, 1, {(rows - 2, 2): last, (rows - 1, 0): last})
     split_gradient(patches, grad_ref, keep_ref, send_ref)
 
@@ -209,14 +212,17 @@
     out_ref[:, taps:] = (keep_second[...].astype(F32) + came_second[...].astype(F32)).astype(BF16)
 
 
-def sum_tiles(in_ref, out_ref, rows_ref):
+def sum_tiles(in_ref, token_ref, out_ref, rows_ref):
+    del token_ref
     chips, taps, share, channels = in_ref.shape
     groups, width, _ = out_ref.shape
     total = in_ref[0].astype(F32)
     for chip in range(1, chips):
         total = total + in_ref[chip].astype(F32)
     rows_ref[...] = jnp.zeros_like(rows_ref)
-    rows_ref[: taps * share] = total.reshape(taps * share, channels)
+    stride = rows_ref.shape[0] // share
+    for row in range(share):
+        rows_ref[row * stride : row * stride + taps] = total[:, row]
     out_ref[...] = rows_ref[...].T.reshape(groups, width, -1).astype(BF16)
 
 
@@ -225,7 +231,10 @@
     total = in_ref[0].astype(F32)
     for group in range(1, groups):
         total = total + in_ref[group].astype(F32)
-    out_ref[...] = total.T[: out_ref.shape[0]] * scale
+    share, _, taps = out_ref.shape
+    stride = total.shape[1] // share
+    for row in range(share):
+        out_ref[row] = total[:, row * stride : row * stride + taps] * scale
 
 
 def shape_of(*dims, dtype=BF16):
@@ -241,8 +250,8 @@
     def patch_scratch(count):
         return (pltpu.VMEM((count, TAPS * channels), BF16),)
 
-    def next_frames(value):
-        return lax.ppermute(value, "frame", [(i, i + 1) for i in range(groups - 1)])
+    def next_frames(value, steps):
+        return lax.ppermute(value, "frame", [(i, i + steps) for i in range(groups - steps)])
 
     def earlier_frames(value):
         return lax.ppermute(value, "frame", [(i + 1, i) for i in range(groups - 1)])
@@ -257,9 +266,10 @@
         return lax.ppermute(value, "tile", [(i, i ^ 1) for i in range(tiles)])
 
     own_0 = (saved_codes.astype(F32) * saved_scales[..., None]).astype(BF16)
-    earlier_0 = next_frames(own_0)
+    earlier_0, earliest_0 = next_frames(own_0, 1), next_frames(own_0, 2)
     sent = jnp.concatenate(
         [
+            earliest_0.reshape(frames * rows, *block),
             earlier_0.reshape(frames * rows, *block),
             own_0.reshape(frames * rows, *block),
             cotangent[:, :2].reshape(frames * 2, *block),
@@ -267,30 +277,20 @@
         axis=0,
     )
     below = from_below(sent)
-    below_0, low = below[: 2 * frames * rows], below[2 * frames * rows :]
     wide = 2 * rows - 2
-    own_1, pre_0 = call(
-        first_forward,
-        (shape_of(wide, frames, *block), shape_of(cells, channels, dtype=F32)),
+    grad_shape = shape_of(rows, frames, *block)
+    next_1, pre_0, grad_1 = call(
+        forward,
+        (shape_of(wide, 2 * frames, *block), shape_of(cells, channels, dtype=F32), grad_shape),
         own_0,
         earlier_0,
-        below_0,
+        earliest_0,
+        below,
+        cotangent,
         kernels[0],
-        norm_gains,
-        scratch=patch_scratch(wide * frames * columns),
-    )
-    earlier_1 = next_frames(own_1)
-    grad_shape = shape_of(rows, frames, *block)
-    grad_1 = call(
-        second_forward,
-        grad_shape,
-        own_1,
-        earlier_1,
-        cotangent,
-        low,
         kernels[1],
         norm_gains,
-        scratch=patch_scratch(cells),
+        scratch=patch_scratch(wide * 2 * frames * columns) + patch_scratch(cells),
     )
 
     def with_neighbours(grad):
@@ -302,7 +302,7 @@
     part = shape_of(tiles // 2, TAPS, share, channels)
     later_1, above_1 = with_neighbours(grad_1)
     keep_1, send_1 = call(
-        second_kernel_gradient, (part, part), own_1, earlier_1, grad_1, scratch=patch_scratch(cells)
+        second_kernel_gradient, (part, part), next_1, grad_1, scratch=patch_scratch(cells)
     )
     came_1 = partner(send_1)
     grad_0 = call(
@@ -321,7 +321,7 @@
         (part, part),
         own_0,
         earlier_0,
-        below_0,
+        below,
         grad_0,
         scratch=patch_scratch(cells),
     )
@@ -334,31 +334,31 @@
         paired, "tile", split_axis=0, concat_axis=0, tiled=True, axis_index_groups=by_core
     )
     later_0, above_0 = with_neighbours(grad_0)
-    input_grad = call(
+    input_grad, token = call(
         first_backward,
-        shape_of(frames, rows, *block),
+        (shape_of(frames, rows, *block), shape_of(8, channels, dtype=F32)),
         grad_0,
         later_0,
         above_0,
         kernels[0],
         scratch=patch_scratch(cells),
     )
-    used = 2 * TAPS * share
-    padded = -(-used // 128) * 128
+    padded = -(-2 * TAPS // 32) * 32 * share
     by_frame = call(
         sum_tiles,
         shape_of(groups, channels // groups, padded),
         arrived,
+        token,
         scratch=(pltpu.VMEM((padded, channels), F32),),
     )
     spread = lax.all_to_all(by_frame, "frame", split_axis=0, concat_axis=0, tiled=True)
     scale = 1.0 / math.sqrt(cells * tiles * groups)
     summed = call(
         lambda *refs: sum_frames(scale, *refs),
-        shape_of(used, channels // groups, dtype=F32),
+        shape_of(share, channels // groups, 2 * TAPS, dtype=F32),
         spread,
     )
-    return (input_grad, summed.reshape(2 * TAPS, share, channels // groups))
+    return (input_grad, jnp.transpose(summed, (2, 0, 1)))
 
 
 def solution(mesh):

time: 109 us -> 103 us (0.945)
  blocking collectives: 0 us -> 25 us
  waiting for transfers between devices: 49 us -> 32.5 us
  starting transfers between devices: 46.5 us -> 31 us
  Pallas kernels: 8.07 us -> 9.73 us
    all_to_all x0 -> x1, blocking collectives: none -> 25 us  [local(): lax.all_to_all(by_frame, 'frame', split_axis=0, concat_axis=0, tiled=True)]
    all_to_all x1 -> x0, starting transfers between devices: 20.5 us -> none  [local(): lax.all_to_all(by_frame, 'frame', split_axis=0, concat_axis=0, tiled=True)]
    all_to_all x1, waiting for transfers between devices: 15.7 us -> 0.94 us  [local(): lax.all_to_all(paired, 'tile', split_axis=0, concat_axis=0, tiled=True, a...]
    ppermute x2, waiting for transfers between devices: 8.81 us -> 18.4 us  [from_above(): lax.ppermute(value, 'tile', [(i, (i + 1) % tiles) for i in range(tiles)])]
    ppermute x2, waiting for transfers between devices: 8.32 us -> 1.12 us  [next_frames(): lax.ppermute(value, 'frame', [(i, i + steps) for i in range(groups - step...]
    ppermute x2, waiting for transfers between devices: 13.2 us -> 8.35 us  [earlier_frames(): return lax.ppermute(value, 'frame', [(i + 1, i) for i in range(groups - 1)])]
    ppermute x1, starting transfers between devices: 2.37 us -> 5.62 us  [from_below(): lax.ppermute(value, 'tile', [((i + 1) % tiles, i) for i in range(tiles)])]
    ppermute x2, starting transfers between devices: 6.8 us -> 9.43 us  [next_frames(): lax.ppermute(value, 'frame', [(i, i + steps) for i in range(groups - step...]
  transfers between devices with their start and end apart: 11 -> 10, of which waited for: 9 -> 8; matrix products, arithmetic and copies ran while one was open for 2% -> 2% of each run, Pallas kernels for 3% -> 4%
where the time goes in v3:
time: 103 us; the launch traced here: 102 us
  waiting for transfers between devices  32.5 us (32%)
  starting transfers between devices  31 us (30%)
  blocking collectives  25 us (24%)
  Pallas kernels  9.73 us (9%)
  local copies, waits for them, and re-layouts  2.38 us (2%)
    all_to_all x1, blocking collectives, local(): lax.all_to_all(by_frame, 'frame', split_axis=0, concat_axis=0, tiled=True)  25 us
    ppermute x2, waiting for transfers between devices, from_above(): lax.ppermute(value, 'tile', [(i, (i + 1) % tiles) for i in range(tiles)])  18.4 us
    pallas_call x8, Pallas kernels, call(): pl.pallas_call(kernel, out_shape=out_shape, scratch_shapes=list(scratch),...  9.73 us
    ppermute x2, starting transfers between devices, next_frames(): lax.ppermute(value, 'frame', [(i, i + steps) for i in range(groups - step...  9.43 us
    ppermute x2, waiting for transfers between devices, earlier_frames(): return lax.ppermute(value, 'frame', [(i + 1, i) for i in range(groups - 1)])  8.35 us
    ppermute x1, starting transfers between devices, from_below(): lax.ppermute(value, 'tile', [((i + 1) % tiles, i) for i in range(tiles)])  5.62 us
    all_to_all x1, starting transfers between devices, local(): lax.all_to_all(paired, 'tile', split_axis=0, concat_axis=0, tiled=True, a...  4.19 us
    ppermute x2, starting transfers between devices, earlier_frames(): return lax.ppermute(value, 'frame', [(i + 1, i) for i in range(groups - 1)])  4.08 us
  transfers between devices with their start and end apart: 10, of which 8 were waited for; matrix products, arithmetic and copies ran while one was open for 2% of the time, Pallas kernels for 4%

profile of v3, /device:TPU:2, one launch (start us, length us, event | category | flops | bytes accessed | tf_op | source)
XLA Modules:
  0.0 102.5 jit_solution(13612355904005522916)
XLA Ops:
  0.6 0.9 multiply_convert_fusion.own_ref
  1.6 4.0 %collective-permute-start.1 = (bf16[2,4,32,128]{3,2,1,0:T(8,128)(2,1)S(1)}, bf16[2,4,32,128]{3,2,1,0:T(8,128)(2,1)S(1)}, u32[]{:S(2)}, u32[]{:S(2)}) collective-permute-start(bf16[2,4,32,128]{3,2,1,0:T(8,128)(2,1)S(1)} %multiply_convert_fusion.own_ref), channel_id=1, source_target_pairs={{0,64},{32,96},{64,128},{96,160},{128,192},{160,224},{192,256},{22... | collective-permute-start | bytes 196616 | tf_op jit(solution)/shard_map/ppermute | solution.py:254
  5.6 5.4 %collective-permute-start = (bf16[2,4,32,128]{3,2,1,0:T(8,128)(2,1)S(1)}, bf16[2,4,32,128]{3,2,1,0:T(8,128)(2,1)S(1)}, u32[]{:S(2)}, u32[]{:S(2)}) collective-permute-start(bf16[2,4,32,128]{3,2,1,0:T(8,128)(2,1)S(1)} %multiply_convert_fusion.own_ref), channel_id=1, source_target_pairs={{0,32},{32,64},{64,96},{96,128},{128,160},{160,192},{192,224},{224... | collective-permute-start | bytes 196616 | tf_op jit(solution)/shard_map/ppermute | solution.py:254
  11.0 0.8 slice.23
  11.8 0.0 collective-permute-done.1.earliest_ref
  11.8 1.1 %collective-permute-done.earlier_ref = bf16[2,4,32,128]{3,2,1,0:T(8,128)(2,1)S(1)} collective-permute-done((bf16[2,4,32,128]{3,2,1,0:T(8,128)(2,1)S(1)}, bf16[2,4,32,128]{3,2,1,0:T(8,128)(2,1)S(1)}, u32[]{:S(2)}, u32[]{:S(2)}) %collective-permute-start) | collective-permute-done | bytes 65568 | tf_op jit(solution)/shard_map/ppermute | solution.py:254
  12.9 0.0 copy-start
  13.0 0.0 copy-start.1
  13.0 5.6 %collective-permute-start.2 = (bf16[28,32,128]{2,1,0:T(8,128)(2,1)S(1)}, bf16[28,32,128]{2,1,0:T(8,128)(2,1)S(1)}, u32[]{:S(2)}, u32[]{:S(2)}) collective-permute-start(bf16[28,32,128]{2,1,0:T(8,128)(2,1)S(1)} %pad_maximum_fusion), channel_id=1, source_target_pairs={{1,0},{2,1},{3,2},{4,3},{5,4},{6,5},{7,6},{8,7},{9,8},{10,9},{11,1... | collective-permute-start | bytes 688136 | tf_op jit(solution)/shard_map/ppermute | solution.py:260
  18.6 1.6 %slice_bitcast_fusion = (bf16[27,128,128]{2,1,0:T(8,128)(2,1)S(1)}, bf16[27,128,128]{2,1,0:T(8,128)(2,1)S(1)}) fusion(bf16[2,27,128,128]{3,2,1,0:T(8,128)(2,1)} %param.7), kind=kLoop, calls=%fused_computation | loop fusion | bytes 3538944 | tf_op jit(solution)/shard_map/squeeze | solution.py:291
  20.2 1.9 %collective-permute-done.2.below_ref = bf16[28,32,128]{2,1,0:T(8,128)(2,1)S(1)} collective-permute-done((bf16[28,32,128]{2,1,0:T(8,128)(2,1)S(1)}, bf16[28,32,128]{2,1,0:T(8,128)(2,1)S(1)}, u32[]{:S(2)}, u32[]{:S(2)}) %collective-permute-start.2) | collective-permute-done | bytes 229408 | tf_op jit(solution)/shard_map/ppermute | solution.py:260
  22.1 0.0 copy-done
  22.1 0.0 copy-done.1
  22.1 3.6 %shard_map.68 = (bf16[6,4,32,128]{3,2,1,0:T(8,128)(2,1)S(1)}, f32[256,128]{1,0:T(8,128)S(1)}, bf16[4,2,32,128]{3,2,1,0:T(8,128)(2,1)S(1)}) custom-call(bf16[2,4,32,128]{3,2,1,0:T(8,128)(2,1)S(1)} %multiply_convert_fusion.own_ref, bf16[2,4,32,128]{3,2,1,0:T(8,128)(2,1)S(1)} %collective-permute-done.earlier_ref, ...), custom_call_target="tpu_custom_call" | custom-call | tf_op jit(solution)/shard_map/pallas_call | solution.py:17
  25.7 1.9 %collective-permute-start.3 = (bf16[4,2,32,128]{3,2,1,0:T(8,128)(2,1)S(1)}, bf16[4,2,32,128]{3,2,1,0:T(8,128)(2,1)S(1)}, u32[]{:S(2)}, u32[]{:S(2)}) collective-permute-start(bf16[4,2,32,128]{3,2,1,0:T(8,128)(2,1)S(1)} %get-tuple-element.11.own_ref.grad_ref), channel_id=1, source_target_pairs={{32,0},{64,32},{96,64},{128,96},{160,128},{192,160},{224,192},{256... | collective-permute-start | bytes 196616 | tf_op jit(solution)/shard_map/ppermute | solution.py:257
  27.7 4.3 %collective-permute-done.3.later_ref = bf16[4,2,32,128]{3,2,1,0:T(8,128)(2,1)S(1)} collective-permute-done((bf16[4,2,32,128]{3,2,1,0:T(8,128)(2,1)S(1)}, bf16[4,2,32,128]{3,2,1,0:T(8,128)(2,1)S(1)}, u32[]{:S(2)}, u32[]{:S(2)}) %collective-permute-start.3) | collective-permute-done | bytes 65568 | tf_op jit(solution)/shard_map/ppermute | solution.py:257
  32.0 1.9 %collective-permute-start.4 = (bf16[2,4,32,128]{3,2,1,0:T(8,128)(2,1)S(1)}, bf16[2,4,32,128]{3,2,1,0:T(8,128)(2,1)S(1)}, u32[]{:S(2)}, u32[]{:S(2)}) collective-permute-start(bf16[2,4,32,128]{3,2,1,0:T(8,128)(2,1)S(1)} %pad_maximum_fusion.1), channel_id=1, source_target_pairs={{0,1},{1,2},{2,3},{3,4},{4,5},{5,6},{6,7},{7,8},{8,9},{9,10},{10,1... | collective-permute-start | bytes 196616 | tf_op jit(solution)/shard_map/ppermute | solution.py:263
  33.9 0.8 shard_map.72
  34.7 1.9 %collective-permute-start.8 = (bf16[16,27,4,128]{3,2,1,0:T(4,128)(2,1)S(1)}, bf16[16,27,4,128]{3,2,1,0:T(4,128)(2,1)S(1)}, u32[]{:S(2)}, u32[]{:S(2)}) collective-permute-start(bf16[16,27,4,128]{3,2,1,0:T(4,128)(2,1)S(1)} %get-tuple-element.18), channel_id=1, source_target_pairs={{0,1},{1,0},{2,3},{3,2},{4,5},{5,4},{6,7},{7,6},{8,9},{9,8},{10,11... | collective-permute-start | bytes 1327112 | tf_op jit(solution)/shard_map/ppermute | solution.py:266
  36.6 3.0 %collective-permute-done.4.above_ref = bf16[2,4,32,128]{3,2,1,0:T(8,128)(2,1)S(1)} collective-permute-done((bf16[2,4,32,128]{3,2,1,0:T(8,128)(2,1)S(1)}, bf16[2,4,32,128]{3,2,1,0:T(8,128)(2,1)S(1)}, u32[]{:S(2)}, u32[]{:S(2)}) %collective-permute-start.4) | collective-permute-done | bytes 65568 | tf_op jit(solution)/shard_map/ppermute | solution.py:263
  39.7 0.8 shard_map.69.own_ref.grad_ref
  40.5 0.8 shard_map.71
  41.3 1.9 %collective-permute-start.7 = (bf16[16,27,4,128]{3,2,1,0:T(4,128)(2,1)S(1)}, bf16[16,27,4,128]{3,2,1,0:T(4,128)(2,1)S(1)}, u32[]{:S(2)}, u32[]{:S(2)}) collective-permute-start(bf16[16,27,4,128]{3,2,1,0:T(4,128)(2,1)S(1)} %get-tuple-element.15), channel_id=1, source_target_pairs={{0,1},{1,0},{2,3},{3,2},{4,5},{5,4},{6,7},{7,6},{8,9},{9,8},{10,11... | collective-permute-start | bytes 1327112 | tf_op jit(solution)/shard_map/ppermute | solution.py:266
  43.2 0.0 collective-permute-done.8.came_second
  43.2 1.7 %collective-permute-done.7.came_first = bf16[16,27,4,128]{3,2,1,0:T(4,128)(2,1)S(1)} collective-permute-done((bf16[16,27,4,128]{3,2,1,0:T(4,128)(2,1)S(1)}, bf16[16,27,4,128]{3,2,1,0:T(4,128)(2,1)S(1)}, u32[]{:S(2)}, u32[]{:S(2)}) %collective-permute-start.7) | collective-permute-done | bytes 442400 | tf_op jit(solution)/shard_map/ppermute | solution.py:266
  45.0 1.4 %shard_map.73 = bf16[16,54,4,128]{3,2,1,0:T(4,128)(2,1)} custom-call(bf16[16,27,4,128]{3,2,1,0:T(4,128)(2,1)S(1)} %get-tuple-element.14.keep_first, bf16[16,27,4,128]{3,2,1,0:T(4,128)(2,1)S(1)} %collective-permute-done.7.came_first, bf16[16,27,4,128]{3,2,1,0:T(4,128)(2,1)S(1)} %get-tuple-element.17.keep_second, ...), custom_call_target="tpu_custom_call" | custom-call | tf_op jit(solution)/shard_map/pallas_call | solution.py:17
  46.3 4.2 %all-to-all-start = ((bf16[16,54,4,128]{3,2,1,0:T(4,128)(2,1)}), bf16[16,54,4,128]{3,2,1,0:T(4,128)(2,1)S(1)}, u32[]{:S(2)}, u32[]{:S(2)}) async-start(bf16[16,54,4,128]{3,2,1,0:T(4,128)(2,1)} %shard_map.73), calls=%async_computation | async-start | bytes 1769472 | tf_op jit(solution)/shard_map/all_to_all | solution.py:333
  50.5 2.2 %collective-permute-start.5 = (bf16[4,2,32,128]{3,2,1,0:T(8,128)(2,1)S(1)}, bf16[4,2,32,128]{3,2,1,0:T(8,128)(2,1)S(1)}, u32[]{:S(2)}, u32[]{:S(2)}) collective-permute-start(bf16[4,2,32,128]{3,2,1,0:T(8,128)(2,1)S(1)} %shard_map.69.own_ref.grad_ref), channel_id=1, source_target_pairs={{32,0},{64,32},{96,64},{128,96},{160,128},{192,160},{224,192},{256... | collective-permute-start | bytes 196616 | tf_op jit(solution)/shard_map/ppermute | solution.py:257
  52.7 4.1 %collective-permute-done.5.later_ref = bf16[4,2,32,128]{3,2,1,0:T(8,128)(2,1)S(1)} collective-permute-done((bf16[4,2,32,128]{3,2,1,0:T(8,128)(2,1)S(1)}, bf16[4,2,32,128]{3,2,1,0:T(8,128)(2,1)S(1)}, u32[]{:S(2)}, u32[]{:S(2)}) %collective-permute-start.5) | collective-permute-done | bytes 65568 | tf_op jit(solution)/shard_map/ppermute | solution.py:257
  56.8 1.9 %collective-permute-start.6 = (bf16[2,4,32,128]{3,2,1,0:T(8,128)(2,1)S(1)}, bf16[2,4,32,128]{3,2,1,0:T(8,128)(2,1)S(1)}, u32[]{:S(2)}, u32[]{:S(2)}) collective-permute-start(bf16[2,4,32,128]{3,2,1,0:T(8,128)(2,1)S(1)} %pad_maximum_fusion.2), channel_id=1, source_target_pairs={{0,1},{1,2},{2,3},{3,4},{4,5},{5,6},{6,7},{7,8},{8,9},{9,10},{10,1... | collective-permute-start | bytes 196616 | tf_op jit(solution)/shard_map/ppermute | solution.py:263
  58.7 15.4 %collective-permute-done.6.above_ref = bf16[2,4,32,128]{3,2,1,0:T(8,128)(2,1)S(1)} collective-permute-done((bf16[2,4,32,128]{3,2,1,0:T(8,128)(2,1)S(1)}, bf16[2,4,32,128]{3,2,1,0:T(8,128)(2,1)S(1)}, u32[]{:S(2)}, u32[]{:S(2)}) %collective-permute-start.6) | collective-permute-done | bytes 65568 | tf_op jit(solution)/shard_map/ppermute | solution.py:263
  74.1 1.3 %shard_map.70 = (bf16[2,4,32,128]{3,2,1,0:T(8,128)(2,1)}, f32[8,128]{1,0:T(8,128)S(1)}) custom-call(bf16[4,2,32,128]{3,2,1,0:T(8,128)(2,1)S(1)} %shard_map.69.own_ref.grad_ref, bf16[4,2,32,128]{3,2,1,0:T(8,128)(2,1)S(1)} %collective-permute-done.5.later_ref, bf16[2,4,32,128]{3,2,1,0:T(8,128)(2,1)S(1)} %collective-permute-done.6.above_ref, ...), custom_call_target="tpu_custom_call" | custom-call | tf_op jit(solution)/shard_map/pallas_call | solution.py:17
  75.4 0.9 all-to-all-done.in_ref
  76.4 0.4 shard_map.74
  76.7 25.0 %all_to_all.10.refs_0_ = bf16[16,8,256]{2,1,0:T(8,128)(2,1)S(1)} all-to-all(bf16[16,8,256]{2,1,0:T(8,128)(2,1)S(1)} %shard_map.74), channel_id=1, replica_groups=mesh['frame'=16,'tile'=32] {'frame'}, dimensions={0} | all-to-all | bytes 131072 | tf_op jit(solution)/shard_map/all_to_all | solution.py:354
  101.8 0.7 shard_map.75
  (7 shorter events, 0.1 us)
Async XLA Ops:
  1.6 10.2 %collective-permute-start.1 = (bf16[2,4,32,128]{3,2,1,0:T(8,128)(2,1)S(1)}, bf16[2,4,32,128]{3,2,1,0:T(8,128)(2,1)S(1)}, u32[]{:S(2)}, u32[]{:S(2)}) collective-permute-start(bf16[2,4,32,128]{3,2,1,0:T(8,128)(2,1)S(1)} %multiply_convert_fusion.own_ref), channel_id=1, source_target_pairs={{0,64},{32,96},{64,128},{96,160},{128,192},{160,224},{192,256},{22... | collective-permute-start | bytes 196616 | tf_op jit(solution)/shard_map/ppermute | solution.py:254
  5.6 7.3 %collective-permute-start = (bf16[2,4,32,128]{3,2,1,0:T(8,128)(2,1)S(1)}, bf16[2,4,32,128]{3,2,1,0:T(8,128)(2,1)S(1)}, u32[]{:S(2)}, u32[]{:S(2)}) collective-permute-start(bf16[2,4,32,128]{3,2,1,0:T(8,128)(2,1)S(1)} %multiply_convert_fusion.own_ref), channel_id=1, source_target_pairs={{0,32},{32,64},{64,96},{96,128},{128,160},{160,192},{192,224},{224... | collective-permute-start | bytes 196616 | tf_op jit(solution)/shard_map/ppermute | solution.py:254
  12.9 9.2 %copy-start = (bf16[2,4,32,128]{3,2,1,0:T(8,128)(2,1)S(1)}, bf16[2,4,32,128]{3,2,1,0:T(8,128)(2,1)}, u32[]{:S(2)}) copy-start(bf16[2,4,32,128]{3,2,1,0:T(8,128)(2,1)} %top_ref.1) | copy-start | bytes 196612
  13.0 9.2 %copy-start.1 = (f32[2,128]{1,0:T(2,128)S(1)}, f32[2,128]{1,0:T(2,128)}, u32[]{:S(2)}) copy-start(f32[2,128]{1,0:T(2,128)} %gain_ref.3) | copy-start | bytes 3076
  13.0 9.1 %collective-permute-start.2 = (bf16[28,32,128]{2,1,0:T(8,128)(2,1)S(1)}, bf16[28,32,128]{2,1,0:T(8,128)(2,1)S(1)}, u32[]{:S(2)}, u32[]{:S(2)}) collective-permute-start(bf16[28,32,128]{2,1,0:T(8,128)(2,1)S(1)} %pad_maximum_fusion), channel_id=1, source_target_pairs={{1,0},{2,1},{3,2},{4,3},{5,4},{6,5},{7,6},{8,7},{9,8},{10,9},{11,1... | collective-permute-start | bytes 688136 | tf_op jit(solution)/shard_map/ppermute | solution.py:260
  25.7 6.2 %collective-permute-start.3 = (bf16[4,2,32,128]{3,2,1,0:T(8,128)(2,1)S(1)}, bf16[4,2,32,128]{3,2,1,0:T(8,128)(2,1)S(1)}, u32[]{:S(2)}, u32[]{:S(2)}) collective-permute-start(bf16[4,2,32,128]{3,2,1,0:T(8,128)(2,1)S(1)} %get-tuple-element.11.own_ref.grad_ref), channel_id=1, source_target_pairs={{32,0},{64,32},{96,64},{128,96},{160,128},{192,160},{224,192},{256... | collective-permute-start | bytes 196616 | tf_op jit(solution)/shard_map/ppermute | solution.py:257
  32.0 7.7 %collective-permute-start.4 = (bf16[2,4,32,128]{3,2,1,0:T(8,128)(2,1)S(1)}, bf16[2,4,32,128]{3,2,1,0:T(8,128)(2,1)S(1)}, u32[]{:S(2)}, u32[]{:S(2)}) collective-permute-start(bf16[2,4,32,128]{3,2,1,0:T(8,128)(2,1)S(1)} %pad_maximum_fusion.1), channel_id=1, source_target_pairs={{0,1},{1,2},{2,3},{3,4},{4,5},{5,6},{6,7},{7,8},{8,9},{9,10},{10,1... | collective-permute-start | bytes 196616 | tf_op jit(solution)/shard_map/ppermute | solution.py:263
  34.7 8.5 %collective-permute-start.8 = (bf16[16,27,4,128]{3,2,1,0:T(4,128)(2,1)S(1)}, bf16[16,27,4,128]{3,2,1,0:T(4,128)(2,1)S(1)}, u32[]{:S(2)}, u32[]{:S(2)}) collective-permute-start(bf16[16,27,4,128]{3,2,1,0:T(4,128)(2,1)S(1)} %get-tuple-element.18), channel_id=1, source_target_pairs={{0,1},{1,0},{2,3},{3,2},{4,5},{5,4},{6,7},{7,6},{8,9},{9,8},{10,11... | collective-permute-start | bytes 1327112 | tf_op jit(solution)/shard_map/ppermute | solution.py:266
  41.3 3.7 %collective-permute-start.7 = (bf16[16,27,4,128]{3,2,1,0:T(4,128)(2,1)S(1)}, bf16[16,27,4,128]{3,2,1,0:T(4,128)(2,1)S(1)}, u32[]{:S(2)}, u32[]{:S(2)}) collective-permute-start(bf16[16,27,4,128]{3,2,1,0:T(4,128)(2,1)S(1)} %get-tuple-element.15), channel_id=1, source_target_pairs={{0,1},{1,0},{2,3},{3,2},{4,5},{5,4},{6,7},{7,6},{8,9},{9,8},{10,11... | collective-permute-start | bytes 1327112 | tf_op jit(solution)/shard_map/ppermute | solution.py:266
  46.3 30.0 %all-to-all-start = ((bf16[16,54,4,128]{3,2,1,0:T(4,128)(2,1)}), bf16[16,54,4,128]{3,2,1,0:T(4,128)(2,1)S(1)}, u32[]{:S(2)}, u32[]{:S(2)}) async-start(bf16[16,54,4,128]{3,2,1,0:T(4,128)(2,1)} %shard_map.73), calls=%async_computation | async-start | bytes 1769472 | tf_op jit(solution)/shard_map/all_to_all | solution.py:333
  50.5 6.2 %collective-permute-start.5 = (bf16[4,2,32,128]{3,2,1,0:T(8,128)(2,1)S(1)}, bf16[4,2,32,128]{3,2,1,0:T(8,128)(2,1)S(1)}, u32[]{:S(2)}, u32[]{:S(2)}) collective-permute-start(bf16[4,2,32,128]{3,2,1,0:T(8,128)(2,1)S(1)} %shard_map.69.own_ref.grad_ref), channel_id=1, source_target_pairs={{32,0},{64,32},{96,64},{128,96},{160,128},{192,160},{224,192},{256... | collective-permute-start | bytes 196616 | tf_op jit(solution)/shard_map/ppermute | solution.py:257
  56.8 17.3 %collective-permute-start.6 = (bf16[2,4,32,128]{3,2,1,0:T(8,128)(2,1)S(1)}, bf16[2,4,32,128]{3,2,1,0:T(8,128)(2,1)S(1)}, u32[]{:S(2)}, u32[]{:S(2)}) collective-permute-start(bf16[2,4,32,128]{3,2,1,0:T(8,128)(2,1)S(1)} %pad_maximum_fusion.2), channel_id=1, source_target_pairs={{0,1},{1,2},{2,3},{3,4},{4,5},{5,6},{6,7},{7,8},{8,9},{9,10},{10,1... | collective-permute-start | bytes 196616 | tf_op jit(solution)/shard_map/ppermute | solution.py:263

commit v4 on v3

--- a/solution.py
+++ b/solution.py
@@ -6,6 +6,7 @@
 from jax.experimental import pallas as pl
 from jax.experimental.pallas import tpu as pltpu
 from jax.sharding import PartitionSpec as P
+
 
 EPS = 1e-06
 TAPS = 27
@@ -58,6 +59,15 @@
     return [[ref[row, frame] for frame in range(ref.shape[1])] for row in range(ref.shape[0])]
 
 
+def product(patches, kernel_ref, chunk=256):
+    weights = kernel_ref[...].reshape(-1, kernel_ref.shape[-1])
+    pieces = [
+        jnp.dot(patches[start : start + chunk], weights, preferred_element_type=F32)
+        for start in range(0, patches.shape[0], chunk)
+    ]
+    return pieces
+
+
 def silu_parts(pre_norm, gain):
     inverse = lax.rsqrt(jnp.mean(pre_norm * pre_norm, axis=-1, keepdims=True) + EPS)
     normed = pre_norm * inverse * gain
@@ -96,29 +106,25 @@
     own_ref, earlier_ref, earliest_ref, below_ref, top_ref, first_kernel_ref, second_kernel_ref,
     gain_ref, next_ref, pre_ref, grad_ref, wide_patches, patches,
 ):
-    frames, rows, columns, channels = own_ref.shape
+    frames, rows, columns, _ = own_ref.shape
     last = at_last_tile()
     window = window_of(first_rows((earliest_ref, earlier_ref, own_ref), below_ref, 2 * rows))
     wide, deep = 2 * rows - 2, 2 * frames
     fill(wide_patches, window, deep, wide, 1, {(rows - 2, 2): last, (rows - 1, 0): last})
-    pre_norm = jnp.dot(
-        wide_patches[...],
-        first_kernel_ref[...].reshape(TAPS * channels, channels),
-        preferred_element_type=F32,
-    )
-    _, normed, sigma = silu_parts(pre_norm, gain_ref[0:1])
-    next_ref[...] = (normed * sigma).astype(BF16).reshape(next_ref.shape)
-    own_cells = frames * columns
-    for row in range(rows):
-        start = row * deep * columns + own_cells
-        pre_ref[row * own_cells : (row + 1) * own_cells] = pre_norm[start : start + own_cells]
+    own_cells, blocks = frames * columns, 8
+    for number, pre_norm in enumerate(product(wide_patches, first_kernel_ref, blocks * columns)):
+        _, normed, sigma = silu_parts(pre_norm, gain_ref[0:1])
+        value = (normed * sigma).astype(BF16)
+        for block in range(blocks):
+            row, frame = divmod(number * blocks + block, deep)
+            cells = slice(block * columns, (block + 1) * columns)
+            next_ref[row, frame] = value[cells]
+            if row < rows and frame >= frames:
+                start = row * own_cells + (frame - frames) * columns
+                pre_ref[start : start + columns] = pre_norm[cells]
     window = window_of(block_rows(next_ref))
     fill(patches, window, frames, rows, 1, {(rows - 3, 2): last, (rows - 2, 0): last})
-    pre_norm = jnp.dot(
-        patches[...],
-        second_kernel_ref[...].reshape(TAPS * channels, channels),
-        preferred_element_type=F32,
-    )
+    (pre_norm,) = product(patches, second_kernel_ref)
     spread = []
     for row in range(rows):
         for frame in range(frames):
@@ -151,9 +157,10 @@
 
 
 def second_backward(
-    own_ref, later_ref, above_ref, kernel_ref, gain_ref, pre_ref, grad_ref, patches
+    own_ref, later_ref, above_ref, kernel_ref, gain_ref, pre_ref, token_ref, grad_ref, patches
 ):
-    rows, frames, columns, channels = own_ref.shape
+    del token_ref
+    rows, frames, _, _ = own_ref.shape
     last = at_last_tile()
     window = window_of(backward_rows(own_ref, later_ref, above_ref, frames))
     fill(patches, window, frames, rows, -1, {(rows - 2, 2): last, (rows - 1, 0): last})
@@ -162,7 +169,7 @@
 
 
 def first_backward(own_ref, later_ref, above_ref, kernel_ref, out_ref, token_ref, patches):
-    rows, frames, columns, channels = own_ref.shape
+    rows, frames, columns, _ = own_ref.shape
     first, last = lax.axis_index("tile") == 0, at_last_tile()
     window = window_of(backward_rows(own_ref, later_ref, above_ref, frames))
     fill(patches, window, frames, rows, -1, {(0, 0): first, (rows - 1, 2): last})
@@ -190,39 +197,48 @@
         send_ref[:, tap] = jnp.where(odd, even_part, odd_part).astype(BF16)
 
 
-def second_kernel_gradient(next_ref, grad_ref, keep_ref, send_ref, patches):
+def second_kernel_gradient(next_ref, grad_ref, keep_ref, send_ref, token_ref, patches):
     rows, frames, _, _ = grad_ref.shape
     last = at_last_tile()
     window = window_of(block_rows(next_ref))
     fill(patches, window, frames, rows, 1, {(rows - 3, 2): last, (rows - 2, 0): last})
     split_gradient(patches, grad_ref, keep_ref, send_ref)
+    token_ref[...] = jnp.zeros_like(token_ref)
 
 
 def first_kernel_gradient(own_ref, earlier_ref, below_ref, grad_ref, keep_ref, send_ref, patches):
-    frames, rows, columns, channels = own_ref.shape
+    frames, rows, _, _ = own_ref.shape
     last = at_last_tile()
     window = window_of(first_rows((earlier_ref, own_ref), below_ref, rows + 2))
     fill(patches, window, frames, rows, 1, {(rows - 2, 2): last, (rows - 1, 0): last})
     split_gradient(patches, grad_ref, keep_ref, send_ref)
 
 
-def add_pairs(keep_first, came_first, keep_second, came_second, out_ref):
-    taps = keep_first.shape[1]
-    out_ref[:, :taps] = (keep_first[...].astype(F32) + came_first[...].astype(F32)).astype(BF16)
-    out_ref[:, taps:] = (keep_second[...].astype(F32) + came_second[...].astype(F32)).astype(BF16)
-
-
-def sum_tiles(in_ref, token_ref, out_ref, rows_ref):
+def pack_rows(own_ref, later_ref, token_ref, out_ref):
     del token_ref
-    chips, taps, share, channels = in_ref.shape
+    frames, first = own_ref.shape[1], own_ref.shape[0] - out_ref.shape[0]
+    out_ref[:, :frames] = own_ref[first:]
+    out_ref[:, frames:] = later_ref[first:]
+
+
+def add_pair(keep_ref, came_ref, out_ref, token_ref):
+    out_ref[...] = (keep_ref[...].astype(F32) + came_ref[...].astype(F32)).astype(BF16)
+    token_ref[...] = jnp.zeros_like(token_ref)
+
+
+def sum_tiles(first_ref, second_ref, token_ref, out_ref, rows_ref):
+    del token_ref
+    chips, taps, share, _ = first_ref.shape
     groups, width, _ = out_ref.shape
-    total = in_ref[0].astype(F32)
-    for chip in range(1, chips):
-        total = total + in_ref[chip].astype(F32)
     rows_ref[...] = jnp.zeros_like(rows_ref)
     stride = rows_ref.shape[0] // share
-    for row in range(share):
-        rows_ref[row * stride : row * stride + taps] = total[:, row]
+    for layer, in_ref in enumerate((first_ref, second_ref)):
+        total = in_ref[0].astype(F32)
+        for chip in range(1, chips):
+            total = total + in_ref[chip].astype(F32)
+        for row in range(share):
+            start = row * stride + layer * taps
+            rows_ref[start : start + taps] = total[:, row]
     out_ref[...] = rows_ref[...].T.reshape(groups, width, -1).astype(BF16)
 
 
@@ -293,18 +309,31 @@
         scratch=patch_scratch(wide * 2 * frames * columns) + patch_scratch(cells),
     )
 
-    def with_neighbours(grad):
-        later = earlier_frames(grad)
-        above = from_above(jnp.concatenate([grad[rows - 2 :], later[rows - 2 :]], axis=1))
-        return later, above
-
     share = channels // tiles
     part = shape_of(tiles // 2, TAPS, share, channels)
-    later_1, above_1 = with_neighbours(grad_1)
-    keep_1, send_1 = call(
-        second_kernel_gradient, (part, part), next_1, grad_1, scratch=patch_scratch(cells)
-    )
-    came_1 = partner(send_1)
+    mark = shape_of(8, channels, dtype=F32)
+
+    def with_neighbours(later, grad, token):
+        edge = shape_of(2, 2 * frames, *block)
+        packed = call(pack_rows, edge, grad, later, token)
+        return from_above(packed)
+
+    by_core = [list(range(core, tiles, 2)) for core in range(2)]
+
+    def sent_and_paired(keep, send):
+        came = partner(send)
+        paired, token = call(add_pair, (part, mark), keep, came)
+        arrived = lax.all_to_all(
+            paired, "tile", split_axis=0, concat_axis=0, tiled=True, axis_index_groups=by_core
+        )
+        return arrived, token
+
+    later_1 = earlier_frames(grad_1)
+    keep_1, send_1, token = call(
+        second_kernel_gradient, (part, part, mark), next_1, grad_1, scratch=patch_scratch(cells)
+    )
+    above_1 = with_neighbours(later_1, grad_1, token)
+    arrived_1, token = sent_and_paired(keep_1, send_1)
     grad_0 = call(
         second_backward,
         grad_shape,
@@ -314,6 +343,7 @@
         kernels[1],
         norm_gains,
         pre_0,
+        token,
         scratch=patch_scratch(cells),
     )
     keep_0, send_0 = call(
@@ -325,18 +355,12 @@
         grad_0,
         scratch=patch_scratch(cells),
     )
-    came_0 = partner(send_0)
-    paired = call(
-        add_pairs, shape_of(tiles // 2, 2 * TAPS, share, channels), keep_0, came_0, keep_1, came_1
-    )
-    by_core = [list(range(core, tiles, 2)) for core in range(2)]
-    arrived = lax.all_to_all(
-        paired, "tile", split_axis=0, concat_axis=0, tiled=True, axis_index_groups=by_core
-    )
-    later_0, above_0 = with_neighbours(grad_0)
+    arrived_0, token = sent_and_paired(keep_0, send_0)
+    later_0 = earlier_frames(grad_0)
+    above_0 = with_neighbours(later_0, grad_0, token)
     input_grad, token = call(
         first_backward,
-        (shape_of(frames, rows, *block), shape_of(8, channels, dtype=F32)),
+        (shape_of(frames, rows, *block), mark),
         grad_0,
         later_0,
         above_0,
@@ -347,7 +371,8 @@
     by_frame = call(
         sum_tiles,
         shape_of(groups, channels // groups, padded),
-        arrived,
+        arrived_0,
+        arrived_1,
         token,
         scratch=(pltpu.VMEM((padded, channels), F32),),
     )
@@ -370,4 +395,5 @@
         P("frame", "tile", None, None),
     )
     out_specs = (P("frame", "tile", None, None), P(None, "tile", "frame"))
+
     return jax.shard_map(local, mesh=mesh, in_specs=in_specs, out_specs=out_specs, check_vma=False)

time: 103 us -> 112 us (1.087)
  the two profiles are of different devices: /device:TPU:2 before, /device:TPU:32 now
where the time goes in v4:
time: 112 us; the launch traced here: 111 us
  starting transfers between devices  38.1 us (34%)
  blocking collectives  30.1 us (27%)
  waiting for transfers between devices  29.5 us (26%)
  Pallas kernels  9.38 us (8%)
  local copies, waits for them, and re-layouts  2.33 us (2%)
    all_to_all x1, blocking collectives, local(): lax.all_to_all(by_frame, 'frame', split_axis=0, concat_axis=0, tiled=True)  30.1 us
    all_to_all x2, starting transfers between devices, sent_and_paired(): lax.all_to_all(paired, 'tile', split_axis=0, concat_axis=0, tiled=True, a...  15.1 us
    ppermute x2, waiting for transfers between devices, from_above(): lax.ppermute(value, 'tile', [(i, (i + 1) % tiles) for i in range(tiles)])  12.1 us
    ppermute x2, waiting for transfers between devices, earlier_frames(): return lax.ppermute(value, 'frame', [(i + 1, i) for i in range(groups - 1)])  11.2 us
    pallas_call x11, Pallas kernels, call(): pl.pallas_call(kernel, out_shape=out_shape, scratch_shapes=list(scratch),...  9.38 us
    ppermute x2, starting transfers between devices, next_frames(): lax.ppermute(value, 'frame', [(i, i + steps) for i in range(groups - step...  8.04 us
    ppermute x2, starting transfers between devices, partner(): return lax.ppermute(value, 'tile', [(i, i ^ 1) for i in range(tiles)])  5.93 us
    ppermute x2, starting transfers between devices, from_above(): lax.ppermute(value, 'tile', [(i, (i + 1) % tiles) for i in range(tiles)])  3.82 us
  transfers between devices with their start and end apart: 11, of which 8 were waited for; matrix products, arithmetic and copies ran while one was open for 2% of the time, Pallas kernels for 3%

profile of v4, /device:TPU:32, one launch (start us, length us, event | category | flops | bytes accessed | tf_op | source)
XLA Modules:
  0.0 111.1 jit_solution(13543467934084779920)
XLA Ops:
  0.6 0.9 multiply_convert_fusion.own_ref
  1.6 3.4 %collective-permute-start = (bf16[2,4,32,128]{3,2,1,0:T(8,128)(2,1)S(1)}, bf16[2,4,32,128]{3,2,1,0:T(8,128)(2,1)S(1)}, u32[]{:S(2)}, u32[]{:S(2)}) collective-permute-start(bf16[2,4,32,128]{3,2,1,0:T(8,128)(2,1)S(1)} %multiply_convert_fusion.own_ref), channel_id=1, source_target_pairs={{0,32},{32,64},{64,96},{96,128},{128,160},{160,192},{192,224},{224... | collective-permute-start | bytes 196616 | tf_op jit(solution)/shard_map/ppermute | solution.py:270
  5.0 4.6 %collective-permute-start.1 = (bf16[2,4,32,128]{3,2,1,0:T(8,128)(2,1)S(1)}, bf16[2,4,32,128]{3,2,1,0:T(8,128)(2,1)S(1)}, u32[]{:S(2)}, u32[]{:S(2)}) collective-permute-start(bf16[2,4,32,128]{3,2,1,0:T(8,128)(2,1)S(1)} %multiply_convert_fusion.own_ref), channel_id=1, source_target_pairs={{0,64},{32,96},{64,128},{96,160},{128,192},{160,224},{192,256},{22... | collective-permute-start | bytes 196616 | tf_op jit(solution)/shard_map/ppermute | solution.py:270
  9.6 0.8 slice.11
  10.4 0.0 collective-permute-done.earlier_ref
  10.4 1.1 %collective-permute-done.1.earliest_ref = bf16[2,4,32,128]{3,2,1,0:T(8,128)(2,1)S(1)} collective-permute-done((bf16[2,4,32,128]{3,2,1,0:T(8,128)(2,1)S(1)}, bf16[2,4,32,128]{3,2,1,0:T(8,128)(2,1)S(1)}, u32[]{:S(2)}, u32[]{:S(2)}) %collective-permute-start.1) | collective-permute-done | bytes 65568 | tf_op jit(solution)/shard_map/ppermute | solution.py:270
  11.5 0.0 copy-start
  11.6 0.0 copy-start.1
  11.6 2.6 %collective-permute-start.2 = (bf16[28,32,128]{2,1,0:T(8,128)(2,1)S(1)}, bf16[28,32,128]{2,1,0:T(8,128)(2,1)S(1)}, u32[]{:S(2)}, u32[]{:S(2)}) collective-permute-start(bf16[28,32,128]{2,1,0:T(8,128)(2,1)S(1)} %pad_maximum_fusion), channel_id=1, source_target_pairs={{1,0},{2,1},{3,2},{4,3},{5,4},{6,5},{7,6},{8,7},{9,8},{10,9},{11,1... | collective-permute-start | bytes 688136 | tf_op jit(solution)/shard_map/ppermute | solution.py:276
  14.2 1.6 %slice_bitcast_fusion = (bf16[27,128,128]{2,1,0:T(8,128)(2,1)S(1)}, bf16[27,128,128]{2,1,0:T(8,128)(2,1)S(1)}) fusion(bf16[2,27,128,128]{3,2,1,0:T(8,128)(2,1)} %param.7), kind=kLoop, calls=%fused_computation | loop fusion | bytes 3538944 | tf_op jit(solution)/shard_map/squeeze | solution.py:307
  15.7 2.0 %collective-permute-done.2.below_ref = bf16[28,32,128]{2,1,0:T(8,128)(2,1)S(1)} collective-permute-done((bf16[28,32,128]{2,1,0:T(8,128)(2,1)S(1)}, bf16[28,32,128]{2,1,0:T(8,128)(2,1)S(1)}, u32[]{:S(2)}, u32[]{:S(2)}) %collective-permute-start.2) | collective-permute-done | bytes 229408 | tf_op jit(solution)/shard_map/ppermute | solution.py:276
  17.7 0.0 copy-done
  17.7 0.0 copy-done.1
  17.7 2.7 %shard_map.68 = (bf16[6,4,32,128]{3,2,1,0:T(8,128)(2,1)S(1)}, f32[256,128]{1,0:T(8,128)S(1)}, bf16[4,2,32,128]{3,2,1,0:T(8,128)(2,1)S(1)}) custom-call(bf16[2,4,32,128]{3,2,1,0:T(8,128)(2,1)S(1)} %multiply_convert_fusion.own_ref, bf16[2,4,32,128]{3,2,1,0:T(8,128)(2,1)S(1)} %collective-permute-done.earlier_ref, ...), custom_call_target="tpu_custom_call" | custom-call | tf_op jit(solution)/shard_map/pallas_call | solution.py:18
  20.4 0.8 shard_map.69
  21.2 4.0 %collective-permute-start.5 = (bf16[16,27,4,128]{3,2,1,0:T(4,128)(2,1)S(1)}, bf16[16,27,4,128]{3,2,1,0:T(4,128)(2,1)S(1)}, u32[]{:S(2)}, u32[]{:S(2)}) collective-permute-start(bf16[16,27,4,128]{3,2,1,0:T(4,128)(2,1)S(1)} %get-tuple-element.21), channel_id=1, source_target_pairs={{0,1},{1,0},{2,3},{3,2},{4,5},{5,4},{6,7},{7,6},{8,9},{9,8},{10,11... | collective-permute-start | bytes 1327112 | tf_op jit(solution)/shard_map/ppermute | solution.py:282
  25.2 1.4 %collective-permute-done.5.came_ref = bf16[16,27,4,128]{3,2,1,0:T(4,128)(2,1)S(1)} collective-permute-done((bf16[16,27,4,128]{3,2,1,0:T(4,128)(2,1)S(1)}, bf16[16,27,4,128]{3,2,1,0:T(4,128)(2,1)S(1)}, u32[]{:S(2)}, u32[]{:S(2)}) %collective-permute-start.5) | collective-permute-done | bytes 442400 | tf_op jit(solution)/shard_map/ppermute | solution.py:282
  26.6 1.0 shard_map.71
  27.6 7.9 %all-to-all-start.1 = ((bf16[16,27,4,128]{3,2,1,0:T(4,128)(2,1)}), bf16[16,27,4,128]{3,2,1,0:T(4,128)(2,1)S(1)}, u32[]{:S(2)}, u32[]{:S(2)}) async-start(bf16[16,27,4,128]{3,2,1,0:T(4,128)(2,1)} %get-tuple-element.28), calls=%async_computation.1 | async-start | bytes 884736 | tf_op jit(solution)/shard_map/all_to_all | solution.py:326
  35.4 1.3 %collective-permute-start.3 = (bf16[4,2,32,128]{3,2,1,0:T(8,128)(2,1)S(1)}, bf16[4,2,32,128]{3,2,1,0:T(8,128)(2,1)S(1)}, u32[]{:S(2)}, u32[]{:S(2)}) collective-permute-start(bf16[4,2,32,128]{3,2,1,0:T(8,128)(2,1)S(1)} %get-tuple-element.16.grad_ref.own_ref), channel_id=1, source_target_pairs={{32,0},{64,32},{96,64},{128,96},{160,128},{192,160},{224,192},{256... | collective-permute-start | bytes 196616 | tf_op jit(solution)/shard_map/ppermute | solution.py:273
  36.7 6.3 %collective-permute-done.3.later_ref = bf16[4,2,32,128]{3,2,1,0:T(8,128)(2,1)S(1)} collective-permute-done((bf16[4,2,32,128]{3,2,1,0:T(8,128)(2,1)S(1)}, bf16[4,2,32,128]{3,2,1,0:T(8,128)(2,1)S(1)}, u32[]{:S(2)}, u32[]{:S(2)}) %collective-permute-start.3) | collective-permute-done | bytes 65568 | tf_op jit(solution)/shard_map/ppermute | solution.py:273
  43.1 1.9 %collective-permute-start.4 = (bf16[2,4,32,128]{3,2,1,0:T(8,128)(2,1)S(1)}, bf16[2,4,32,128]{3,2,1,0:T(8,128)(2,1)S(1)}, u32[]{:S(2)}, u32[]{:S(2)}) collective-permute-start(bf16[2,4,32,128]{3,2,1,0:T(8,128)(2,1)S(1)} %shard_map.70), channel_id=1, source_target_pairs={{0,1},{1,2},{2,3},{3,4},{4,5},{5,6},{6,7},{7,8},{8,9},{9,10},{10,1... | collective-permute-start | bytes 196616 | tf_op jit(solution)/shard_map/ppermute | solution.py:279
  45.0 5.8 %collective-permute-done.4.above_ref = bf16[2,4,32,128]{3,2,1,0:T(8,128)(2,1)S(1)} collective-permute-done((bf16[2,4,32,128]{3,2,1,0:T(8,128)(2,1)S(1)}, bf16[2,4,32,128]{3,2,1,0:T(8,128)(2,1)S(1)}, u32[]{:S(2)}, u32[]{:S(2)}) %collective-permute-start.4) | collective-permute-done | bytes 65568 | tf_op jit(solution)/shard_map/ppermute | solution.py:279
  50.8 0.8 shard_map.72.grad_ref.own_ref
  51.5 0.8 shard_map.73
  52.3 1.9 %collective-permute-start.7 = (bf16[16,27,4,128]{3,2,1,0:T(4,128)(2,1)S(1)}, bf16[16,27,4,128]{3,2,1,0:T(4,128)(2,1)S(1)}, u32[]{:S(2)}, u32[]{:S(2)}) collective-permute-start(bf16[16,27,4,128]{3,2,1,0:T(4,128)(2,1)S(1)} %get-tuple-element.24), channel_id=1, source_target_pairs={{0,1},{1,0},{2,3},{3,2},{4,5},{5,4},{6,7},{7,6},{8,9},{9,8},{10,11... | collective-permute-start | bytes 1327112 | tf_op jit(solution)/shard_map/ppermute | solution.py:282
  54.2 1.8 %collective-permute-done.7.came_ref = bf16[16,27,4,128]{3,2,1,0:T(4,128)(2,1)S(1)} collective-permute-done((bf16[16,27,4,128]{3,2,1,0:T(4,128)(2,1)S(1)}, bf16[16,27,4,128]{3,2,1,0:T(4,128)(2,1)S(1)}, u32[]{:S(2)}, u32[]{:S(2)}) %collective-permute-start.7) | collective-permute-done | bytes 442400 | tf_op jit(solution)/shard_map/ppermute | solution.py:282
  56.0 1.0 shard_map.74
  57.0 0.0 all-to-all-done.1.second_ref
  57.0 7.2 %all-to-all-start = ((bf16[16,27,4,128]{3,2,1,0:T(4,128)(2,1)}), bf16[16,27,4,128]{3,2,1,0:T(4,128)(2,1)S(1)}, u32[]{:S(2)}, u32[]{:S(2)}) async-start(bf16[16,27,4,128]{3,2,1,0:T(4,128)(2,1)} %get-tuple-element.27), calls=%async_computation | async-start | bytes 884736 | tf_op jit(solution)/shard_map/all_to_all | solution.py:326
  64.2 1.3 %collective-permute-start.6 = (bf16[4,2,32,128]{3,2,1,0:T(8,128)(2,1)S(1)}, bf16[4,2,32,128]{3,2,1,0:T(8,128)(2,1)S(1)}, u32[]{:S(2)}, u32[]{:S(2)}) collective-permute-start(bf16[4,2,32,128]{3,2,1,0:T(8,128)(2,1)S(1)} %shard_map.72.grad_ref.own_ref), channel_id=1, source_target_pairs={{32,0},{64,32},{96,64},{128,96},{160,128},{192,160},{224,192},{256... | collective-permute-start | bytes 196616 | tf_op jit(solution)/shard_map/ppermute | solution.py:273
  65.5 4.9 %collective-permute-done.6.later_ref = bf16[4,2,32,128]{3,2,1,0:T(8,128)(2,1)S(1)} collective-permute-done((bf16[4,2,32,128]{3,2,1,0:T(8,128)(2,1)S(1)}, bf16[4,2,32,128]{3,2,1,0:T(8,128)(2,1)S(1)}, u32[]{:S(2)}, u32[]{:S(2)}) %collective-permute-start.6) | collective-permute-done | bytes 65568 | tf_op jit(solution)/shard_map/ppermute | solution.py:273
  70.4 1.9 %collective-permute-start.8 = (bf16[2,4,32,128]{3,2,1,0:T(8,128)(2,1)S(1)}, bf16[2,4,32,128]{3,2,1,0:T(8,128)(2,1)S(1)}, u32[]{:S(2)}, u32[]{:S(2)}) collective-permute-start(bf16[2,4,32,128]{3,2,1,0:T(8,128)(2,1)S(1)} %shard_map.75), channel_id=1, source_target_pairs={{0,1},{1,2},{2,3},{3,4},{4,5},{5,6},{6,7},{7,8},{8,9},{9,10},{10,1... | collective-permute-start | bytes 196616 | tf_op jit(solution)/shard_map/ppermute | solution.py:279
  72.3 6.3 %collective-permute-done.8.above_ref = bf16[2,4,32,128]{3,2,1,0:T(8,128)(2,1)S(1)} collective-permute-done((bf16[2,4,32,128]{3,2,1,0:T(8,128)(2,1)S(1)}, bf16[2,4,32,128]{3,2,1,0:T(8,128)(2,1)S(1)}, u32[]{:S(2)}, u32[]{:S(2)}) %collective-permute-start.8) | collective-permute-done | bytes 65568 | tf_op jit(solution)/shard_map/ppermute | solution.py:279
  78.6 1.3 %shard_map.76 = (bf16[2,4,32,128]{3,2,1,0:T(8,128)(2,1)}, f32[8,128]{1,0:T(8,128)S(1)}) custom-call(bf16[4,2,32,128]{3,2,1,0:T(8,128)(2,1)S(1)} %shard_map.72.grad_ref.own_ref, bf16[4,2,32,128]{3,2,1,0:T(8,128)(2,1)S(1)} %collective-permute-done.6.later_ref, bf16[2,4,32,128]{3,2,1,0:T(8,128)(2,1)S(1)} %collective-permute-done.8.above_ref, ...), custom_call_target="tpu_custom_call" | custom-call | tf_op jit(solution)/shard_map/pallas_call | solution.py:18
  79.9 0.0 all-to-all-done.first_ref
  80.0 0.4 shard_map.77
  80.3 30.1 %all_to_all.15.refs_0_ = bf16[16,8,256]{2,1,0:T(8,128)(2,1)S(1)} all-to-all(bf16[16,8,256]{2,1,0:T(8,128)(2,1)S(1)} %shard_map.77), channel_id=1, replica_groups=mesh['frame'=16,'tile'=32] {'frame'}, dimensions={0} | all-to-all | bytes 131072 | tf_op jit(solution)/shard_map/all_to_all | solution.py:379
  110.4 0.7 shard_map.78
  (3 shorter events, 0.0 us)
Async XLA Ops:
  1.6 8.8 %collective-permute-start = (bf16[2,4,32,128]{3,2,1,0:T(8,128)(2,1)S(1)}, bf16[2,4,32,128]{3,2,1,0:T(8,128)(2,1)S(1)}, u32[]{:S(2)}, u32[]{:S(2)}) collective-permute-start(bf16[2,4,32,128]{3,2,1,0:T(8,128)(2,1)S(1)} %multiply_convert_fusion.own_ref), channel_id=1, source_target_pairs={{0,32},{32,64},{64,96},{96,128},{128,160},{160,192},{192,224},{224... | collective-permute-start | bytes 196616 | tf_op jit(solution)/shard_map/ppermute | solution.py:270
  5.0 6.5 %collective-permute-start.1 = (bf16[2,4,32,128]{3,2,1,0:T(8,128)(2,1)S(1)}, bf16[2,4,32,128]{3,2,1,0:T(8,128)(2,1)S(1)}, u32[]{:S(2)}, u32[]{:S(2)}) collective-permute-start(bf16[2,4,32,128]{3,2,1,0:T(8,128)(2,1)S(1)} %multiply_convert_fusion.own_ref), channel_id=1, source_target_pairs={{0,64},{32,96},{64,128},{96,160},{128,192},{160,224},{192,256},{22... | collective-permute-start | bytes 196616 | tf_op jit(solution)/shard_map/ppermute | solution.py:270
  11.5 6.2 %copy-start = (bf16[2,4,32,128]{3,2,1,0:T(8,128)(2,1)S(1)}, bf16[2,4,32,128]{3,2,1,0:T(8,128)(2,1)}, u32[]{:S(2)}) copy-start(bf16[2,4,32,128]{3,2,1,0:T(8,128)(2,1)} %top_ref.1) | copy-start | bytes 196612
  11.6 6.1 %copy-start.1 = (f32[2,128]{1,0:T(2,128)S(1)}, f32[2,128]{1,0:T(2,128)}, u32[]{:S(2)}) copy-start(f32[2,128]{1,0:T(2,128)} %gain_ref.3) | copy-start | bytes 3076
  11.6 6.1 %collective-permute-start.2 = (bf16[28,32,128]{2,1,0:T(8,128)(2,1)S(1)}, bf16[28,32,128]{2,1,0:T(8,128)(2,1)S(1)}, u32[]{:S(2)}, u32[]{:S(2)}) collective-permute-start(bf16[28,32,128]{2,1,0:T(8,128)(2,1)S(1)} %pad_maximum_fusion), channel_id=1, source_target_pairs={{1,0},{2,1},{3,2},{4,3},{5,4},{6,5},{7,6},{8,7},{9,8},{10,9},{11,1... | collective-permute-start | bytes 688136 | tf_op jit(solution)/shard_map/ppermute | solution.py:276
  21.2 5.4 %collective-permute-start.5 = (bf16[16,27,4,128]{3,2,1,0:T(4,128)(2,1)S(1)}, bf16[16,27,4,128]{3,2,1,0:T(4,128)(2,1)S(1)}, u32[]{:S(2)}, u32[]{:S(2)}) collective-permute-start(bf16[16,27,4,128]{3,2,1,0:T(4,128)(2,1)S(1)} %get-tuple-element.21), channel_id=1, source_target_pairs={{0,1},{1,0},{2,3},{3,2},{4,5},{5,4},{6,7},{7,6},{8,9},{9,8},{10,11... | collective-permute-start | bytes 1327112 | tf_op jit(solution)/shard_map/ppermute | solution.py:282
  27.6 29.4 %all-to-all-start.1 = ((bf16[16,27,4,128]{3,2,1,0:T(4,128)(2,1)}), bf16[16,27,4,128]{3,2,1,0:T(4,128)(2,1)S(1)}, u32[]{:S(2)}, u32[]{:S(2)}) async-start(bf16[16,27,4,128]{3,2,1,0:T(4,128)(2,1)} %get-tuple-element.28), calls=%async_computation.1 | async-start | bytes 884736 | tf_op jit(solution)/shard_map/all_to_all | solution.py:326
  35.4 7.6 %collective-permute-start.3 = (bf16[4,2,32,128]{3,2,1,0:T(8,128)(2,1)S(1)}, bf16[4,2,32,128]{3,2,1,0:T(8,128)(2,1)S(1)}, u32[]{:S(2)}, u32[]{:S(2)}) collective-permute-start(bf16[4,2,32,128]{3,2,1,0:T(8,128)(2,1)S(1)} %get-tuple-element.16.grad_ref.own_ref), channel_id=1, source_target_pairs={{32,0},{64,32},{96,64},{128,96},{160,128},{192,160},{224,192},{256... | collective-permute-start | bytes 196616 | tf_op jit(solution)/shard_map/ppermute | solution.py:273
  43.1 7.7 %collective-permute-start.4 = (bf16[2,4,32,128]{3,2,1,0:T(8,128)(2,1)S(1)}, bf16[2,4,32,128]{3,2,1,0:T(8,128)(2,1)S(1)}, u32[]{:S(2)}, u32[]{:S(2)}) collective-permute-start(bf16[2,4,32,128]{3,2,1,0:T(8,128)(2,1)S(1)} %shard_map.70), channel_id=1, source_target_pairs={{0,1},{1,2},{2,3},{3,4},{4,5},{5,6},{6,7},{7,8},{8,9},{9,10},{10,1... | collective-permute-start | bytes 196616 | tf_op jit(solution)/shard_map/ppermute | solution.py:279
  52.3 3.7 %collective-permute-start.7 = (bf16[16,27,4,128]{3,2,1,0:T(4,128)(2,1)S(1)}, bf16[16,27,4,128]{3,2,1,0:T(4,128)(2,1)S(1)}, u32[]{:S(2)}, u32[]{:S(2)}) collective-permute-start(bf16[16,27,4,128]{3,2,1,0:T(4,128)(2,1)S(1)} %get-tuple-element.24), channel_id=1, source_target_pairs={{0,1},{1,0},{2,3},{3,2},{4,5},{5,4},{6,7},{7,6},{8,9},{9,8},{10,11... | collective-permute-start | bytes 1327112 | tf_op jit(solution)/shard_map/ppermute | solution.py:282
  57.0 22.9 %all-to-all-start = ((bf16[16,27,4,128]{3,2,1,0:T(4,128)(2,1)}), bf16[16,27,4,128]{3,2,1,0:T(4,128)(2,1)S(1)}, u32[]{:S(2)}, u32[]{:S(2)}) async-start(bf16[16,27,4,128]{3,2,1,0:T(4,128)(2,1)} %get-tuple-element.27), calls=%async_computation | async-start | bytes 884736 | tf_op jit(solution)/shard_map/all_to_all | solution.py:326
  64.2 6.2 %collective-permute-start.6 = (bf16[4,2,32,128]{3,2,1,0:T(8,128)(2,1)S(1)}, bf16[4,2,32,128]{3,2,1,0:T(8,128)(2,1)S(1)}, u32[]{:S(2)}, u32[]{:S(2)}) collective-permute-start(bf16[4,2,32,128]{3,2,1,0:T(8,128)(2,1)S(1)} %shard_map.72.grad_ref.own_ref), channel_id=1, source_target_pairs={{32,0},{64,32},{96,64},{128,96},{160,128},{192,160},{224,192},{256... | collective-permute-start | bytes 196616 | tf_op jit(solution)/shard_map/ppermute | solution.py:273
  70.4 8.2 %collective-permute-start.8 = (bf16[2,4,32,128]{3,2,1,0:T(8,128)(2,1)S(1)}, bf16[2,4,32,128]{3,2,1,0:T(8,128)(2,1)S(1)}, u32[]{:S(2)}, u32[]{:S(2)}) collective-permute-start(bf16[2,4,32,128]{3,2,1,0:T(8,128)(2,1)S(1)} %shard_map.75), channel_id=1, source_target_pairs={{0,1},{1,2},{2,3},{3,4},{4,5},{5,6},{6,7},{7,8},{8,9},{9,10},{10,1... | collective-permute-start | bytes 196616 | tf_op jit(solution)/shard_map/ppermute | solution.py:279

commit v5 on v4

--- a/solution.py
+++ b/solution.py
@@ -33,22 +33,46 @@
     return before.astype(BF16).reshape(shape), block, after.astype(BF16).reshape(shape)
 
 
-def fill(patches, window, frames, rows, sign, seams):
-    columns, channels = window[0][0][0].shape
-    for row in range(rows):
-        for frame in range(frames):
-            first = (row * frames + frame) * columns
-            for tap in range(TAPS):
-                depth, down, across = tap // 9, tap // 3 % 3, tap % 3
-                if sign > 0:
-                    source = window[row + down][frame + depth][across]
-                else:
-                    source = window[row + 2 - down][frame + 2 - depth][2 - across]
-                    down = 2 - down
-                seam = seams.get((row, down))
-                if seam is not None:
-                    source = jnp.where(seam, jnp.zeros_like(source), source)
-                patches[first : first + columns, tap * channels : (tap + 1) * channels] = source
+def store_columns(store, window, order, seams):
+    for row, blocks in enumerate(window):
+        for frame, triple in enumerate(blocks):
+            store[row, frame] = jnp.concatenate([triple[across] for across in order], axis=1)
+    for extra, ((row, offset), seam) in enumerate(seams.items()):
+        for frame in range(store.shape[1]):
+            source = store[row + offset, frame]
+            store[len(window) + extra, frame] = jnp.where(seam, jnp.zeros_like(source), source)
+
+
+def side_by_side(store, seams, rows, frames, sign, index):
+    depth, down = divmod(index, 3)
+    if sign < 0:
+        depth, down = 2 - depth, 2 - down
+    extra, total = list(seams), store.shape[0] - len(seams)
+    pieces = []
+    for row in rows:
+        place = total + extra.index((row, down)) if (row, down) in seams else row + down
+        pieces.append(store[place, depth : depth + frames].reshape(-1, store.shape[-1]))
+    return jnp.concatenate(pieces, axis=0)
+
+
+def product(store, seams, rows, frames, sign, kernel_ref):
+    total = None
+    for index in range(0, 9, 2):
+        members = range(index, min(index + 2, 9))
+        cells = jnp.concatenate(
+            [side_by_side(store, seams, rows, frames, sign, member) for member in members], axis=1
+        )
+        taps = range(3 * members[0], 3 * members[-1] + 3)
+        if sign > 0:
+            weights = kernel_ref[taps[0] : taps[-1] + 1].reshape(-1, kernel_ref.shape[-1])
+            part = jnp.dot(cells, weights, preferred_element_type=F32)
+        else:
+            weights = jnp.concatenate([kernel_ref[tap] for tap in taps], axis=1)
+            part = lax.dot_general(
+                cells, weights, (((1,), (1,)), ((), ())), preferred_element_type=F32
+            )
+        total = part if total is None else total + part
+    return total
 
 
 def window_of(rows):
@@ -57,15 +81,6 @@
 
 def block_rows(ref):
     return [[ref[row, frame] for frame in range(ref.shape[1])] for row in range(ref.shape[0])]
-
-
-def product(patches, kernel_ref, chunk=256):
-    weights = kernel_ref[...].reshape(-1, kernel_ref.shape[-1])
-    pieces = [
-        jnp.dot(patches[start : start + chunk], weights, preferred_element_type=F32)
-        for start in range(0, patches.shape[0], chunk)
-    ]
-    return pieces
 
 
 def silu_parts(pre_norm, gain):
@@ -104,27 +119,29 @@
 
 def forward(
     own_ref, earlier_ref, earliest_ref, below_ref, top_ref, first_kernel_ref, second_kernel_ref,
-    gain_ref, next_ref, pre_ref, grad_ref, wide_patches, patches,
+    gain_ref, next_ref, pre_ref, grad_ref, wide_store, store,
 ):
     frames, rows, columns, _ = own_ref.shape
     last = at_last_tile()
     window = window_of(first_rows((earliest_ref, earlier_ref, own_ref), below_ref, 2 * rows))
     wide, deep = 2 * rows - 2, 2 * frames
-    fill(wide_patches, window, deep, wide, 1, {(rows - 2, 2): last, (rows - 1, 0): last})
-    own_cells, blocks = frames * columns, 8
-    for number, pre_norm in enumerate(product(wide_patches, first_kernel_ref, blocks * columns)):
+    seams = {(rows - 2, 2): last, (rows - 1, 0): last}
+    store_columns(wide_store, window, (0, 1, 2), seams)
+    own_cells = frames * columns
+    for first in range(0, wide, 2):
+        pre_norm = product(wide_store, seams, (first, first + 1), deep, 1, first_kernel_ref)
         _, normed, sigma = silu_parts(pre_norm, gain_ref[0:1])
         value = (normed * sigma).astype(BF16)
-        for block in range(blocks):
-            row, frame = divmod(number * blocks + block, deep)
+        for block in range(2 * deep):
+            row, frame = first + block // deep, block % deep
             cells = slice(block * columns, (block + 1) * columns)
             next_ref[row, frame] = value[cells]
             if row < rows and frame >= frames:
                 start = row * own_cells + (frame - frames) * columns
                 pre_ref[start : start + columns] = pre_norm[cells]
-    window = window_of(block_rows(next_ref))
-    fill(patches, window, frames, rows, 1, {(rows - 3, 2): last, (rows - 2, 0): last})
-    (pre_norm,) = product(patches, second_kernel_ref)
+    seams = {(rows - 3, 2): last, (rows - 2, 0): last}
+    store_columns(store, window_of(block_rows(next_ref)), (0, 1, 2), seams)
+    pre_norm = product(store, seams, range(rows), frames, 1, second_kernel_ref)
     spread = []
     for row in range(rows):
         for frame in range(frames):
@@ -149,31 +166,25 @@
     return result
 
 
-def back_product(patches, kernel_ref):
-    turned = jnp.concatenate([kernel_ref[tap] for tap in range(TAPS)], axis=1)
-    return lax.dot_general(
-        patches[...], turned, (((1,), (1,)), ((), ())), preferred_element_type=F32
-    )
-
-
 def second_backward(
-    own_ref, later_ref, above_ref, kernel_ref, gain_ref, pre_ref, token_ref, grad_ref, patches
+    own_ref, later_ref, above_ref, kernel_ref, gain_ref, pre_ref, token_ref, grad_ref, store
 ):
     del token_ref
     rows, frames, _, _ = own_ref.shape
     last = at_last_tile()
+    seams = {(rows - 2, 2): last, (rows - 1, 0): last}
     window = window_of(backward_rows(own_ref, later_ref, above_ref, frames))
-    fill(patches, window, frames, rows, -1, {(rows - 2, 2): last, (rows - 1, 0): last})
-    upstream = back_product(patches, kernel_ref).astype(BF16).astype(F32)
+    store_columns(store, window, (2, 1, 0), seams)
+    upstream = product(store, seams, range(rows), frames, -1, kernel_ref).astype(BF16).astype(F32)
     grad_ref[...] = pre_norm_gradient(pre_ref[...], gain_ref[0:1], upstream).reshape(grad_ref.shape)
 
 
-def first_backward(own_ref, later_ref, above_ref, kernel_ref, out_ref, token_ref, patches):
+def first_backward(own_ref, later_ref, above_ref, kernel_ref, out_ref, token_ref, store):
     rows, frames, columns, _ = own_ref.shape
-    first, last = lax.axis_index("tile") == 0, at_last_tile()
+    seams = {(0, 0): lax.axis_index("tile") == 0, (rows - 1, 2): at_last_tile()}
     window = window_of(backward_rows(own_ref, later_ref, above_ref, frames))
-    fill(patches, window, frames, rows, -1, {(0, 0): first, (rows - 1, 2): last})
-    grad = back_product(patches, kernel_ref).astype(BF16)
+    store_columns(store, window, (2, 1, 0), seams)
+    grad = product(store, seams, range(rows), frames, -1, kernel_ref).astype(BF16)
     for row in range(rows):
         for frame in range(frames):
             cell = (row * frames + frame) * columns
@@ -181,37 +192,43 @@
     token_ref[...] = grad[: token_ref.shape[0]].astype(F32)
 
 
-def split_gradient(patches, grad_ref, keep_ref, send_ref):
+def split_gradient(store, seams, grad_ref, keep_ref, send_ref):
     chips, _, share, channels = keep_ref.shape
+    rows, frames, _, _ = grad_ref.shape
     odd = lax.axis_index("tile") % 2 == 1
     grad = grad_ref[...].reshape(-1, channels)
-    for tap in range(TAPS):
-        block = lax.dot_general(
-            patches[:, tap * channels : (tap + 1) * channels],
+    for index in range(9):
+        blocks = lax.dot_general(
+            side_by_side(store, seams, range(rows), frames, 1, index),
             grad,
             (((0,), (0,)), ((), ())),
             preferred_element_type=F32,
-        ).reshape(chips, 2, share, channels)
-        even_part, odd_part = block[:, 0], block[:, 1]
-        keep_ref[:, tap] = jnp.where(odd, odd_part, even_part).astype(BF16)
-        send_ref[:, tap] = jnp.where(odd, even_part, odd_part).astype(BF16)
-
-
-def second_kernel_gradient(next_ref, grad_ref, keep_ref, send_ref, token_ref, patches):
-    rows, frames, _, _ = grad_ref.shape
+        )
+        for across in range(3):
+            block = blocks[across * channels : (across + 1) * channels]
+            block = block.reshape(chips, 2, share, channels)
+            even_part, odd_part = block[:, 0], block[:, 1]
+            tap = 3 * index + across
+            keep_ref[:, tap] = jnp.where(odd, odd_part, even_part).astype(BF16)
+            send_ref[:, tap] = jnp.where(odd, even_part, odd_part).astype(BF16)
+
+
+def second_kernel_gradient(next_ref, grad_ref, keep_ref, send_ref, token_ref, store):
+    rows = grad_ref.shape[0]
     last = at_last_tile()
-    window = window_of(block_rows(next_ref))
-    fill(patches, window, frames, rows, 1, {(rows - 3, 2): last, (rows - 2, 0): last})
-    split_gradient(patches, grad_ref, keep_ref, send_ref)
+    seams = {(rows - 3, 2): last, (rows - 2, 0): last}
+    store_columns(store, window_of(block_rows(next_ref)), (0, 1, 2), seams)
+    split_gradient(store, seams, grad_ref, keep_ref, send_ref)
     token_ref[...] = jnp.zeros_like(token_ref)
 
 
-def first_kernel_gradient(own_ref, earlier_ref, below_ref, grad_ref, keep_ref, send_ref, patches):
-    frames, rows, _, _ = own_ref.shape
+def first_kernel_gradient(own_ref, earlier_ref, below_ref, grad_ref, keep_ref, send_ref, store):
+    rows = grad_ref.shape[0]
     last = at_last_tile()
+    seams = {(rows - 2, 2): last, (rows - 1, 0): last}
     window = window_of(first_rows((earlier_ref, own_ref), below_ref, rows + 2))
-    fill(patches, window, frames, rows, 1, {(rows - 2, 2): last, (rows - 1, 0): last})
-    split_gradient(patches, grad_ref, keep_ref, send_ref)
+    store_columns(store, window, (0, 1, 2), seams)
+    split_gradient(store, seams, grad_ref, keep_ref, send_ref)
 
 
 def pack_rows(own_ref, later_ref, token_ref, out_ref):
@@ -263,8 +280,8 @@
     cells = frames * rows * columns
     block = (columns, channels)
 
-    def patch_scratch(count):
-        return (pltpu.VMEM((count, TAPS * channels), BF16),)
+    def column_store(window_rows, window_frames):
+        return (pltpu.VMEM((window_rows + 2, window_frames, columns, 3 * channels), BF16),)
 
     def next_frames(value, steps):
         return lax.ppermute(value, "frame", [(i, i + steps) for i in range(groups - steps)])
@@ -306,7 +323,7 @@
         kernels[0],
         kernels[1],
         norm_gains,
-        scratch=patch_scratch(wide * 2 * frames * columns) + patch_scratch(cells),
+        scratch=column_store(2 * rows, 3 * frames) + column_store(wide, 2 * frames),
     )
 
     share = channels // tiles
@@ -330,7 +347,7 @@
 
     later_1 = earlier_frames(grad_1)
     keep_1, send_1, token = call(
-        second_kernel_gradient, (part, part, mark), next_1, grad_1, scratch=patch_scratch(cells)
+        second_kernel_gradient, (part, part, mark), next_1, grad_1, scratch=column_store(rows + 2, 2 * frames)
     )
     above_1 = with_neighbours(later_1, grad_1, token)
     arrived_1, token = sent_and_paired(keep_1, send_1)
@@ -344,7 +361,7 @@
         norm_gains,
         pre_0,
         token,
-        scratch=patch_scratch(cells),
+        scratch=column_store(rows + 2, 2 * frames),
     )
     keep_0, send_0 = call(
         first_kernel_gradient,
@@ -353,7 +370,7 @@
         earlier_0,
         below,
         grad_0,
-        scratch=patch_scratch(cells),
+        scratch=column_store(rows + 2, 2 * frames),
     )
     arrived_0, token = sent_and_paired(keep_0, send_0)
     later_0 = earlier_frames(grad_0)
@@ -365,7 +382,7 @@
         later_0,
         above_0,
         kernels[0],
-        scratch=patch_scratch(cells),
+        scratch=column_store(rows + 2, 2 * frames),
     )
     padded = -(-2 * TAPS // 32) * 32 * share
     by_frame = call(

time: 112 us -> 112 us (level)
  no operation moved by 1% of the time
where the time goes in v5:
time: 112 us; the launch traced here: 111 us
  starting transfers between devices  38 us (34%)
  blocking collectives  30.1 us (27%)
  waiting for transfers between devices  29.5 us (26%)
  Pallas kernels  9.11 us (8%)
  local copies, waits for them, and re-layouts  2.33 us (2%)
    all_to_all x1, blocking collectives, local(): lax.all_to_all(by_frame, 'frame', split_axis=0, concat_axis=0, tiled=True)  30.1 us
    all_to_all x2, starting transfers between devices, sent_and_paired(): lax.all_to_all(paired, 'tile', split_axis=0, concat_axis=0, tiled=True, a...  15.1 us
    ppermute x2, waiting for transfers between devices, from_above(): lax.ppermute(value, 'tile', [(i, (i + 1) % tiles) for i in range(tiles)])  12.1 us
    ppermute x2, waiting for transfers between devices, earlier_frames(): return lax.ppermute(value, 'frame', [(i + 1, i) for i in range(groups - 1)])  11.2 us
    pallas_call x11, Pallas kernels, call(): pl.pallas_call(kernel, out_shape=out_shape, scratch_shapes=list(scratch),...  9.11 us
    ppermute x2, starting transfers between devices, next_frames(): lax.ppermute(value, 'frame', [(i, i + steps) for i in range(groups - step...  8.04 us
    ppermute x2, starting transfers between devices, partner(): return lax.ppermute(value, 'tile', [(i, i ^ 1) for i in range(tiles)])  5.93 us
    ppermute x2, starting transfers between devices, from_above(): lax.ppermute(value, 'tile', [(i, (i + 1) % tiles) for i in range(tiles)])  3.82 us
  transfers between devices with their start and end apart: 11, of which 8 were waited for; matrix products, arithmetic and copies ran while one was open for 2% of the time, Pallas kernels for 3%

profile of v5, /device:TPU:32, one launch (start us, length us, event | category | flops | bytes accessed | tf_op | source)
XLA Modules:
  0.0 110.9 jit_solution(16519706290639431640)
XLA Ops:
  0.6 0.9 multiply_convert_fusion.own_ref
  1.6 3.4 %collective-permute-start = (bf16[2,4,32,128]{3,2,1,0:T(8,128)(2,1)S(1)}, bf16[2,4,32,128]{3,2,1,0:T(8,128)(2,1)S(1)}, u32[]{:S(2)}, u32[]{:S(2)}) collective-permute-start(bf16[2,4,32,128]{3,2,1,0:T(8,128)(2,1)S(1)} %multiply_convert_fusion.own_ref), channel_id=1, source_target_pairs={{0,32},{32,64},{64,96},{96,128},{128,160},{160,192},{192,224},{224... | collective-permute-start | bytes 196616 | tf_op jit(solution)/shard_map/ppermute | solution.py:287
  5.0 4.6 %collective-permute-start.1 = (bf16[2,4,32,128]{3,2,1,0:T(8,128)(2,1)S(1)}, bf16[2,4,32,128]{3,2,1,0:T(8,128)(2,1)S(1)}, u32[]{:S(2)}, u32[]{:S(2)}) collective-permute-start(bf16[2,4,32,128]{3,2,1,0:T(8,128)(2,1)S(1)} %multiply_convert_fusion.own_ref), channel_id=1, source_target_pairs={{0,64},{32,96},{64,128},{96,160},{128,192},{160,224},{192,256},{22... | collective-permute-start | bytes 196616 | tf_op jit(solution)/shard_map/ppermute | solution.py:287
  9.6 0.8 slice.11
  10.4 0.0 collective-permute-done.earlier_ref
  10.4 1.1 %collective-permute-done.1.earliest_ref = bf16[2,4,32,128]{3,2,1,0:T(8,128)(2,1)S(1)} collective-permute-done((bf16[2,4,32,128]{3,2,1,0:T(8,128)(2,1)S(1)}, bf16[2,4,32,128]{3,2,1,0:T(8,128)(2,1)S(1)}, u32[]{:S(2)}, u32[]{:S(2)}) %collective-permute-start.1) | collective-permute-done | bytes 65568 | tf_op jit(solution)/shard_map/ppermute | solution.py:287
  11.5 0.0 copy-start
  11.6 0.0 copy-start.1
  11.6 2.6 %collective-permute-start.2 = (bf16[28,32,128]{2,1,0:T(8,128)(2,1)S(1)}, bf16[28,32,128]{2,1,0:T(8,128)(2,1)S(1)}, u32[]{:S(2)}, u32[]{:S(2)}) collective-permute-start(bf16[28,32,128]{2,1,0:T(8,128)(2,1)S(1)} %pad_maximum_fusion), channel_id=1, source_target_pairs={{1,0},{2,1},{3,2},{4,3},{5,4},{6,5},{7,6},{8,7},{9,8},{10,9},{11,1... | collective-permute-start | bytes 688136 | tf_op jit(solution)/shard_map/ppermute | solution.py:293
  14.2 1.6 %slice_bitcast_fusion = (bf16[27,128,128]{2,1,0:T(8,128)(2,1)S(1)}, bf16[27,128,128]{2,1,0:T(8,128)(2,1)S(1)}) fusion(bf16[2,27,128,128]{3,2,1,0:T(8,128)(2,1)} %param.7), kind=kLoop, calls=%fused_computation | loop fusion | bytes 3538944 | tf_op jit(solution)/shard_map/squeeze | solution.py:324
  15.7 2.0 %collective-permute-done.2.below_ref = bf16[28,32,128]{2,1,0:T(8,128)(2,1)S(1)} collective-permute-done((bf16[28,32,128]{2,1,0:T(8,128)(2,1)S(1)}, bf16[28,32,128]{2,1,0:T(8,128)(2,1)S(1)}, u32[]{:S(2)}, u32[]{:S(2)}) %collective-permute-start.2) | collective-permute-done | bytes 229408 | tf_op jit(solution)/shard_map/ppermute | solution.py:293
  17.7 0.0 copy-done
  17.7 0.0 copy-done.1
  17.7 2.5 %shard_map.68 = (bf16[6,4,32,128]{3,2,1,0:T(8,128)(2,1)S(1)}, f32[256,128]{1,0:T(8,128)S(1)}, bf16[4,2,32,128]{3,2,1,0:T(8,128)(2,1)S(1)}) custom-call(bf16[2,4,32,128]{3,2,1,0:T(8,128)(2,1)S(1)} %multiply_convert_fusion.own_ref, bf16[2,4,32,128]{3,2,1,0:T(8,128)(2,1)S(1)} %collective-permute-done.earlier_ref, ...), custom_call_target="tpu_custom_call" | custom-call | tf_op jit(solution)/shard_map/pallas_call | solution.py:18
  20.2 0.7 shard_map.69
  21.0 4.0 %collective-permute-start.5 = (bf16[16,27,4,128]{3,2,1,0:T(4,128)(2,1)S(1)}, bf16[16,27,4,128]{3,2,1,0:T(4,128)(2,1)S(1)}, u32[]{:S(2)}, u32[]{:S(2)}) collective-permute-start(bf16[16,27,4,128]{3,2,1,0:T(4,128)(2,1)S(1)} %get-tuple-element.21), channel_id=1, source_target_pairs={{0,1},{1,0},{2,3},{3,2},{4,5},{5,4},{6,7},{7,6},{8,9},{9,8},{10,11... | collective-permute-start | bytes 1327112 | tf_op jit(solution)/shard_map/ppermute | solution.py:299
  25.0 1.4 %collective-permute-done.5.came_ref = bf16[16,27,4,128]{3,2,1,0:T(4,128)(2,1)S(1)} collective-permute-done((bf16[16,27,4,128]{3,2,1,0:T(4,128)(2,1)S(1)}, bf16[16,27,4,128]{3,2,1,0:T(4,128)(2,1)S(1)}, u32[]{:S(2)}, u32[]{:S(2)}) %collective-permute-start.5) | collective-permute-done | bytes 442400 | tf_op jit(solution)/shard_map/ppermute | solution.py:299
  26.4 1.0 shard_map.71
  27.4 7.9 %all-to-all-start.1 = ((bf16[16,27,4,128]{3,2,1,0:T(4,128)(2,1)}), bf16[16,27,4,128]{3,2,1,0:T(4,128)(2,1)S(1)}, u32[]{:S(2)}, u32[]{:S(2)}) async-start(bf16[16,27,4,128]{3,2,1,0:T(4,128)(2,1)} %get-tuple-element.28), calls=%async_computation.1 | async-start | bytes 884736 | tf_op jit(solution)/shard_map/all_to_all | solution.py:343
  35.3 1.3 %collective-permute-start.3 = (bf16[4,2,32,128]{3,2,1,0:T(8,128)(2,1)S(1)}, bf16[4,2,32,128]{3,2,1,0:T(8,128)(2,1)S(1)}, u32[]{:S(2)}, u32[]{:S(2)}) collective-permute-start(bf16[4,2,32,128]{3,2,1,0:T(8,128)(2,1)S(1)} %get-tuple-element.16.grad_ref.own_ref), channel_id=1, source_target_pairs={{32,0},{64,32},{96,64},{128,96},{160,128},{192,160},{224,192},{256... | collective-permute-start | bytes 196616 | tf_op jit(solution)/shard_map/ppermute | solution.py:290
  36.6 6.3 %collective-permute-done.3.later_ref = bf16[4,2,32,128]{3,2,1,0:T(8,128)(2,1)S(1)} collective-permute-done((bf16[4,2,32,128]{3,2,1,0:T(8,128)(2,1)S(1)}, bf16[4,2,32,128]{3,2,1,0:T(8,128)(2,1)S(1)}, u32[]{:S(2)}, u32[]{:S(2)}) %collective-permute-start.3) | collective-permute-done | bytes 65568 | tf_op jit(solution)/shard_map/ppermute | solution.py:290
  42.9 1.9 %collective-permute-start.4 = (bf16[2,4,32,128]{3,2,1,0:T(8,128)(2,1)S(1)}, bf16[2,4,32,128]{3,2,1,0:T(8,128)(2,1)S(1)}, u32[]{:S(2)}, u32[]{:S(2)}) collective-permute-start(bf16[2,4,32,128]{3,2,1,0:T(8,128)(2,1)S(1)} %shard_map.70), channel_id=1, source_target_pairs={{0,1},{1,2},{2,3},{3,4},{4,5},{5,6},{6,7},{7,8},{8,9},{9,10},{10,1... | collective-permute-start | bytes 196616 | tf_op jit(solution)/shard_map/ppermute | solution.py:296
  44.8 5.8 %collective-permute-done.4.above_ref = bf16[2,4,32,128]{3,2,1,0:T(8,128)(2,1)S(1)} collective-permute-done((bf16[2,4,32,128]{3,2,1,0:T(8,128)(2,1)S(1)}, bf16[2,4,32,128]{3,2,1,0:T(8,128)(2,1)S(1)}, u32[]{:S(2)}, u32[]{:S(2)}) %collective-permute-start.4) | collective-permute-done | bytes 65568 | tf_op jit(solution)/shard_map/ppermute | solution.py:296
  50.6 0.7 shard_map.72.grad_ref.own_ref
  51.3 0.7 shard_map.73
  52.1 1.9 %collective-permute-start.7 = (bf16[16,27,4,128]{3,2,1,0:T(4,128)(2,1)S(1)}, bf16[16,27,4,128]{3,2,1,0:T(4,128)(2,1)S(1)}, u32[]{:S(2)}, u32[]{:S(2)}) collective-permute-start(bf16[16,27,4,128]{3,2,1,0:T(4,128)(2,1)S(1)} %get-tuple-element.24), channel_id=1, source_target_pairs={{0,1},{1,0},{2,3},{3,2},{4,5},{5,4},{6,7},{7,6},{8,9},{9,8},{10,11... | collective-permute-start | bytes 1327112 | tf_op jit(solution)/shard_map/ppermute | solution.py:299
  54.0 1.8 %collective-permute-done.7.came_ref = bf16[16,27,4,128]{3,2,1,0:T(4,128)(2,1)S(1)} collective-permute-done((bf16[16,27,4,128]{3,2,1,0:T(4,128)(2,1)S(1)}, bf16[16,27,4,128]{3,2,1,0:T(4,128)(2,1)S(1)}, u32[]{:S(2)}, u32[]{:S(2)}) %collective-permute-start.7) | collective-permute-done | bytes 442400 | tf_op jit(solution)/shard_map/ppermute | solution.py:299
  55.8 1.0 shard_map.74
  56.8 0.0 all-to-all-done.1.second_ref
  56.8 7.2 %all-to-all-start = ((bf16[16,27,4,128]{3,2,1,0:T(4,128)(2,1)}), bf16[16,27,4,128]{3,2,1,0:T(4,128)(2,1)S(1)}, u32[]{:S(2)}, u32[]{:S(2)}) async-start(bf16[16,27,4,128]{3,2,1,0:T(4,128)(2,1)} %get-tuple-element.27), calls=%async_computation | async-start | bytes 884736 | tf_op jit(solution)/shard_map/all_to_all | solution.py:343
  64.0 1.3 %collective-permute-start.6 = (bf16[4,2,32,128]{3,2,1,0:T(8,128)(2,1)S(1)}, bf16[4,2,32,128]{3,2,1,0:T(8,128)(2,1)S(1)}, u32[]{:S(2)}, u32[]{:S(2)}) collective-permute-start(bf16[4,2,32,128]{3,2,1,0:T(8,128)(2,1)S(1)} %shard_map.72.grad_ref.own_ref), channel_id=1, source_target_pairs={{32,0},{64,32},{96,64},{128,96},{160,128},{192,160},{224,192},{256... | collective-permute-start | bytes 196616 | tf_op jit(solution)/shard_map/ppermute | solution.py:290
  65.3 4.9 %collective-permute-done.6.later_ref = bf16[4,2,32,128]{3,2,1,0:T(8,128)(2,1)S(1)} collective-permute-done((bf16[4,2,32,128]{3,2,1,0:T(8,128)(2,1)S(1)}, bf16[4,2,32,128]{3,2,1,0:T(8,128)(2,1)S(1)}, u32[]{:S(2)}, u32[]{:S(2)}) %collective-permute-start.6) | collective-permute-done | bytes 65568 | tf_op jit(solution)/shard_map/ppermute | solution.py:290
  70.1 1.9 %collective-permute-start.8 = (bf16[2,4,32,128]{3,2,1,0:T(8,128)(2,1)S(1)}, bf16[2,4,32,128]{3,2,1,0:T(8,128)(2,1)S(1)}, u32[]{:S(2)}, u32[]{:S(2)}) collective-permute-start(bf16[2,4,32,128]{3,2,1,0:T(8,128)(2,1)S(1)} %shard_map.75), channel_id=1, source_target_pairs={{0,1},{1,2},{2,3},{3,4},{4,5},{5,6},{6,7},{7,8},{8,9},{9,10},{10,1... | collective-permute-start | bytes 196616 | tf_op jit(solution)/shard_map/ppermute | solution.py:296
  72.1 6.3 %collective-permute-done.8.above_ref = bf16[2,4,32,128]{3,2,1,0:T(8,128)(2,1)S(1)} collective-permute-done((bf16[2,4,32,128]{3,2,1,0:T(8,128)(2,1)S(1)}, bf16[2,4,32,128]{3,2,1,0:T(8,128)(2,1)S(1)}, u32[]{:S(2)}, u32[]{:S(2)}) %collective-permute-start.8) | collective-permute-done | bytes 65568 | tf_op jit(solution)/shard_map/ppermute | solution.py:296
  78.4 1.3 %shard_map.76 = (bf16[2,4,32,128]{3,2,1,0:T(8,128)(2,1)}, f32[8,128]{1,0:T(8,128)S(1)}) custom-call(bf16[4,2,32,128]{3,2,1,0:T(8,128)(2,1)S(1)} %shard_map.72.grad_ref.own_ref, bf16[4,2,32,128]{3,2,1,0:T(8,128)(2,1)S(1)} %collective-permute-done.6.later_ref, bf16[2,4,32,128]{3,2,1,0:T(8,128)(2,1)S(1)} %collective-permute-done.8.above_ref, ...), custom_call_target="tpu_custom_call" | custom-call | tf_op jit(solution)/shard_map/pallas_call | solution.py:18
  79.7 0.0 all-to-all-done.first_ref
  79.7 0.4 shard_map.77
  80.1 30.1 %all_to_all.15.refs_0_ = bf16[16,8,256]{2,1,0:T(8,128)(2,1)S(1)} all-to-all(bf16[16,8,256]{2,1,0:T(8,128)(2,1)S(1)} %shard_map.77), channel_id=1, replica_groups=mesh['frame'=16,'tile'=32] {'frame'}, dimensions={0} | all-to-all | bytes 131072 | tf_op jit(solution)/shard_map/all_to_all | solution.py:396
  110.2 0.7 shard_map.78
  (3 shorter events, 0.0 us)
Async XLA Ops:
  1.6 8.8 %collective-permute-start = (bf16[2,4,32,128]{3,2,1,0:T(8,128)(2,1)S(1)}, bf16[2,4,32,128]{3,2,1,0:T(8,128)(2,1)S(1)}, u32[]{:S(2)}, u32[]{:S(2)}) collective-permute-start(bf16[2,4,32,128]{3,2,1,0:T(8,128)(2,1)S(1)} %multiply_convert_fusion.own_ref), channel_id=1, source_target_pairs={{0,32},{32,64},{64,96},{96,128},{128,160},{160,192},{192,224},{224... | collective-permute-start | bytes 196616 | tf_op jit(solution)/shard_map/ppermute | solution.py:287
  5.0 6.5 %collective-permute-start.1 = (bf16[2,4,32,128]{3,2,1,0:T(8,128)(2,1)S(1)}, bf16[2,4,32,128]{3,2,1,0:T(8,128)(2,1)S(1)}, u32[]{:S(2)}, u32[]{:S(2)}) collective-permute-start(bf16[2,4,32,128]{3,2,1,0:T(8,128)(2,1)S(1)} %multiply_convert_fusion.own_ref), channel_id=1, source_target_pairs={{0,64},{32,96},{64,128},{96,160},{128,192},{160,224},{192,256},{22... | collective-permute-start | bytes 196616 | tf_op jit(solution)/shard_map/ppermute | solution.py:287
  11.5 6.2 %copy-start = (bf16[2,4,32,128]{3,2,1,0:T(8,128)(2,1)S(1)}, bf16[2,4,32,128]{3,2,1,0:T(8,128)(2,1)}, u32[]{:S(2)}) copy-start(bf16[2,4,32,128]{3,2,1,0:T(8,128)(2,1)} %top_ref.1) | copy-start | bytes 196612
  11.6 6.1 %copy-start.1 = (f32[2,128]{1,0:T(2,128)S(1)}, f32[2,128]{1,0:T(2,128)}, u32[]{:S(2)}) copy-start(f32[2,128]{1,0:T(2,128)} %gain_ref.3) | copy-start | bytes 3076
  11.6 6.1 %collective-permute-start.2 = (bf16[28,32,128]{2,1,0:T(8,128)(2,1)S(1)}, bf16[28,32,128]{2,1,0:T(8,128)(2,1)S(1)}, u32[]{:S(2)}, u32[]{:S(2)}) collective-permute-start(bf16[28,32,128]{2,1,0:T(8,128)(2,1)S(1)} %pad_maximum_fusion), channel_id=1, source_target_pairs={{1,0},{2,1},{3,2},{4,3},{5,4},{6,5},{7,6},{8,7},{9,8},{10,9},{11,1... | collective-permute-start | bytes 688136 | tf_op jit(solution)/shard_map/ppermute | solution.py:293
  21.0 5.4 %collective-permute-start.5 = (bf16[16,27,4,128]{3,2,1,0:T(4,128)(2,1)S(1)}, bf16[16,27,4,128]{3,2,1,0:T(4,128)(2,1)S(1)}, u32[]{:S(2)}, u32[]{:S(2)}) collective-permute-start(bf16[16,27,4,128]{3,2,1,0:T(4,128)(2,1)S(1)} %get-tuple-element.21), channel_id=1, source_target_pairs={{0,1},{1,0},{2,3},{3,2},{4,5},{5,4},{6,7},{7,6},{8,9},{9,8},{10,11... | collective-permute-start | bytes 1327112 | tf_op jit(solution)/shard_map/ppermute | solution.py:299
  27.4 29.4 %all-to-all-start.1 = ((bf16[16,27,4,128]{3,2,1,0:T(4,128)(2,1)}), bf16[16,27,4,128]{3,2,1,0:T(4,128)(2,1)S(1)}, u32[]{:S(2)}, u32[]{:S(2)}) async-start(bf16[16,27,4,128]{3,2,1,0:T(4,128)(2,1)} %get-tuple-element.28), calls=%async_computation.1 | async-start | bytes 884736 | tf_op jit(solution)/shard_map/all_to_all | solution.py:343
  35.3 7.6 %collective-permute-start.3 = (bf16[4,2,32,128]{3,2,1,0:T(8,128)(2,1)S(1)}, bf16[4,2,32,128]{3,2,1,0:T(8,128)(2,1)S(1)}, u32[]{:S(2)}, u32[]{:S(2)}) collective-permute-start(bf16[4,2,32,128]{3,2,1,0:T(8,128)(2,1)S(1)} %get-tuple-element.16.grad_ref.own_ref), channel_id=1, source_target_pairs={{32,0},{64,32},{96,64},{128,96},{160,128},{192,160},{224,192},{256... | collective-permute-start | bytes 196616 | tf_op jit(solution)/shard_map/ppermute | solution.py:290
  42.9 7.7 %collective-permute-start.4 = (bf16[2,4,32,128]{3,2,1,0:T(8,128)(2,1)S(1)}, bf16[2,4,32,128]{3,2,1,0:T(8,128)(2,1)S(1)}, u32[]{:S(2)}, u32[]{:S(2)}) collective-permute-start(bf16[2,4,32,128]{3,2,1,0:T(8,128)(2,1)S(1)} %shard_map.70), channel_id=1, source_target_pairs={{0,1},{1,2},{2,3},{3,4},{4,5},{5,6},{6,7},{7,8},{8,9},{9,10},{10,1... | collective-permute-start | bytes 196616 | tf_op jit(solution)/shard_map/ppermute | solution.py:296
  52.1 3.7 %collective-permute-start.7 = (bf16[16,27,4,128]{3,2,1,0:T(4,128)(2,1)S(1)}, bf16[16,27,4,128]{3,2,1,0:T(4,128)(2,1)S(1)}, u32[]{:S(2)}, u32[]{:S(2)}) collective-permute-start(bf16[16,27,4,128]{3,2,1,0:T(4,128)(2,1)S(1)} %get-tuple-element.24), channel_id=1, source_target_pairs={{0,1},{1,0},{2,3},{3,2},{4,5},{5,4},{6,7},{7,6},{8,9},{9,8},{10,11... | collective-permute-start | bytes 1327112 | tf_op jit(solution)/shard_map/ppermute | solution.py:299
  56.8 22.9 %all-to-all-start = ((bf16[16,27,4,128]{3,2,1,0:T(4,128)(2,1)}), bf16[16,27,4,128]{3,2,1,0:T(4,128)(2,1)S(1)}, u32[]{:S(2)}, u32[]{:S(2)}) async-start(bf16[16,27,4,128]{3,2,1,0:T(4,128)(2,1)} %get-tuple-element.27), calls=%async_computation | async-start | bytes 884736 | tf_op jit(solution)/shard_map/all_to_all | solution.py:343
  64.0 6.1 %collective-permute-start.6 = (bf16[4,2,32,128]{3,2,1,0:T(8,128)(2,1)S(1)}, bf16[4,2,32,128]{3,2,1,0:T(8,128)(2,1)S(1)}, u32[]{:S(2)}, u32[]{:S(2)}) collective-permute-start(bf16[4,2,32,128]{3,2,1,0:T(8,128)(2,1)S(1)} %shard_map.72.grad_ref.own_ref), channel_id=1, source_target_pairs={{32,0},{64,32},{96,64},{128,96},{160,128},{192,160},{224,192},{256... | collective-permute-start | bytes 196616 | tf_op jit(solution)/shard_map/ppermute | solution.py:290
  70.1 8.2 %collective-permute-start.8 = (bf16[2,4,32,128]{3,2,1,0:T(8,128)(2,1)S(1)}, bf16[2,4,32,128]{3,2,1,0:T(8,128)(2,1)S(1)}, u32[]{:S(2)}, u32[]{:S(2)}) collective-permute-start(bf16[2,4,32,128]{3,2,1,0:T(8,128)(2,1)S(1)} %shard_map.75), channel_id=1, source_target_pairs={{0,1},{1,2},{2,3},{3,4},{4,5},{5,6},{6,7},{7,8},{8,9},{9,10},{10,1... | collective-permute-start | bytes 196616 | tf_op jit(solution)/shard_map/ppermute | solution.py:296

commit v6 on v5

--- a/solution.py
+++ b/solution.py
@@ -10,6 +10,7 @@
 
 EPS = 1e-06
 TAPS = 27
+SLOTS = 28
 F32 = jnp.float32
 BF16 = jnp.bfloat16
 
@@ -167,9 +168,8 @@
 
 
 def second_backward(
-    own_ref, later_ref, above_ref, kernel_ref, gain_ref, pre_ref, token_ref, grad_ref, store
+    own_ref, later_ref, above_ref, kernel_ref, gain_ref, pre_ref, grad_ref, store
 ):
-    del token_ref
     rows, frames, _, _ = own_ref.shape
     last = at_last_tile()
     seams = {(rows - 2, 2): last, (rows - 1, 0): last}
@@ -192,43 +192,86 @@
     token_ref[...] = grad[: token_ref.shape[0]].astype(F32)
 
 
-def split_gradient(store, seams, grad_ref, keep_ref, send_ref):
-    chips, _, share, channels = keep_ref.shape
+def regrouped(rows, share):
+    channels = rows[0][0].shape[-1]
+    source = lax.broadcasted_iota(jnp.int32, (channels, channels), 0)
+    target = lax.broadcasted_iota(jnp.int32, (channels, channels), 1)
+    core, chip, place = source // share % 2, source // (2 * share), source % share
+    moved = core * (channels // 2) + chip * share + place
+    select = jnp.where(moved == target, 1.0, 0.0).astype(BF16)
+    columns = rows[0][0].shape[0]
+    joined = jnp.concatenate([block for row in rows for block in row], axis=0)
+    joined = jnp.dot(joined, select, preferred_element_type=F32).astype(BF16)
+    frames = len(rows[0])
+    return [
+        [
+            joined[(row * frames + frame) * columns : (row * frames + frame + 1) * columns]
+            for frame in range(frames)
+        ]
+        for row in range(len(rows))
+    ]
+
+
+def split_gradient(store, seams, grad_ref, first_slot, even_ref, odd_ref):
+    chips, _, share, channels = even_ref.shape
     rows, frames, _, _ = grad_ref.shape
-    odd = lax.axis_index("tile") % 2 == 1
+    half = channels // 2
     grad = grad_ref[...].reshape(-1, channels)
+    turned = grad.astype(F32).T.astype(BF16)
+    right = []
     for index in range(9):
-        blocks = lax.dot_general(
-            side_by_side(store, seams, range(rows), frames, 1, index),
-            grad,
-            (((0,), (0,)), ((), ())),
-            preferred_element_type=F32,
-        )
-        for across in range(3):
-            block = blocks[across * channels : (across + 1) * channels]
-            block = block.reshape(chips, 2, share, channels)
-            even_part, odd_part = block[:, 0], block[:, 1]
-            tap = 3 * index + across
-            keep_ref[:, tap] = jnp.where(odd, odd_part, even_part).astype(BF16)
-            send_ref[:, tap] = jnp.where(odd, even_part, odd_part).astype(BF16)
-
-
-def second_kernel_gradient(next_ref, grad_ref, keep_ref, send_ref, token_ref, store):
-    rows = grad_ref.shape[0]
+        cells = side_by_side(store, seams, range(rows), frames, 1, index)
+        left = lax.dot_general(cells, grad, (((0,), (0,)), ((), ())), preferred_element_type=F32)
+        across = jnp.dot(turned, cells, preferred_element_type=F32)
+        for member in range(3):
+            first = member * channels
+            block = left[first : first + half].reshape(chips, share, channels)
+            even_ref[:, first_slot + 3 * index + member] = block.astype(BF16)
+            right.append(across[:, first : first + channels])
+    even_ref[:, first_slot + TAPS] = jnp.zeros((chips, share, channels), BF16)
+    lane = lax.broadcasted_iota(jnp.int32, right[0].shape, 1)
+    for pair in range(SLOTS // 2):
+        block = pltpu.roll(right[pair], half, 1)
+        if pair + SLOTS // 2 < TAPS:
+            upper = right[pair + SLOTS // 2]
+        else:
+            upper = jnp.zeros_like(block)
+        block = jnp.where(lane < half, block, upper).reshape(chips, 2, share, channels)
+        odd_ref[:, first_slot + 2 * pair] = block[:, 0].astype(BF16)
+        odd_ref[:, first_slot + 2 * pair + 1] = block[:, 1].astype(BF16)
+
+
+def second_kernel_gradient(next_ref, grad_ref, even_ref, odd_ref, token_ref, store):
+    rows, share = grad_ref.shape[0], even_ref.shape[2]
     last = at_last_tile()
     seams = {(rows - 3, 2): last, (rows - 2, 0): last}
-    store_columns(store, window_of(block_rows(next_ref)), (0, 1, 2), seams)
-    split_gradient(store, seams, grad_ref, keep_ref, send_ref)
+    window = window_of(regrouped(block_rows(next_ref), share))
+    store_columns(store, window, (0, 1, 2), seams)
+    split_gradient(store, seams, grad_ref, 0, even_ref, odd_ref)
     token_ref[...] = jnp.zeros_like(token_ref)
 
 
-def first_kernel_gradient(own_ref, earlier_ref, below_ref, grad_ref, keep_ref, send_ref, store):
-    rows = grad_ref.shape[0]
+def first_kernel_gradient(
+    own_ref, earlier_ref, below_ref, grad_ref, even_second, odd_second, keep_ref, send_ref, store,
+    even_ref, odd_ref,
+):
+    rows, share = grad_ref.shape[0], keep_ref.shape[2]
     last = at_last_tile()
     seams = {(rows - 2, 2): last, (rows - 1, 0): last}
-    window = window_of(first_rows((earlier_ref, own_ref), below_ref, rows + 2))
-    store_columns(store, window, (0, 1, 2), seams)
-    split_gradient(store, seams, grad_ref, keep_ref, send_ref)
+    blocks = first_rows((earlier_ref, own_ref), below_ref, rows + 2)
+    store_columns(store, window_of(regrouped(blocks, share)), (0, 1, 2), seams)
+    split_gradient(store, seams, grad_ref, 0, even_ref, odd_ref)
+    odd = lax.axis_index("tile") % 2 == 1
+
+    @pl.when(odd)
+    def _():
+        keep_ref[:, :SLOTS], keep_ref[:, SLOTS:] = odd_ref[...], odd_second[...]
+        send_ref[:, :SLOTS], send_ref[:, SLOTS:] = even_ref[...], even_second[...]
+
+    @pl.when(jnp.logical_not(odd))
+    def _():
+        keep_ref[:, :SLOTS], keep_ref[:, SLOTS:] = even_ref[...], even_second[...]
+        send_ref[:, :SLOTS], send_ref[:, SLOTS:] = odd_ref[...], odd_second[...]
 
 
 def pack_rows(own_ref, later_ref, token_ref, out_ref):
@@ -243,31 +286,66 @@
     token_ref[...] = jnp.zeros_like(token_ref)
 
 
-def sum_tiles(first_ref, second_ref, token_ref, out_ref, rows_ref):
+def sum_first(in_ref, token_ref, out_ref, rows_ref):
     del token_ref
-    chips, taps, share, _ = first_ref.shape
-    groups, width, _ = out_ref.shape
+    total = in_ref[0].astype(F32)
+    for source in range(1, in_ref.shape[0]):
+        total = total + in_ref[source].astype(F32)
+    slots, share, channels = total.shape
+    groups, width, lanes = out_ref.shape
     rows_ref[...] = jnp.zeros_like(rows_ref)
-    stride = rows_ref.shape[0] // share
-    for layer, in_ref in enumerate((first_ref, second_ref)):
-        total = in_ref[0].astype(F32)
-        for chip in range(1, chips):
-            total = total + in_ref[chip].astype(F32)
-        for row in range(share):
-            start = row * stride + layer * taps
-            rows_ref[start : start + taps] = total[:, row]
-    out_ref[...] = rows_ref[...].T.reshape(groups, width, -1).astype(BF16)
-
-
-def sum_frames(scale, in_ref, out_ref):
-    groups = in_ref.shape[0]
+    odd = lax.axis_index("tile") % 2 == 1
+
+    @pl.when(jnp.logical_not(odd))
+    def _():
+        stride = lanes // share
+        for place in range(share):
+            rows_ref[place * stride : place * stride + slots] = total[:, place]
+        out_ref[...] = rows_ref[...].T.reshape(groups, width, lanes).astype(BF16)
+
+    @pl.when(odd)
+    def _():
+        stride = lanes // width
+        pairs = total.reshape(slots // 2, 2, share, channels)
+        for channel in range(width):
+            value = pairs[:, channel // share, channel % share]
+            rows_ref[channel * stride : channel * stride + slots // 2] = value
+        turned = rows_ref[...].T.reshape(2, groups, share, lanes).astype(BF16)
+        for upper in range(2):
+            out_ref[:, upper * share : (upper + 1) * share] = turned[upper]
+
+
+def sum_second(scale, in_ref, out_ref):
     total = in_ref[0].astype(F32)
-    for group in range(1, groups):
-        total = total + in_ref[group].astype(F32)
-    share, _, taps = out_ref.shape
-    stride = total.shape[1] // share
-    for row in range(share):
-        out_ref[row] = total[:, row * stride : row * stride + taps] * scale
+    for source in range(1, in_ref.shape[0]):
+        total = total + in_ref[source].astype(F32)
+    total = total * scale
+    lanes = total.shape[1]
+    share, width, _ = out_ref.shape
+    odd = lax.axis_index("tile") % 2 == 1
+
+    @pl.when(jnp.logical_not(odd))
+    def _():
+        stride = lanes // share
+        for place in range(share):
+            for layer in range(2):
+                start = place * stride + layer * SLOTS
+                out_ref[place, :, layer * TAPS : (layer + 1) * TAPS] = total[:, start : start + TAPS]
+
+    @pl.when(odd)
+    def _():
+        stride, pairs = lanes // width, SLOTS // 2
+        for upper in range(2):
+            count = TAPS - pairs if upper else pairs
+            for layer in range(2):
+                first = layer * TAPS + upper * pairs
+                for place in range(share):
+                    row = upper * share + place
+                    for channel in range(width):
+                        start = channel * stride + layer * pairs
+                        out_ref[place, channel : channel + 1, first : first + count] = total[
+                            row : row + 1, start : start + count
+                        ]
 
 
 def shape_of(*dims, dtype=BF16):
@@ -327,7 +405,8 @@
     )
 
     share = channels // tiles
-    part = shape_of(tiles // 2, TAPS, share, channels)
+    part = shape_of(tiles // 2, SLOTS, share, channels)
+    both = shape_of(tiles // 2, 2 * SLOTS, share, channels)
     mark = shape_of(8, channels, dtype=F32)
 
     def with_neighbours(later, grad, token):
@@ -335,22 +414,25 @@
         packed = call(pack_rows, edge, grad, later, token)
         return from_above(packed)
 
-    by_core = [list(range(core, tiles, 2)) for core in range(2)]
-
-    def sent_and_paired(keep, send):
-        came = partner(send)
-        paired, token = call(add_pair, (part, mark), keep, came)
-        arrived = lax.all_to_all(
-            paired, "tile", split_axis=0, concat_axis=0, tiled=True, axis_index_groups=by_core
+    chips = [[f * tiles + t for t in range(0, tiles, 2)] for f in range(groups)]
+    odd_chips = [[f * tiles + t for t in range(1, tiles, 2)] for f in range(groups)]
+    even_frames = [[f * tiles + t for f in range(groups)] for t in range(0, tiles, 2)]
+    odd_frames = [[f * tiles + t for f in range(groups)] for t in range(1, tiles, 2)]
+
+    def exchanged(value, members):
+        return lax.all_to_all(
+            value, ("frame", "tile"), 0, 0, tiled=True, axis_index_groups=members
         )
-        return arrived, token
 
     later_1 = earlier_frames(grad_1)
-    keep_1, send_1, token = call(
-        second_kernel_gradient, (part, part, mark), next_1, grad_1, scratch=column_store(rows + 2, 2 * frames)
+    even_1, odd_1, token = call(
+        second_kernel_gradient,
+        (part, part, mark),
+        next_1,
+        grad_1,
+        scratch=column_store(wide, 2 * frames),
     )
     above_1 = with_neighbours(later_1, grad_1, token)
-    arrived_1, token = sent_and_paired(keep_1, send_1)
     grad_0 = call(
         second_backward,
         grad_shape,
@@ -360,19 +442,22 @@
         kernels[1],
         norm_gains,
         pre_0,
-        token,
         scratch=column_store(rows + 2, 2 * frames),
     )
-    keep_0, send_0 = call(
+    keep, send = call(
         first_kernel_gradient,
-        (part, part),
+        (both, both),
         own_0,
         earlier_0,
         below,
         grad_0,
-        scratch=column_store(rows + 2, 2 * frames),
-    )
-    arrived_0, token = sent_and_paired(keep_0, send_0)
+        even_1,
+        odd_1,
+        scratch=column_store(rows + 2, 2 * frames)
+        + (pltpu.VMEM(part.shape, BF16), pltpu.VMEM(part.shape, BF16)),
+    )
+    paired, token = call(add_pair, (both, mark), keep, partner(send))
+    arrived = exchanged(paired, chips + odd_frames)
     later_0 = earlier_frames(grad_0)
     above_0 = with_neighbours(later_0, grad_0, token)
     input_grad, token = call(
@@ -384,19 +469,18 @@
         kernels[0],
         scratch=column_store(rows + 2, 2 * frames),
     )
-    padded = -(-2 * TAPS // 32) * 32 * share
-    by_frame = call(
-        sum_tiles,
-        shape_of(groups, channels // groups, padded),
-        arrived_0,
-        arrived_1,
+    lanes = share * 64
+    halfway = call(
+        sum_first,
+        shape_of(groups, channels // groups, lanes),
+        arrived,
         token,
-        scratch=(pltpu.VMEM((padded, channels), F32),),
-    )
-    spread = lax.all_to_all(by_frame, "frame", split_axis=0, concat_axis=0, tiled=True)
+        scratch=(pltpu.VMEM((lanes, channels), F32),),
+    )
+    spread = exchanged(halfway, even_frames + odd_chips)
     scale = 1.0 / math.sqrt(cells * tiles * groups)
     summed = call(
-        lambda *refs: sum_frames(scale, *refs),
+        lambda *refs: sum_second(scale, *refs),
         shape_of(share, channels // groups, 2 * TAPS, dtype=F32),
         spread,
     )

time: 112 us -> 105 us (0.938)
  the two profiles are of different devices: /device:TPU:32 before, /device:TPU:2 now
where the time goes in v6:
time: 105 us; the launch traced here: 104 us
  starting transfers between devices  39.5 us (38%)
  blocking collectives  30.6 us (29%)
  waiting for transfers between devices  20.2 us (19%)
  Pallas kernels  9.77 us (9%)
  local copies, waits for them, and re-layouts  2.37 us (2%)
    all_to_all x1, blocking collectives, exchanged(): lax.all_to_all(value, ('frame', 'tile'), 0, 0, tiled=True, axis_index_gro...  30.6 us
    ppermute x2, starting transfers between devices, from_above(): lax.ppermute(value, 'tile', [(i, (i + 1) % tiles) for i in range(tiles)])  13.6 us
    ppermute x2, starting transfers between devices, next_frames(): lax.ppermute(value, 'frame', [(i, i + steps) for i in range(groups - step...  10 us
    pallas_call x10, Pallas kernels, call(): pl.pallas_call(kernel, out_shape=out_shape, scratch_shapes=list(scratch),...  9.77 us
    ppermute x2, waiting for transfers between devices, from_above(): lax.ppermute(value, 'tile', [(i, (i + 1) % tiles) for i in range(tiles)])  7.61 us
    ppermute x2, waiting for transfers between devices, earlier_frames(): return lax.ppermute(value, 'frame', [(i + 1, i) for i in range(groups - 1)])  7.1 us
    ppermute x1, starting transfers between devices, from_below(): lax.ppermute(value, 'tile', [((i + 1) % tiles, i) for i in range(tiles)])  5.62 us
    all_to_all x1, starting transfers between devices, exchanged(): lax.all_to_all(value, ('frame', 'tile'), 0, 0, tiled=True, axis_index_gro...  4.18 us
  transfers between devices with their start and end apart: 9, of which 7 were waited for; matrix products, arithmetic and copies ran while one was open for 2% of the time, Pallas kernels for 2%

profile of v6, /device:TPU:2, one launch (start us, length us, event | category | flops | bytes accessed | tf_op | source)
XLA Modules:
  0.0 104.1 jit_solution(16826541847837618813)
XLA Ops:
  0.6 0.9 multiply_convert_fusion.own_ref
  1.6 3.4 %collective-permute-start = (bf16[2,4,32,128]{3,2,1,0:T(8,128)(2,1)S(1)}, bf16[2,4,32,128]{3,2,1,0:T(8,128)(2,1)S(1)}, u32[]{:S(2)}, u32[]{:S(2)}) collective-permute-start(bf16[2,4,32,128]{3,2,1,0:T(8,128)(2,1)S(1)} %multiply_convert_fusion.own_ref), channel_id=1, source_target_pairs={{0,32},{32,64},{64,96},{96,128},{128,160},{160,192},{192,224},{224... | collective-permute-start | bytes 196616 | tf_op jit(solution)/shard_map/ppermute | solution.py:365
  5.0 6.6 %collective-permute-start.1 = (bf16[2,4,32,128]{3,2,1,0:T(8,128)(2,1)S(1)}, bf16[2,4,32,128]{3,2,1,0:T(8,128)(2,1)S(1)}, u32[]{:S(2)}, u32[]{:S(2)}) collective-permute-start(bf16[2,4,32,128]{3,2,1,0:T(8,128)(2,1)S(1)} %multiply_convert_fusion.own_ref), channel_id=1, source_target_pairs={{0,64},{32,96},{64,128},{96,160},{128,192},{160,224},{192,256},{22... | collective-permute-start | bytes 196616 | tf_op jit(solution)/shard_map/ppermute | solution.py:365
  11.6 0.8 slice.11
  12.4 0.0 collective-permute-done.earlier_ref
  12.4 1.1 %collective-permute-done.1.earliest_ref = bf16[2,4,32,128]{3,2,1,0:T(8,128)(2,1)S(1)} collective-permute-done((bf16[2,4,32,128]{3,2,1,0:T(8,128)(2,1)S(1)}, bf16[2,4,32,128]{3,2,1,0:T(8,128)(2,1)S(1)}, u32[]{:S(2)}, u32[]{:S(2)}) %collective-permute-start.1) | collective-permute-done | bytes 65568 | tf_op jit(solution)/shard_map/ppermute | solution.py:365
  13.5 0.0 copy-start
  13.6 0.0 copy-start.1
  13.6 5.6 %collective-permute-start.2 = (bf16[28,32,128]{2,1,0:T(8,128)(2,1)S(1)}, bf16[28,32,128]{2,1,0:T(8,128)(2,1)S(1)}, u32[]{:S(2)}, u32[]{:S(2)}) collective-permute-start(bf16[28,32,128]{2,1,0:T(8,128)(2,1)S(1)} %pad_maximum_fusion), channel_id=1, source_target_pairs={{1,0},{2,1},{3,2},{4,3},{5,4},{6,5},{7,6},{8,7},{9,8},{10,9},{11,1... | collective-permute-start | bytes 688136 | tf_op jit(solution)/shard_map/ppermute | solution.py:371
  19.2 1.6 %slice_bitcast_fusion = (bf16[27,128,128]{2,1,0:T(8,128)(2,1)S(1)}, bf16[27,128,128]{2,1,0:T(8,128)(2,1)S(1)}) fusion(bf16[2,27,128,128]{3,2,1,0:T(8,128)(2,1)} %param.7), kind=kLoop, calls=%fused_computation | loop fusion | bytes 3538944 | tf_op jit(solution)/shard_map/squeeze | solution.py:402
  20.8 1.9 %collective-permute-done.2.below_ref = bf16[28,32,128]{2,1,0:T(8,128)(2,1)S(1)} collective-permute-done((bf16[28,32,128]{2,1,0:T(8,128)(2,1)S(1)}, bf16[28,32,128]{2,1,0:T(8,128)(2,1)S(1)}, u32[]{:S(2)}, u32[]{:S(2)}) %collective-permute-start.2) | collective-permute-done | bytes 229408 | tf_op jit(solution)/shard_map/ppermute | solution.py:371
  22.7 0.0 copy-done
  22.7 0.0 copy-done.1
  22.7 2.5 %shard_map.68 = (bf16[6,4,32,128]{3,2,1,0:T(8,128)(2,1)S(1)}, f32[256,128]{1,0:T(8,128)S(1)}, bf16[4,2,32,128]{3,2,1,0:T(8,128)(2,1)S(1)}) custom-call(bf16[2,4,32,128]{3,2,1,0:T(8,128)(2,1)S(1)} %multiply_convert_fusion.own_ref, bf16[2,4,32,128]{3,2,1,0:T(8,128)(2,1)S(1)} %collective-permute-done.earlier_ref, ...), custom_call_target="tpu_custom_call" | custom-call | tf_op jit(solution)/shard_map/pallas_call | solution.py:19
  25.3 1.9 %collective-permute-start.3 = (bf16[4,2,32,128]{3,2,1,0:T(8,128)(2,1)S(1)}, bf16[4,2,32,128]{3,2,1,0:T(8,128)(2,1)S(1)}, u32[]{:S(2)}, u32[]{:S(2)}) collective-permute-start(bf16[4,2,32,128]{3,2,1,0:T(8,128)(2,1)S(1)} %get-tuple-element.14.grad_ref.own_ref), channel_id=1, source_target_pairs={{32,0},{64,32},{96,64},{128,96},{160,128},{192,160},{224,192},{256... | collective-permute-start | bytes 196616 | tf_op jit(solution)/shard_map/ppermute | solution.py:368
  27.2 1.2 %shard_map.69 = (bf16[16,28,4,128]{3,2,1,0:T(4,128)(2,1)S(1)}, bf16[16,28,4,128]{3,2,1,0:T(4,128)(2,1)S(1)}, f32[8,128]{1,0:T(8,128)S(1)}) custom-call(bf16[6,4,32,128]{3,2,1,0:T(8,128)(2,1)S(1)} %get-tuple-element.15.next_ref, bf16[4,2,32,128]{3,2,1,0:T(8,128)(2,1)S(1)} %get-tuple-element.14.grad_ref.own_ref), custom_call_target="tpu_custom_call" | custom-call | tf_op jit(solution)/shard_map/pallas_call | solution.py:19
  28.4 3.0 %collective-permute-done.3.later_ref = bf16[4,2,32,128]{3,2,1,0:T(8,128)(2,1)S(1)} collective-permute-done((bf16[4,2,32,128]{3,2,1,0:T(8,128)(2,1)S(1)}, bf16[4,2,32,128]{3,2,1,0:T(8,128)(2,1)S(1)}, u32[]{:S(2)}, u32[]{:S(2)}) %collective-permute-start.3) | collective-permute-done | bytes 65568 | tf_op jit(solution)/shard_map/ppermute | solution.py:368
  31.4 1.9 %collective-permute-start.4 = (bf16[2,4,32,128]{3,2,1,0:T(8,128)(2,1)S(1)}, bf16[2,4,32,128]{3,2,1,0:T(8,128)(2,1)S(1)}, u32[]{:S(2)}, u32[]{:S(2)}) collective-permute-start(bf16[2,4,32,128]{3,2,1,0:T(8,128)(2,1)S(1)} %shard_map.70), channel_id=1, source_target_pairs={{0,1},{1,2},{2,3},{3,4},{4,5},{5,6},{6,7},{7,8},{8,9},{9,10},{10,1... | collective-permute-start | bytes 196616 | tf_op jit(solution)/shard_map/ppermute | solution.py:374
  33.4 5.8 %collective-permute-done.4.above_ref = bf16[2,4,32,128]{3,2,1,0:T(8,128)(2,1)S(1)} collective-permute-done((bf16[2,4,32,128]{3,2,1,0:T(8,128)(2,1)S(1)}, bf16[2,4,32,128]{3,2,1,0:T(8,128)(2,1)S(1)}, u32[]{:S(2)}, u32[]{:S(2)}) %collective-permute-start.4) | collective-permute-done | bytes 65568 | tf_op jit(solution)/shard_map/ppermute | solution.py:374
  39.1 0.8 shard_map.71.grad_ref.own_ref
  39.9 1.3 %shard_map.72 = (bf16[16,56,4,128]{3,2,1,0:T(4,128)(2,1)S(1)}, bf16[16,56,4,128]{3,2,1,0:T(4,128)(2,1)S(1)}) custom-call(bf16[2,4,32,128]{3,2,1,0:T(8,128)(2,1)S(1)} %multiply_convert_fusion.own_ref, bf16[2,4,32,128]{3,2,1,0:T(8,128)(2,1)S(1)} %collective-permute-done.earlier_ref, bf16[28,32,128]{2,1,0:T(8,128)(2,1)S(1)} %collective-permute-done.2.below_ref, ...), custom_call_target="tpu_custom_call" | custom-call | tf_op jit(solution)/shard_map/pallas_call | solution.py:19
  41.2 1.9 %collective-permute-start.6 = (bf16[16,56,4,128]{3,2,1,0:T(4,128)(2,1)S(1)}, bf16[16,56,4,128]{3,2,1,0:T(4,128)(2,1)S(1)}, u32[]{:S(2)}, u32[]{:S(2)}) collective-permute-start(bf16[16,56,4,128]{3,2,1,0:T(4,128)(2,1)S(1)} %get-tuple-element.21), channel_id=1, source_target_pairs={{0,1},{1,0},{2,3},{3,2},{4,5},{5,4},{6,7},{7,6},{8,9},{9,8},{10,11... | collective-permute-start | bytes 2752520 | tf_op jit(solution)/shard_map/ppermute | solution.py:377
  43.1 2.4 %collective-permute-done.6.came_ref = bf16[16,56,4,128]{3,2,1,0:T(4,128)(2,1)S(1)} collective-permute-done((bf16[16,56,4,128]{3,2,1,0:T(4,128)(2,1)S(1)}, bf16[16,56,4,128]{3,2,1,0:T(4,128)(2,1)S(1)}, u32[]{:S(2)}, u32[]{:S(2)}) %collective-permute-start.6) | collective-permute-done | bytes 917536 | tf_op jit(solution)/shard_map/ppermute | solution.py:377
  45.6 1.4 %shard_map.73 = (bf16[16,56,4,128]{3,2,1,0:T(4,128)(2,1)}, f32[8,128]{1,0:T(8,128)S(1)}) custom-call(bf16[16,56,4,128]{3,2,1,0:T(4,128)(2,1)S(1)} %get-tuple-element.20.keep_ref, bf16[16,56,4,128]{3,2,1,0:T(4,128)(2,1)S(1)} %collective-permute-done.6.came_ref), custom_call_target="tpu_custom_call" | custom-call | tf_op jit(solution)/shard_map/pallas_call | solution.py:19
  47.0 4.2 %all-to-all-start = ((bf16[16,56,4,128]{3,2,1,0:T(4,128)(2,1)}), bf16[16,56,4,128]{3,2,1,0:T(4,128)(2,1)S(1)}, u32[]{:S(2)}, u32[]{:S(2)}) async-start(bf16[16,56,4,128]{3,2,1,0:T(4,128)(2,1)} %get-tuple-element.24), calls=%async_computation | async-start | bytes 1835008 | tf_op jit(solution)/shard_map/all_to_all | solution.py:423
  51.2 2.2 %collective-permute-start.5 = (bf16[4,2,32,128]{3,2,1,0:T(8,128)(2,1)S(1)}, bf16[4,2,32,128]{3,2,1,0:T(8,128)(2,1)S(1)}, u32[]{:S(2)}, u32[]{:S(2)}) collective-permute-start(bf16[4,2,32,128]{3,2,1,0:T(8,128)(2,1)S(1)} %shard_map.71.grad_ref.own_ref), channel_id=1, source_target_pairs={{32,0},{64,32},{96,64},{128,96},{160,128},{192,160},{224,192},{256... | collective-permute-start | bytes 196616 | tf_op jit(solution)/shard_map/ppermute | solution.py:368
  53.4 4.1 %collective-permute-done.5.later_ref = bf16[4,2,32,128]{3,2,1,0:T(8,128)(2,1)S(1)} collective-permute-done((bf16[4,2,32,128]{3,2,1,0:T(8,128)(2,1)S(1)}, bf16[4,2,32,128]{3,2,1,0:T(8,128)(2,1)S(1)}, u32[]{:S(2)}, u32[]{:S(2)}) %collective-permute-start.5) | collective-permute-done | bytes 65568 | tf_op jit(solution)/shard_map/ppermute | solution.py:368
  57.4 11.7 %collective-permute-start.7 = (bf16[2,4,32,128]{3,2,1,0:T(8,128)(2,1)S(1)}, bf16[2,4,32,128]{3,2,1,0:T(8,128)(2,1)S(1)}, u32[]{:S(2)}, u32[]{:S(2)}) collective-permute-start(bf16[2,4,32,128]{3,2,1,0:T(8,128)(2,1)S(1)} %shard_map.74), channel_id=1, source_target_pairs={{0,1},{1,2},{2,3},{3,4},{4,5},{5,6},{6,7},{7,8},{8,9},{9,10},{10,1... | collective-permute-start | bytes 196616 | tf_op jit(solution)/shard_map/ppermute | solution.py:374
  69.1 1.8 %collective-permute-done.7.above_ref = bf16[2,4,32,128]{3,2,1,0:T(8,128)(2,1)S(1)} collective-permute-done((bf16[2,4,32,128]{3,2,1,0:T(8,128)(2,1)S(1)}, bf16[2,4,32,128]{3,2,1,0:T(8,128)(2,1)S(1)}, u32[]{:S(2)}, u32[]{:S(2)}) %collective-permute-start.7) | collective-permute-done | bytes 65568 | tf_op jit(solution)/shard_map/ppermute | solution.py:374
  71.0 1.3 %shard_map.75 = (bf16[2,4,32,128]{3,2,1,0:T(8,128)(2,1)}, f32[8,128]{1,0:T(8,128)S(1)}) custom-call(bf16[4,2,32,128]{3,2,1,0:T(8,128)(2,1)S(1)} %shard_map.71.grad_ref.own_ref, bf16[4,2,32,128]{3,2,1,0:T(8,128)(2,1)S(1)} %collective-permute-done.5.later_ref, bf16[2,4,32,128]{3,2,1,0:T(8,128)(2,1)S(1)} %collective-permute-done.7.above_ref, ...), custom_call_target="tpu_custom_call" | custom-call | tf_op jit(solution)/shard_map/pallas_call | solution.py:19
  72.3 0.0 all-to-all-done.in_ref
  72.3 0.6 shard_map.76
  72.8 30.6 %all_to_all.10.refs_0_ = bf16[16,8,256]{2,1,0:T(8,128)(2,1)S(1)} all-to-all(bf16[16,8,256]{2,1,0:T(8,128)(2,1)S(1)} %shard_map.76), channel_id=1, replica_groups={{0,32,64,96,128,160,192,224,256,288,320,352,384,416,448,480},{2,34,66,9..., dimensions={0} | all-to-all | bytes 131072 | tf_op jit(solution)/shard_map/all_to_all | solution.py:423
  103.4 0.7 shard_map.77
  (3 shorter events, 0.0 us)
Async XLA Ops:
  1.6 10.8 %collective-permute-start = (bf16[2,4,32,128]{3,2,1,0:T(8,128)(2,1)S(1)}, bf16[2,4,32,128]{3,2,1,0:T(8,128)(2,1)S(1)}, u32[]{:S(2)}, u32[]{:S(2)}) collective-permute-start(bf16[2,4,32,128]{3,2,1,0:T(8,128)(2,1)S(1)} %multiply_convert_fusion.own_ref), channel_id=1, source_target_pairs={{0,32},{32,64},{64,96},{96,128},{128,160},{160,192},{192,224},{224... | collective-permute-start | bytes 196616 | tf_op jit(solution)/shard_map/ppermute | solution.py:365
  5.0 8.5 %collective-permute-start.1 = (bf16[2,4,32,128]{3,2,1,0:T(8,128)(2,1)S(1)}, bf16[2,4,32,128]{3,2,1,0:T(8,128)(2,1)S(1)}, u32[]{:S(2)}, u32[]{:S(2)}) collective-permute-start(bf16[2,4,32,128]{3,2,1,0:T(8,128)(2,1)S(1)} %multiply_convert_fusion.own_ref), channel_id=1, source_target_pairs={{0,64},{32,96},{64,128},{96,160},{128,192},{160,224},{192,256},{22... | collective-permute-start | bytes 196616 | tf_op jit(solution)/shard_map/ppermute | solution.py:365
  13.5 9.2 %copy-start = (bf16[2,4,32,128]{3,2,1,0:T(8,128)(2,1)S(1)}, bf16[2,4,32,128]{3,2,1,0:T(8,128)(2,1)}, u32[]{:S(2)}) copy-start(bf16[2,4,32,128]{3,2,1,0:T(8,128)(2,1)} %top_ref.1) | copy-start | bytes 196612
  13.6 9.2 %copy-start.1 = (f32[2,128]{1,0:T(2,128)S(1)}, f32[2,128]{1,0:T(2,128)}, u32[]{:S(2)}) copy-start(f32[2,128]{1,0:T(2,128)} %gain_ref.3) | copy-start | bytes 3076
  13.6 9.1 %collective-permute-start.2 = (bf16[28,32,128]{2,1,0:T(8,128)(2,1)S(1)}, bf16[28,32,128]{2,1,0:T(8,128)(2,1)S(1)}, u32[]{:S(2)}, u32[]{:S(2)}) collective-permute-start(bf16[28,32,128]{2,1,0:T(8,128)(2,1)S(1)} %pad_maximum_fusion), channel_id=1, source_target_pairs={{1,0},{2,1},{3,2},{4,3},{5,4},{6,5},{7,6},{8,7},{9,8},{10,9},{11,1... | collective-permute-start | bytes 688136 | tf_op jit(solution)/shard_map/ppermute | solution.py:371
  25.3 6.2 %collective-permute-start.3 = (bf16[4,2,32,128]{3,2,1,0:T(8,128)(2,1)S(1)}, bf16[4,2,32,128]{3,2,1,0:T(8,128)(2,1)S(1)}, u32[]{:S(2)}, u32[]{:S(2)}) collective-permute-start(bf16[4,2,32,128]{3,2,1,0:T(8,128)(2,1)S(1)} %get-tuple-element.14.grad_ref.own_ref), channel_id=1, source_target_pairs={{32,0},{64,32},{96,64},{128,96},{160,128},{192,160},{224,192},{256... | collective-permute-start | bytes 196616 | tf_op jit(solution)/shard_map/ppermute | solution.py:368
  31.4 7.7 %collective-permute-start.4 = (bf16[2,4,32,128]{3,2,1,0:T(8,128)(2,1)S(1)}, bf16[2,4,32,128]{3,2,1,0:T(8,128)(2,1)S(1)}, u32[]{:S(2)}, u32[]{:S(2)}) collective-permute-start(bf16[2,4,32,128]{3,2,1,0:T(8,128)(2,1)S(1)} %shard_map.70), channel_id=1, source_target_pairs={{0,1},{1,2},{2,3},{3,4},{4,5},{5,6},{6,7},{7,8},{8,9},{9,10},{10,1... | collective-permute-start | bytes 196616 | tf_op jit(solution)/shard_map/ppermute | solution.py:374
  41.2 4.4 %collective-permute-start.6 = (bf16[16,56,4,128]{3,2,1,0:T(4,128)(2,1)S(1)}, bf16[16,56,4,128]{3,2,1,0:T(4,128)(2,1)S(1)}, u32[]{:S(2)}, u32[]{:S(2)}) collective-permute-start(bf16[16,56,4,128]{3,2,1,0:T(4,128)(2,1)S(1)} %get-tuple-element.21), channel_id=1, source_target_pairs={{0,1},{1,0},{2,3},{3,2},{4,5},{5,4},{6,7},{7,6},{8,9},{9,8},{10,11... | collective-permute-start | bytes 2752520 | tf_op jit(solution)/shard_map/ppermute | solution.py:377
  47.0 25.3 %all-to-all-start = ((bf16[16,56,4,128]{3,2,1,0:T(4,128)(2,1)}), bf16[16,56,4,128]{3,2,1,0:T(4,128)(2,1)S(1)}, u32[]{:S(2)}, u32[]{:S(2)}) async-start(bf16[16,56,4,128]{3,2,1,0:T(4,128)(2,1)} %get-tuple-element.24), calls=%async_computation | async-start | bytes 1835008 | tf_op jit(solution)/shard_map/all_to_all | solution.py:423
  51.2 6.3 %collective-permute-start.5 = (bf16[4,2,32,128]{3,2,1,0:T(8,128)(2,1)S(1)}, bf16[4,2,32,128]{3,2,1,0:T(8,128)(2,1)S(1)}, u32[]{:S(2)}, u32[]{:S(2)}) collective-permute-start(bf16[4,2,32,128]{3,2,1,0:T(8,128)(2,1)S(1)} %shard_map.71.grad_ref.own_ref), channel_id=1, source_target_pairs={{32,0},{64,32},{96,64},{128,96},{160,128},{192,160},{224,192},{256... | collective-permute-start | bytes 196616 | tf_op jit(solution)/shard_map/ppermute | solution.py:368
  57.4 13.5 %collective-permute-start.7 = (bf16[2,4,32,128]{3,2,1,0:T(8,128)(2,1)S(1)}, bf16[2,4,32,128]{3,2,1,0:T(8,128)(2,1)S(1)}, u32[]{:S(2)}, u32[]{:S(2)}) collective-permute-start(bf16[2,4,32,128]{3,2,1,0:T(8,128)(2,1)S(1)} %shard_map.74), channel_id=1, source_target_pairs={{0,1},{1,2},{2,3},{3,4},{4,5},{5,6},{6,7},{7,8},{8,9},{9,10},{10,1... | collective-permute-start | bytes 196616 | tf_op jit(solution)/shard_map/ppermute | solution.py:374

commit v7 on v5

--- a/solution.py
+++ b/solution.py
@@ -100,30 +100,28 @@
     return lax.axis_index("tile") == lax.axis_size("tile") - 1
 
 
-def first_rows(parts, below_ref, total):
+def first_rows(parts, below_parts, total):
     frames, rows = parts[0].shape[:2]
-    skipped = (3 - len(parts)) * frames
     result = []
     for row in range(total):
-        if row < rows:
-            result.append([part[frame, row] for part in parts for frame in range(frames)])
-        else:
-            result.append(
-                [
-                    below_ref[(skipped + frame) * rows + row - rows]
-                    for frame in range(len(parts) * frames)
-                ]
-            )
+        source, place = (parts, row) if row < rows else (below_parts, row - rows)
+        result.append([part[frame, place] for part in source for frame in range(frames)])
     return result
 
 
 def forward(
-    own_ref, earlier_ref, earliest_ref, below_ref, top_ref, first_kernel_ref, second_kernel_ref,
-    gain_ref, next_ref, pre_ref, grad_ref, wide_store, store,
+    own_ref, earlier_ref, earliest_ref, below_ref, below_earlier_ref, below_earliest_ref, top_ref,
+    first_kernel_ref, second_kernel_ref, gain_ref, next_ref, pre_ref, grad_ref, wide_store, store,
 ):
     frames, rows, columns, _ = own_ref.shape
     last = at_last_tile()
-    window = window_of(first_rows((earliest_ref, earlier_ref, own_ref), below_ref, 2 * rows))
+    window = window_of(
+        first_rows(
+            (earliest_ref, earlier_ref, own_ref),
+            (below_earliest_ref, below_earlier_ref, below_ref),
+            2 * rows,
+        )
+    )
     wide, deep = 2 * rows - 2, 2 * frames
     seams = {(rows - 2, 2): last, (rows - 1, 0): last}
     store_columns(wide_store, window, (0, 1, 2), seams)
@@ -148,41 +146,36 @@
             if row < rows - 2:
                 spread.append(top_ref[frame, row + 2])
             else:
-                spread.append(below_ref[3 * frames * rows + frame * 2 + row - rows + 2])
+                spread.append(below_ref[frame, row + 2])
     upstream = jnp.concatenate(spread, axis=0).astype(F32)
     grad_ref[...] = pre_norm_gradient(pre_norm, gain_ref[1:2], upstream).reshape(grad_ref.shape)
 
 
-def backward_rows(own_ref, later_ref, above_ref, frames):
-    rows = own_ref.shape[0]
-    result = []
-    for row in range(2):
-        result.append([above_ref[row, frame] for frame in range(2 * frames)])
-    for row in range(rows):
-        result.append(
-            [own_ref[row, frame] for frame in range(frames)]
-            + [later_ref[row, frame] for frame in range(frames)]
-        )
-    return result
+def backward_rows(own_ref, later_ref, above_ref, corner_ref):
+    window = []
+    for near_ref, far_ref in ((above_ref, corner_ref), (own_ref, later_ref)):
+        window += [near + far for near, far in zip(block_rows(near_ref), block_rows(far_ref))]
+    return window
 
 
 def second_backward(
-    own_ref, later_ref, above_ref, kernel_ref, gain_ref, pre_ref, token_ref, grad_ref, store
+    own_ref, later_ref, above_ref, corner_ref, kernel_ref, gain_ref, pre_ref, grad_ref, store
 ):
-    del token_ref
     rows, frames, _, _ = own_ref.shape
     last = at_last_tile()
     seams = {(rows - 2, 2): last, (rows - 1, 0): last}
-    window = window_of(backward_rows(own_ref, later_ref, above_ref, frames))
+    window = window_of(backward_rows(own_ref, later_ref, above_ref, corner_ref))
     store_columns(store, window, (2, 1, 0), seams)
     upstream = product(store, seams, range(rows), frames, -1, kernel_ref).astype(BF16).astype(F32)
     grad_ref[...] = pre_norm_gradient(pre_ref[...], gain_ref[0:1], upstream).reshape(grad_ref.shape)
 
 
-def first_backward(own_ref, later_ref, above_ref, kernel_ref, out_ref, token_ref, store):
+def first_backward(
+    own_ref, later_ref, above_ref, corner_ref, kernel_ref, out_ref, token_ref, store
+):
     rows, frames, columns, _ = own_ref.shape
     seams = {(0, 0): lax.axis_index("tile") == 0, (rows - 1, 2): at_last_tile()}
-    window = window_of(backward_rows(own_ref, later_ref, above_ref, frames))
+    window = window_of(backward_rows(own_ref, later_ref, above_ref, corner_ref))
     store_columns(store, window, (2, 1, 0), seams)
     grad = product(store, seams, range(rows), frames, -1, kernel_ref).astype(BF16)
     for row in range(rows):
@@ -213,61 +206,55 @@
             send_ref[:, tap] = jnp.where(odd, even_part, odd_part).astype(BF16)
 
 
-def second_kernel_gradient(next_ref, grad_ref, keep_ref, send_ref, token_ref, store):
+def second_kernel_gradient(next_ref, grad_ref, keep_ref, send_ref, store):
     rows = grad_ref.shape[0]
     last = at_last_tile()
     seams = {(rows - 3, 2): last, (rows - 2, 0): last}
     store_columns(store, window_of(block_rows(next_ref)), (0, 1, 2), seams)
     split_gradient(store, seams, grad_ref, keep_ref, send_ref)
-    token_ref[...] = jnp.zeros_like(token_ref)
-
-
-def first_kernel_gradient(own_ref, earlier_ref, below_ref, grad_ref, keep_ref, send_ref, store):
+
+
+def first_kernel_gradient(
+    own_ref, earlier_ref, below_ref, below_earlier_ref, grad_ref, keep_second, send_second,
+    keep_ref, send_ref, store,
+):
     rows = grad_ref.shape[0]
     last = at_last_tile()
     seams = {(rows - 2, 2): last, (rows - 1, 0): last}
-    window = window_of(first_rows((earlier_ref, own_ref), below_ref, rows + 2))
+    window = window_of(
+        first_rows((earlier_ref, own_ref), (below_earlier_ref, below_ref), rows + 2)
+    )
     store_columns(store, window, (0, 1, 2), seams)
+    keep_ref[:, TAPS:], send_ref[:, TAPS:] = keep_second[...], send_second[...]
     split_gradient(store, seams, grad_ref, keep_ref, send_ref)
 
 
-def pack_rows(own_ref, later_ref, token_ref, out_ref):
+def add_pair(keep_ref, came_ref, out_ref):
+    out_ref[...] = (keep_ref[...].astype(F32) + came_ref[...].astype(F32)).astype(BF16)
+
+
+def sum_tiles(in_ref, token_ref, out_ref, rows_ref):
     del token_ref
-    frames, first = own_ref.shape[1], own_ref.shape[0] - out_ref.shape[0]
-    out_ref[:, :frames] = own_ref[first:]
-    out_ref[:, frames:] = later_ref[first:]
-
-
-def add_pair(keep_ref, came_ref, out_ref, token_ref):
-    out_ref[...] = (keep_ref[...].astype(F32) + came_ref[...].astype(F32)).astype(BF16)
-    token_ref[...] = jnp.zeros_like(token_ref)
-
-
-def sum_tiles(first_ref, second_ref, token_ref, out_ref, rows_ref):
-    del token_ref
-    chips, taps, share, _ = first_ref.shape
-    groups, width, _ = out_ref.shape
+    total = in_ref[0].astype(F32)
+    for chip in range(1, in_ref.shape[0]):
+        total = total + in_ref[chip].astype(F32)
+    taps, share, _ = total.shape
+    groups, width, lanes = out_ref.shape
+    stride = lanes // share
     rows_ref[...] = jnp.zeros_like(rows_ref)
-    stride = rows_ref.shape[0] // share
-    for layer, in_ref in enumerate((first_ref, second_ref)):
-        total = in_ref[0].astype(F32)
-        for chip in range(1, chips):
-            total = total + in_ref[chip].astype(F32)
-        for row in range(share):
-            start = row * stride + layer * taps
-            rows_ref[start : start + taps] = total[:, row]
-    out_ref[...] = rows_ref[...].T.reshape(groups, width, -1).astype(BF16)
+    for place in range(share):
+        rows_ref[place * stride : place * stride + taps] = total[:, place]
+    out_ref[...] = rows_ref[...].T.reshape(groups, width, lanes).astype(BF16)
 
 
 def sum_frames(scale, in_ref, out_ref):
-    groups = in_ref.shape[0]
     total = in_ref[0].astype(F32)
-    for group in range(1, groups):
+    for group in range(1, in_ref.shape[0]):
         total = total + in_ref[group].astype(F32)
     share, _, taps = out_ref.shape
     stride = total.shape[1] // share
-    for row in range(share):
-        out_ref[row] = total[:, row * stride : row * stride + taps] * scale
+    for place in range(share):
+        out_ref[place] = total[:, place * stride : place * stride + taps] * scale
 
 
 def shape_of(*dims, dtype=BF16):
@@ -283,33 +270,19 @@
     def column_store(window_rows, window_frames):
         return (pltpu.VMEM((window_rows + 2, window_frames, columns, 3 * channels), BF16),)
 
-    def next_frames(value, steps):
-        return lax.ppermute(value, "frame", [(i, i + steps) for i in range(groups - steps)])
-
-    def earlier_frames(value):
-        return lax.ppermute(value, "frame", [(i + 1, i) for i in range(groups - 1)])
-
-    def from_below(value):
-        return lax.ppermute(value, "tile", [((i + 1) % tiles, i) for i in range(tiles)])
-
-    def from_above(value):
-        return lax.ppermute(value, "tile", [(i, (i + 1) % tiles) for i in range(tiles)])
-
-    def partner(value):
-        return lax.ppermute(value, "tile", [(i, i ^ 1) for i in range(tiles)])
+    def moved(value, frame_steps, tile_steps):
+        pairs = [
+            (f * tiles + t, (f + frame_steps) * tiles + (t + tile_steps) % tiles)
+            for f in range(groups)
+            for t in range(tiles)
+            if 0 <= f + frame_steps < groups
+        ]
+        return lax.ppermute(value, ("frame", "tile"), pairs)
 
     own_0 = (saved_codes.astype(F32) * saved_scales[..., None]).astype(BF16)
-    earlier_0, earliest_0 = next_frames(own_0, 1), next_frames(own_0, 2)
-    sent = jnp.concatenate(
-        [
-            earliest_0.reshape(frames * rows, *block),
-            earlier_0.reshape(frames * rows, *block),
-            own_0.reshape(frames * rows, *block),
-            cotangent[:, :2].reshape(frames * 2, *block),
-        ],
-        axis=0,
-    )
-    below = from_below(sent)
+    earliest_0, below_earliest = moved(own_0, 2, 0), moved(own_0, 2, -1)
+    earlier_0, below_earlier = moved(own_0, 1, 0), moved(own_0, 1, -1)
+    below = moved(jnp.concatenate([own_0, cotangent[:, :2]], axis=1), 0, -1)
     wide = 2 * rows - 2
     grad_shape = shape_of(rows, frames, *block)
     next_1, pre_0, grad_1 = call(
@@ -319,6 +292,8 @@
         earlier_0,
         earliest_0,
         below,
+        below_earlier,
+        below_earliest,
         cotangent,
         kernels[0],
         kernels[1],
@@ -326,74 +301,69 @@
         scratch=column_store(2 * rows, 3 * frames) + column_store(wide, 2 * frames),
     )
 
+    def neighbours(grad):
+        edge = grad[rows - 2 :]
+        later = moved(grad, -1, 0)
+        corner = moved(edge, -1, 1)
+        above = moved(edge, 0, 1)
+        return later, above, corner
+
     share = channels // tiles
     part = shape_of(tiles // 2, TAPS, share, channels)
+    both = shape_of(tiles // 2, 2 * TAPS, share, channels)
     mark = shape_of(8, channels, dtype=F32)
-
-    def with_neighbours(later, grad, token):
-        edge = shape_of(2, 2 * frames, *block)
-        packed = call(pack_rows, edge, grad, later, token)
-        return from_above(packed)
-
-    by_core = [list(range(core, tiles, 2)) for core in range(2)]
-
-    def sent_and_paired(keep, send):
-        came = partner(send)
-        paired, token = call(add_pair, (part, mark), keep, came)
-        arrived = lax.all_to_all(
-            paired, "tile", split_axis=0, concat_axis=0, tiled=True, axis_index_groups=by_core
-        )
-        return arrived, token
-
-    later_1 = earlier_frames(grad_1)
-    keep_1, send_1, token = call(
-        second_kernel_gradient, (part, part, mark), next_1, grad_1, scratch=column_store(rows + 2, 2 * frames)
-    )
-    above_1 = with_neighbours(later_1, grad_1, token)
-    arrived_1, token = sent_and_paired(keep_1, send_1)
+    next_to = neighbours(grad_1)
+    keep_1, send_1 = call(
+        second_kernel_gradient,
+        (part, part),
+        next_1,
+        grad_1,
+        scratch=column_store(wide, 2 * frames),
+    )
     grad_0 = call(
         second_backward,
         grad_shape,
         grad_1,
-        later_1,
-        above_1,
+        *next_to,
         kernels[1],
         norm_gains,
         pre_0,
-        token,
         scratch=column_store(rows + 2, 2 * frames),
     )
-    keep_0, send_0 = call(
+    keep, send = call(
         first_kernel_gradient,
-        (part, part),
+        (both, both),
         own_0,
         earlier_0,
         below,
+        below_earlier,
         grad_0,
+        keep_1,
+        send_1,
         scratch=column_store(rows + 2, 2 * frames),
     )
-    arrived_0, token = sent_and_paired(keep_0, send_0)
-    later_0 = earlier_frames(grad_0)
-    above_0 = with_neighbours(later_0, grad_0, token)
+    came = lax.ppermute(send, "tile", [(i, i ^ 1) for i in range(tiles)])
+    paired = call(add_pair, both, keep, came)
+    by_core = [list(range(core, tiles, 2)) for core in range(2)]
+    arrived = lax.all_to_all(paired, "tile", 0, 0, tiled=True, axis_index_groups=by_core)
+    next_to = neighbours(grad_0)
     input_grad, token = call(
         first_backward,
         (shape_of(frames, rows, *block), mark),
         grad_0,
-        later_0,
-        above_0,
+        *next_to,
         kernels[0],
         scratch=column_store(rows + 2, 2 * frames),
     )
-    padded = -(-2 * TAPS // 32) * 32 * share
+    lanes = 64 * share
     by_frame = call(
         sum_tiles,
-        shape_of(groups, channels // groups, padded),
-        arrived_0,
-        arrived_1,
+        shape_of(groups, channels // groups, lanes),
+        arrived,
         token,
-        scratch=(pltpu.VMEM((padded, channels), F32),),
-    )
-    spread = lax.all_to_all(by_frame, "frame", split_axis=0, concat_axis=0, tiled=True)
+        scratch=(pltpu.VMEM((lanes, channels), F32),),
+    )
+    spread = lax.all_to_all(by_frame, "frame", 0, 0, tiled=True)
     scale = 1.0 / math.sqrt(cells * tiles * groups)
     summed = call(
         lambda *refs: sum_frames(scale, *refs),

time: 112 us -> 106 us (0.946)
  the two profiles are of different devices: /device:TPU:32 before, /device:TPU:2 now
where the time goes in v7:
time: 106 us; the launch traced here: 105 us
  starting transfers between devices  43.9 us (41%)
  waiting for transfers between devices  25.5 us (24%)
  blocking collectives  22.7 us (21%)
  Pallas kernels  8.63 us (8%)
  local copies, waits for them, and re-layouts  2.38 us (2%)
    ppermute x11, starting transfers between devices, moved(): return lax.ppermute(value, ('frame', 'tile'), pairs)  37.8 us
    all_to_all x1, blocking collectives, local(): spread = lax.all_to_all(by_frame, 'frame', 0, 0, tiled=True)  22.7 us
    ppermute x11, waiting for transfers between devices, moved(): return lax.ppermute(value, ('frame', 'tile'), pairs)  22.3 us
    pallas_call x8, Pallas kernels, call(): pl.pallas_call(kernel, out_shape=out_shape, scratch_shapes=list(scratch),...  8.63 us
    all_to_all x1, starting transfers between devices, local(): lax.all_to_all(paired, 'tile', 0, 0, tiled=True, axis_index_groups=by_core)  4.18 us
    ppermute x1, waiting for transfers between devices, local(): came = lax.ppermute(send, 'tile', [(i, i ^ 1) for i in range(tiles)])  2.39 us
  transfers between devices with their start and end apart: 13, of which 6 were waited for; matrix products, arithmetic and copies ran while one was open for 2% of the time, Pallas kernels for 2%

profile of v7, /device:TPU:2, one launch (start us, length us, event | category | flops | bytes accessed | tf_op | source)
XLA Modules:
  0.0 104.9 jit_solution(15270355667080424990)
XLA Ops:
  0.6 0.9 multiply_convert_fusion.own_ref
  1.6 8.2 %collective-permute-start.4 = (bf16[2,4,32,128]{3,2,1,0:T(8,128)(2,1)S(1)}, bf16[2,4,32,128]{3,2,1,0:T(8,128)(2,1)S(1)}, u32[]{:S(2)}, u32[]{:S(2)}) collective-permute-start(bf16[2,4,32,128]{3,2,1,0:T(8,128)(2,1)S(1)} %multiply_convert_fusion.own_ref), channel_id=1, source_target_pairs={{0,95},{1,64},{2,65},{3,66},{4,67},{5,68},{6,69},{7,70},{8,71},{9,... | collective-permute-start | bytes 196616 | tf_op jit(solution)/shard_map/ppermute | solution.py:280
  9.8 5.7 %collective-permute-start.3 = (bf16[2,4,32,128]{3,2,1,0:T(8,128)(2,1)S(1)}, bf16[2,4,32,128]{3,2,1,0:T(8,128)(2,1)S(1)}, u32[]{:S(2)}, u32[]{:S(2)}) collective-permute-start(bf16[2,4,32,128]{3,2,1,0:T(8,128)(2,1)S(1)} %multiply_convert_fusion.own_ref), channel_id=1, source_target_pairs={{0,63},{1,32},{2,33},{3,34},{4,35},{5,36},{6,37},{7,38},{8,39},{9,... | collective-permute-start | bytes 196616 | tf_op jit(solution)/shard_map/ppermute | solution.py:280
  15.5 5.5 %collective-permute-start.1 = (bf16[2,4,32,128]{3,2,1,0:T(8,128)(2,1)S(1)}, bf16[2,4,32,128]{3,2,1,0:T(8,128)(2,1)S(1)}, u32[]{:S(2)}, u32[]{:S(2)}) collective-permute-start(bf16[2,4,32,128]{3,2,1,0:T(8,128)(2,1)S(1)} %multiply_convert_fusion.own_ref), channel_id=1, source_target_pairs={{0,64},{1,65},{2,66},{3,67},{4,68},{5,69},{6,70},{7,71},{8,72},{9,... | collective-permute-start | bytes 196616 | tf_op jit(solution)/shard_map/ppermute | solution.py:280
  21.0 1.9 %collective-permute-start = (bf16[2,4,32,128]{3,2,1,0:T(8,128)(2,1)S(1)}, bf16[2,4,32,128]{3,2,1,0:T(8,128)(2,1)S(1)}, u32[]{:S(2)}, u32[]{:S(2)}) collective-permute-start(bf16[2,4,32,128]{3,2,1,0:T(8,128)(2,1)S(1)} %multiply_convert_fusion.own_ref), channel_id=1, source_target_pairs={{0,32},{1,33},{2,34},{3,35},{4,36},{5,37},{6,38},{7,39},{8,40},{9,... | collective-permute-start | bytes 196616 | tf_op jit(solution)/shard_map/ppermute | solution.py:280
  22.9 0.8 slice.17
  23.7 0.0 copy-start
  23.7 0.0 copy-start.1
  23.7 2.1 %collective-permute-start.2 = (bf16[2,6,32,128]{3,2,1,0:T(8,128)(2,1)S(1)}, bf16[2,6,32,128]{3,2,1,0:T(8,128)(2,1)S(1)}, u32[]{:S(2)}, u32[]{:S(2)}) collective-permute-start(bf16[2,6,32,128]{3,2,1,0:T(8,128)(2,1)S(1)} %pad_maximum_fusion), channel_id=1, source_target_pairs={{0,31},{1,0},{2,1},{3,2},{4,3},{5,4},{6,5},{7,6},{8,7},{9,8},{10,9... | collective-permute-start | bytes 294920 | tf_op jit(solution)/shard_map/ppermute | solution.py:280
  25.8 1.6 %slice_bitcast_fusion = (bf16[27,128,128]{2,1,0:T(8,128)(2,1)S(1)}, bf16[27,128,128]{2,1,0:T(8,128)(2,1)S(1)}) fusion(bf16[2,27,128,128]{3,2,1,0:T(8,128)(2,1)} %param.7), kind=kLoop, calls=%fused_computation | loop fusion | bytes 3538944 | tf_op jit(solution)/shard_map/squeeze | solution.py:299
  27.4 0.0 collective-permute-done.4.below_earliest_ref
  27.4 0.0 collective-permute-done.3.below_earlier_ref
  27.4 0.0 collective-permute-done.1.earliest_ref
  27.4 0.0 collective-permute-done.earlier_ref
  27.4 0.6 collective-permute-done.2.below_ref
  28.0 0.0 copy-done
  28.0 0.0 copy-done.1
  28.0 2.5 %shard_map.68 = (bf16[6,4,32,128]{3,2,1,0:T(8,128)(2,1)S(1)}, f32[256,128]{1,0:T(8,128)S(1)}, bf16[4,2,32,128]{3,2,1,0:T(8,128)(2,1)S(1)}) custom-call(bf16[2,4,32,128]{3,2,1,0:T(8,128)(2,1)S(1)} %multiply_convert_fusion.own_ref, bf16[2,4,32,128]{3,2,1,0:T(8,128)(2,1)S(1)} %collective-permute-done.earlier_ref, ...), custom_call_target="tpu_custom_call" | custom-call | tf_op jit(solution)/shard_map/pallas_call | solution.py:18
  30.5 3.9 %collective-permute-start.5 = (bf16[4,2,32,128]{3,2,1,0:T(8,128)(2,1)S(1)}, bf16[4,2,32,128]{3,2,1,0:T(8,128)(2,1)S(1)}, u32[]{:S(2)}, u32[]{:S(2)}) collective-permute-start(bf16[4,2,32,128]{3,2,1,0:T(8,128)(2,1)S(1)} %get-tuple-element.11.own_ref.grad_ref), channel_id=1, source_target_pairs={{32,0},{33,1},{34,2},{35,3},{36,4},{37,5},{38,6},{39,7},{40,8},{41... | collective-permute-start | bytes 196616 | tf_op jit(solution)/shard_map/ppermute | solution.py:280
  34.5 2.0 %collective-permute-start.7 = (bf16[2,2,32,128]{3,2,1,0:T(8,128)(2,1)S(1)}, bf16[2,2,32,128]{3,2,1,0:T(8,128)(2,1)S(1)}, u32[]{:S(2)}, u32[]{:S(2)}) collective-permute-start(bf16[2,2,32,128]{3,2,1,0:T(8,128)(2,1)S(1)} %slice.20), channel_id=1, source_target_pairs={{32,1},{33,2},{34,3},{35,4},{36,5},{37,6},{38,7},{39,8},{40,9},{41... | collective-permute-start | bytes 98312 | tf_op jit(solution)/shard_map/ppermute | solution.py:280
  36.5 2.7 %collective-permute-start.6 = (bf16[2,2,32,128]{3,2,1,0:T(8,128)(2,1)S(1)}, bf16[2,2,32,128]{3,2,1,0:T(8,128)(2,1)S(1)}, u32[]{:S(2)}, u32[]{:S(2)}) collective-permute-start(bf16[2,2,32,128]{3,2,1,0:T(8,128)(2,1)S(1)} %slice.20), channel_id=1, source_target_pairs={{0,1},{1,2},{2,3},{3,4},{4,5},{5,6},{6,7},{7,8},{8,9},{9,10},{10,1... | collective-permute-start | bytes 98312 | tf_op jit(solution)/shard_map/ppermute | solution.py:280
  39.1 0.7 shard_map.71
  39.9 3.9 %collective-permute-done.7.corner_ref = bf16[2,2,32,128]{3,2,1,0:T(8,128)(2,1)S(1)} collective-permute-done((bf16[2,2,32,128]{3,2,1,0:T(8,128)(2,1)S(1)}, bf16[2,2,32,128]{3,2,1,0:T(8,128)(2,1)S(1)}, u32[]{:S(2)}, u32[]{:S(2)}) %collective-permute-start.7) | collective-permute-done | bytes 32800 | tf_op jit(solution)/shard_map/ppermute | solution.py:280
  43.7 0.1 collective-permute-done.6.above_ref
  43.8 0.0 collective-permute-done.5.later_ref
  43.8 0.8 shard_map.69.own_ref.grad_ref
  44.6 0.9 shard_map.72
  45.4 1.9 %collective-permute-start.11 = (bf16[16,54,4,128]{3,2,1,0:T(4,128)(2,1)S(1)}, bf16[16,54,4,128]{3,2,1,0:T(4,128)(2,1)S(1)}, u32[]{:S(2)}, u32[]{:S(2)}) collective-permute-start(bf16[16,54,4,128]{3,2,1,0:T(4,128)(2,1)S(1)} %get-tuple-element.18), channel_id=1, source_target_pairs={{0,1},{1,0},{2,3},{3,2},{4,5},{5,4},{6,7},{7,6},{8,9},{9,8},{10,11... | collective-permute-start | bytes 2654216 | tf_op jit(solution)/shard_map/ppermute | solution.py:345
  47.4 2.4 %collective-permute-done.11.came_ref = bf16[16,54,4,128]{3,2,1,0:T(4,128)(2,1)S(1)} collective-permute-done((bf16[16,54,4,128]{3,2,1,0:T(4,128)(2,1)S(1)}, bf16[16,54,4,128]{3,2,1,0:T(4,128)(2,1)S(1)}, u32[]{:S(2)}, u32[]{:S(2)}) %collective-permute-start.11) | collective-permute-done | bytes 884768 | tf_op jit(solution)/shard_map/ppermute | solution.py:345
  49.8 1.4 %shard_map.73 = bf16[16,54,4,128]{3,2,1,0:T(4,128)(2,1)} custom-call(bf16[16,54,4,128]{3,2,1,0:T(4,128)(2,1)S(1)} %get-tuple-element.17.keep_ref, bf16[16,54,4,128]{3,2,1,0:T(4,128)(2,1)S(1)} %collective-permute-done.11.came_ref), custom_call_target="tpu_custom_call" | custom-call | tf_op jit(solution)/shard_map/pallas_call | solution.py:18
  51.1 4.2 %all-to-all-start = ((bf16[16,54,4,128]{3,2,1,0:T(4,128)(2,1)}), bf16[16,54,4,128]{3,2,1,0:T(4,128)(2,1)S(1)}, u32[]{:S(2)}, u32[]{:S(2)}) async-start(bf16[16,54,4,128]{3,2,1,0:T(4,128)(2,1)} %shard_map.73), calls=%async_computation | async-start | bytes 1769472 | tf_op jit(solution)/shard_map/all_to_all | solution.py:348
  55.3 1.9 %collective-permute-start.8 = (bf16[4,2,32,128]{3,2,1,0:T(8,128)(2,1)S(1)}, bf16[4,2,32,128]{3,2,1,0:T(8,128)(2,1)S(1)}, u32[]{:S(2)}, u32[]{:S(2)}) collective-permute-start(bf16[4,2,32,128]{3,2,1,0:T(8,128)(2,1)S(1)} %shard_map.69.own_ref.grad_ref), channel_id=1, source_target_pairs={{32,0},{33,1},{34,2},{35,3},{36,4},{37,5},{38,6},{39,7},{40,8},{41... | collective-permute-start | bytes 196616 | tf_op jit(solution)/shard_map/ppermute | solution.py:280
  57.3 1.9 %collective-permute-start.10 = (bf16[2,2,32,128]{3,2,1,0:T(8,128)(2,1)S(1)}, bf16[2,2,32,128]{3,2,1,0:T(8,128)(2,1)S(1)}, u32[]{:S(2)}, u32[]{:S(2)}) collective-permute-start(bf16[2,2,32,128]{3,2,1,0:T(8,128)(2,1)S(1)} %slice.22), channel_id=1, source_target_pairs={{32,1},{33,2},{34,3},{35,4},{36,5},{37,6},{38,7},{39,8},{40,9},{41... | collective-permute-start | bytes 98312 | tf_op jit(solution)/shard_map/ppermute | solution.py:280
  59.2 2.0 %collective-permute-start.9 = (bf16[2,2,32,128]{3,2,1,0:T(8,128)(2,1)S(1)}, bf16[2,2,32,128]{3,2,1,0:T(8,128)(2,1)S(1)}, u32[]{:S(2)}, u32[]{:S(2)}) collective-permute-start(bf16[2,2,32,128]{3,2,1,0:T(8,128)(2,1)S(1)} %slice.22), channel_id=1, source_target_pairs={{0,1},{1,2},{2,3},{3,4},{4,5},{5,6},{6,7},{7,8},{8,9},{9,10},{10,1... | collective-permute-start | bytes 98312 | tf_op jit(solution)/shard_map/ppermute | solution.py:280
  61.2 17.8 %collective-permute-done.10.corner_ref = bf16[2,2,32,128]{3,2,1,0:T(8,128)(2,1)S(1)} collective-permute-done((bf16[2,2,32,128]{3,2,1,0:T(8,128)(2,1)S(1)}, bf16[2,2,32,128]{3,2,1,0:T(8,128)(2,1)S(1)}, u32[]{:S(2)}, u32[]{:S(2)}) %collective-permute-start.10) | collective-permute-done | bytes 32800 | tf_op jit(solution)/shard_map/ppermute | solution.py:280
  79.0 0.0 collective-permute-done.9.above_ref
  79.0 0.0 collective-permute-done.8.later_ref
  79.0 1.3 %shard_map.70 = (bf16[2,4,32,128]{3,2,1,0:T(8,128)(2,1)}, f32[8,128]{1,0:T(8,128)S(1)}) custom-call(bf16[4,2,32,128]{3,2,1,0:T(8,128)(2,1)S(1)} %shard_map.69.own_ref.grad_ref, bf16[4,2,32,128]{3,2,1,0:T(8,128)(2,1)S(1)} %collective-permute-done.8.later_ref, bf16[2,2,32,128]{3,2,1,0:T(8,128)(2,1)S(1)} %collective-permute-done.9.above_ref, ...), custom_call_target="tpu_custom_call" | custom-call | tf_op jit(solution)/shard_map/pallas_call | solution.py:18
  80.3 0.9 all-to-all-done.in_ref
  81.2 0.4 shard_map.74
  81.5 22.7 %all_to_all.10.refs_0_ = bf16[16,8,256]{2,1,0:T(8,128)(2,1)S(1)} all-to-all(bf16[16,8,256]{2,1,0:T(8,128)(2,1)S(1)} %shard_map.74), channel_id=1, replica_groups=mesh['frame'=16,'tile'=32] {'frame'}, dimensions={0} | all-to-all | bytes 131072 | tf_op jit(solution)/shard_map/all_to_all | solution.py:366
  104.2 0.7 shard_map.75
  (3 shorter events, 0.0 us)
Async XLA Ops:
  1.6 25.8 %collective-permute-start.4 = (bf16[2,4,32,128]{3,2,1,0:T(8,128)(2,1)S(1)}, bf16[2,4,32,128]{3,2,1,0:T(8,128)(2,1)S(1)}, u32[]{:S(2)}, u32[]{:S(2)}) collective-permute-start(bf16[2,4,32,128]{3,2,1,0:T(8,128)(2,1)S(1)} %multiply_convert_fusion.own_ref), channel_id=1, source_target_pairs={{0,95},{1,64},{2,65},{3,66},{4,67},{5,68},{6,69},{7,70},{8,71},{9,... | collective-permute-start | bytes 196616 | tf_op jit(solution)/shard_map/ppermute | solution.py:280
  9.8 17.6 %collective-permute-start.3 = (bf16[2,4,32,128]{3,2,1,0:T(8,128)(2,1)S(1)}, bf16[2,4,32,128]{3,2,1,0:T(8,128)(2,1)S(1)}, u32[]{:S(2)}, u32[]{:S(2)}) collective-permute-start(bf16[2,4,32,128]{3,2,1,0:T(8,128)(2,1)S(1)} %multiply_convert_fusion.own_ref), channel_id=1, source_target_pairs={{0,63},{1,32},{2,33},{3,34},{4,35},{5,36},{6,37},{7,38},{8,39},{9,... | collective-permute-start | bytes 196616 | tf_op jit(solution)/shard_map/ppermute | solution.py:280
  15.5 12.0 %collective-permute-start.1 = (bf16[2,4,32,128]{3,2,1,0:T(8,128)(2,1)S(1)}, bf16[2,4,32,128]{3,2,1,0:T(8,128)(2,1)S(1)}, u32[]{:S(2)}, u32[]{:S(2)}) collective-permute-start(bf16[2,4,32,128]{3,2,1,0:T(8,128)(2,1)S(1)} %multiply_convert_fusion.own_ref), channel_id=1, source_target_pairs={{0,64},{1,65},{2,66},{3,67},{4,68},{5,69},{6,70},{7,71},{8,72},{9,... | collective-permute-start | bytes 196616 | tf_op jit(solution)/shard_map/ppermute | solution.py:280
  21.0 6.4 %collective-permute-start = (bf16[2,4,32,128]{3,2,1,0:T(8,128)(2,1)S(1)}, bf16[2,4,32,128]{3,2,1,0:T(8,128)(2,1)S(1)}, u32[]{:S(2)}, u32[]{:S(2)}) collective-permute-start(bf16[2,4,32,128]{3,2,1,0:T(8,128)(2,1)S(1)} %multiply_convert_fusion.own_ref), channel_id=1, source_target_pairs={{0,32},{1,33},{2,34},{3,35},{4,36},{5,37},{6,38},{7,39},{8,40},{9,... | collective-permute-start | bytes 196616 | tf_op jit(solution)/shard_map/ppermute | solution.py:280
  23.7 4.3 %copy-start = (bf16[2,4,32,128]{3,2,1,0:T(8,128)(2,1)S(1)}, bf16[2,4,32,128]{3,2,1,0:T(8,128)(2,1)}, u32[]{:S(2)}) copy-start(bf16[2,4,32,128]{3,2,1,0:T(8,128)(2,1)} %top_ref.1) | copy-start | bytes 196612
  23.7 4.3 %copy-start.1 = (f32[2,128]{1,0:T(2,128)S(1)}, f32[2,128]{1,0:T(2,128)}, u32[]{:S(2)}) copy-start(f32[2,128]{1,0:T(2,128)} %gain_ref.3) | copy-start | bytes 3076
  23.7 4.3 %collective-permute-start.2 = (bf16[2,6,32,128]{3,2,1,0:T(8,128)(2,1)S(1)}, bf16[2,6,32,128]{3,2,1,0:T(8,128)(2,1)S(1)}, u32[]{:S(2)}, u32[]{:S(2)}) collective-permute-start(bf16[2,6,32,128]{3,2,1,0:T(8,128)(2,1)S(1)} %pad_maximum_fusion), channel_id=1, source_target_pairs={{0,31},{1,0},{2,1},{3,2},{4,3},{5,4},{6,5},{7,6},{8,7},{9,8},{10,9... | collective-permute-start | bytes 294920 | tf_op jit(solution)/shard_map/ppermute | solution.py:280
  30.5 13.3 %collective-permute-start.5 = (bf16[4,2,32,128]{3,2,1,0:T(8,128)(2,1)S(1)}, bf16[4,2,32,128]{3,2,1,0:T(8,128)(2,1)S(1)}, u32[]{:S(2)}, u32[]{:S(2)}) collective-permute-start(bf16[4,2,32,128]{3,2,1,0:T(8,128)(2,1)S(1)} %get-tuple-element.11.own_ref.grad_ref), channel_id=1, source_target_pairs={{32,0},{33,1},{34,2},{35,3},{36,4},{37,5},{38,6},{39,7},{40,8},{41... | collective-permute-start | bytes 196616 | tf_op jit(solution)/shard_map/ppermute | solution.py:280
  34.5 9.2 %collective-permute-start.7 = (bf16[2,2,32,128]{3,2,1,0:T(8,128)(2,1)S(1)}, bf16[2,2,32,128]{3,2,1,0:T(8,128)(2,1)S(1)}, u32[]{:S(2)}, u32[]{:S(2)}) collective-permute-start(bf16[2,2,32,128]{3,2,1,0:T(8,128)(2,1)S(1)} %slice.20), channel_id=1, source_target_pairs={{32,1},{33,2},{34,3},{35,4},{36,5},{37,6},{38,7},{39,8},{40,9},{41... | collective-permute-start | bytes 98312 | tf_op jit(solution)/shard_map/ppermute | solution.py:280
  36.5 7.3 %collective-permute-start.6 = (bf16[2,2,32,128]{3,2,1,0:T(8,128)(2,1)S(1)}, bf16[2,2,32,128]{3,2,1,0:T(8,128)(2,1)S(1)}, u32[]{:S(2)}, u32[]{:S(2)}) collective-permute-start(bf16[2,2,32,128]{3,2,1,0:T(8,128)(2,1)S(1)} %slice.20), channel_id=1, source_target_pairs={{0,1},{1,2},{2,3},{3,4},{4,5},{5,6},{6,7},{7,8},{8,9},{9,10},{10,1... | collective-permute-start | bytes 98312 | tf_op jit(solution)/shard_map/ppermute | solution.py:280
  45.4 4.3 %collective-permute-start.11 = (bf16[16,54,4,128]{3,2,1,0:T(4,128)(2,1)S(1)}, bf16[16,54,4,128]{3,2,1,0:T(4,128)(2,1)S(1)}, u32[]{:S(2)}, u32[]{:S(2)}) collective-permute-start(bf16[16,54,4,128]{3,2,1,0:T(4,128)(2,1)S(1)} %get-tuple-element.18), channel_id=1, source_target_pairs={{0,1},{1,0},{2,3},{3,2},{4,5},{5,4},{6,7},{7,6},{8,9},{9,8},{10,11... | collective-permute-start | bytes 2654216 | tf_op jit(solution)/shard_map/ppermute | solution.py:345
  51.1 30.0 %all-to-all-start = ((bf16[16,54,4,128]{3,2,1,0:T(4,128)(2,1)}), bf16[16,54,4,128]{3,2,1,0:T(4,128)(2,1)S(1)}, u32[]{:S(2)}, u32[]{:S(2)}) async-start(bf16[16,54,4,128]{3,2,1,0:T(4,128)(2,1)} %shard_map.73), calls=%async_computation | async-start | bytes 1769472 | tf_op jit(solution)/shard_map/all_to_all | solution.py:348
  55.3 23.7 %collective-permute-start.8 = (bf16[4,2,32,128]{3,2,1,0:T(8,128)(2,1)S(1)}, bf16[4,2,32,128]{3,2,1,0:T(8,128)(2,1)S(1)}, u32[]{:S(2)}, u32[]{:S(2)}) collective-permute-start(bf16[4,2,32,128]{3,2,1,0:T(8,128)(2,1)S(1)} %shard_map.69.own_ref.grad_ref), channel_id=1, source_target_pairs={{32,0},{33,1},{34,2},{35,3},{36,4},{37,5},{38,6},{39,7},{40,8},{41... | collective-permute-start | bytes 196616 | tf_op jit(solution)/shard_map/ppermute | solution.py:280
  57.3 21.7 %collective-permute-start.10 = (bf16[2,2,32,128]{3,2,1,0:T(8,128)(2,1)S(1)}, bf16[2,2,32,128]{3,2,1,0:T(8,128)(2,1)S(1)}, u32[]{:S(2)}, u32[]{:S(2)}) collective-permute-start(bf16[2,2,32,128]{3,2,1,0:T(8,128)(2,1)S(1)} %slice.22), channel_id=1, source_target_pairs={{32,1},{33,2},{34,3},{35,4},{36,5},{37,6},{38,7},{39,8},{40,9},{41... | collective-permute-start | bytes 98312 | tf_op jit(solution)/shard_map/ppermute | solution.py:280
  59.2 19.8 %collective-permute-start.9 = (bf16[2,2,32,128]{3,2,1,0:T(8,128)(2,1)S(1)}, bf16[2,2,32,128]{3,2,1,0:T(8,128)(2,1)S(1)}, u32[]{:S(2)}, u32[]{:S(2)}) collective-permute-start(bf16[2,2,32,128]{3,2,1,0:T(8,128)(2,1)S(1)} %slice.22), channel_id=1, source_target_pairs={{0,1},{1,2},{2,3},{3,4},{4,5},{5,6},{6,7},{7,8},{8,9},{9,10},{10,1... | collective-permute-start | bytes 98312 | tf_op jit(solution)/shard_map/ppermute | solution.py:280

commit v8 on v5

--- a/solution.py
+++ b/solution.py
@@ -167,9 +167,8 @@
 
 
 def second_backward(
-    own_ref, later_ref, above_ref, kernel_ref, gain_ref, pre_ref, token_ref, grad_ref, store
+    own_ref, later_ref, above_ref, kernel_ref, gain_ref, pre_ref, grad_ref, store
 ):
-    del token_ref
     rows, frames, _, _ = own_ref.shape
     last = at_last_tile()
     seams = {(rows - 2, 2): last, (rows - 1, 0): last}
@@ -213,61 +212,58 @@
             send_ref[:, tap] = jnp.where(odd, even_part, odd_part).astype(BF16)
 
 
-def second_kernel_gradient(next_ref, grad_ref, keep_ref, send_ref, token_ref, store):
+def second_kernel_gradient(next_ref, grad_ref, keep_ref, send_ref, store):
     rows = grad_ref.shape[0]
     last = at_last_tile()
     seams = {(rows - 3, 2): last, (rows - 2, 0): last}
     store_columns(store, window_of(block_rows(next_ref)), (0, 1, 2), seams)
     split_gradient(store, seams, grad_ref, keep_ref, send_ref)
-    token_ref[...] = jnp.zeros_like(token_ref)
-
-
-def first_kernel_gradient(own_ref, earlier_ref, below_ref, grad_ref, keep_ref, send_ref, store):
+
+
+def first_kernel_gradient(
+    own_ref, earlier_ref, below_ref, grad_ref, keep_second, send_second, keep_ref, send_ref, store
+):
     rows = grad_ref.shape[0]
     last = at_last_tile()
     seams = {(rows - 2, 2): last, (rows - 1, 0): last}
     window = window_of(first_rows((earlier_ref, own_ref), below_ref, rows + 2))
     store_columns(store, window, (0, 1, 2), seams)
+    keep_ref[:, TAPS:], send_ref[:, TAPS:] = keep_second[...], send_second[...]
     split_gradient(store, seams, grad_ref, keep_ref, send_ref)
 
 
-def pack_rows(own_ref, later_ref, token_ref, out_ref):
-    del token_ref
+def pack_rows(own_ref, later_ref, out_ref):
     frames, first = own_ref.shape[1], own_ref.shape[0] - out_ref.shape[0]
     out_ref[:, :frames] = own_ref[first:]
     out_ref[:, frames:] = later_ref[first:]
 
 
-def add_pair(keep_ref, came_ref, out_ref, token_ref):
+def add_pair(keep_ref, came_ref, out_ref):
     out_ref[...] = (keep_ref[...].astype(F32) + came_ref[...].astype(F32)).astype(BF16)
-    token_ref[...] = jnp.zeros_like(token_ref)
-
-
-def sum_tiles(first_ref, second_ref, token_ref, out_ref, rows_ref):
+
+
+def sum_tiles(share, in_ref, token_ref, out_ref, rows_ref):
     del token_ref
-    chips, taps, share, _ = first_ref.shape
-    groups, width, _ = out_ref.shape
+    total = in_ref[0].astype(F32)
+    for chip in range(1, in_ref.shape[0]):
+        total = total + in_ref[chip].astype(F32)
+    groups, width, lanes = out_ref.shape
+    stride, taps = lanes // share, 2 * TAPS
+    total = total.reshape(taps, share, -1)
     rows_ref[...] = jnp.zeros_like(rows_ref)
-    stride = rows_ref.shape[0] // share
-    for layer, in_ref in enumerate((first_ref, second_ref)):
-        total = in_ref[0].astype(F32)
-        for chip in range(1, chips):
-            total = total + in_ref[chip].astype(F32)
-        for row in range(share):
-            start = row * stride + layer * taps
-            rows_ref[start : start + taps] = total[:, row]
-    out_ref[...] = rows_ref[...].T.reshape(groups, width, -1).astype(BF16)
+    for place in range(share):
+        rows_ref[place * stride : place * stride + taps] = total[:, place]
+    out_ref[...] = rows_ref[...].T.reshape(groups, width, lanes).astype(BF16)
 
 
 def sum_frames(scale, in_ref, out_ref):
-    groups = in_ref.shape[0]
     total = in_ref[0].astype(F32)
-    for group in range(1, groups):
+    for group in range(1, in_ref.shape[0]):
         total = total + in_ref[group].astype(F32)
     share, _, taps = out_ref.shape
     stride = total.shape[1] // share
-    for row in range(share):
-        out_ref[row] = total[:, row * stride : row * stride + taps] * scale
+    for place in range(share):
+        out_ref[place] = total[:, place * stride : place * stride + taps] * scale
 
 
 def shape_of(*dims, dtype=BF16):
@@ -328,72 +324,66 @@
 
     share = channels // tiles
     part = shape_of(tiles // 2, TAPS, share, channels)
+    both = shape_of(tiles // 2, 2 * TAPS, share, channels)
     mark = shape_of(8, channels, dtype=F32)
 
-    def with_neighbours(later, grad, token):
-        edge = shape_of(2, 2 * frames, *block)
-        packed = call(pack_rows, edge, grad, later, token)
-        return from_above(packed)
-
-    by_core = [list(range(core, tiles, 2)) for core in range(2)]
-
-    def sent_and_paired(keep, send):
-        came = partner(send)
-        paired, token = call(add_pair, (part, mark), keep, came)
-        arrived = lax.all_to_all(
-            paired, "tile", split_axis=0, concat_axis=0, tiled=True, axis_index_groups=by_core
-        )
-        return arrived, token
-
-    later_1 = earlier_frames(grad_1)
-    keep_1, send_1, token = call(
-        second_kernel_gradient, (part, part, mark), next_1, grad_1, scratch=column_store(rows + 2, 2 * frames)
-    )
-    above_1 = with_neighbours(later_1, grad_1, token)
-    arrived_1, token = sent_and_paired(keep_1, send_1)
+    def neighbours(grad):
+        later = earlier_frames(grad)
+        packed = call(pack_rows, shape_of(2, 2 * frames, *block), grad, later)
+        return later, from_above(packed)
+
+    next_to = neighbours(grad_1)
+    keep_1, send_1 = call(
+        second_kernel_gradient,
+        (part, part),
+        next_1,
+        grad_1,
+        scratch=column_store(wide, 2 * frames),
+    )
     grad_0 = call(
         second_backward,
         grad_shape,
         grad_1,
-        later_1,
-        above_1,
+        *next_to,
         kernels[1],
         norm_gains,
         pre_0,
-        token,
         scratch=column_store(rows + 2, 2 * frames),
     )
-    keep_0, send_0 = call(
+    keep, send = call(
         first_kernel_gradient,
-        (part, part),
+        (both, both),
         own_0,
         earlier_0,
         below,
         grad_0,
+        keep_1,
+        send_1,
         scratch=column_store(rows + 2, 2 * frames),
     )
-    arrived_0, token = sent_and_paired(keep_0, send_0)
-    later_0 = earlier_frames(grad_0)
-    above_0 = with_neighbours(later_0, grad_0, token)
+    full = shape_of(tiles // 2, 2 * TAPS * share, channels)
+    came = partner(send).reshape(full.shape)
+    paired = call(add_pair, full, keep.reshape(full.shape), came)
+    by_core = [list(range(core, tiles, 2)) for core in range(2)]
+    arrived = lax.all_to_all(paired, "tile", 0, 0, tiled=True, axis_index_groups=by_core)
+    next_to = neighbours(grad_0)
     input_grad, token = call(
         first_backward,
         (shape_of(frames, rows, *block), mark),
         grad_0,
-        later_0,
-        above_0,
+        *next_to,
         kernels[0],
         scratch=column_store(rows + 2, 2 * frames),
     )
-    padded = -(-2 * TAPS // 32) * 32 * share
+    lanes = 64 * share
     by_frame = call(
-        sum_tiles,
-        shape_of(groups, channels // groups, padded),
-        arrived_0,
-        arrived_1,
+        lambda *refs: sum_tiles(share, *refs),
+        shape_of(groups, channels // groups, lanes),
+        arrived,
         token,
-        scratch=(pltpu.VMEM((padded, channels), F32),),
-    )
-    spread = lax.all_to_all(by_frame, "frame", split_axis=0, concat_axis=0, tiled=True)
+        scratch=(pltpu.VMEM((lanes, channels), F32),),
+    )
+    spread = lax.all_to_all(by_frame, "frame", 0, 0, tiled=True)
     scale = 1.0 / math.sqrt(cells * tiles * groups)
     summed = call(
         lambda *refs: sum_frames(scale, *refs),

time: 112 us -> 102 us (0.911)
  the two profiles are of different devices: /device:TPU:32 before, /device:TPU:2 now
where the time goes in v8:
time: 102 us; the launch traced here: 101 us
  waiting for transfers between devices  35.2 us (35%)
  starting transfers between devices  29.1 us (29%)
  blocking collectives  24.7 us (24%)
  Pallas kernels  8.28 us (8%)
  local copies, waits for them, and re-layouts  2.37 us (2%)
    all_to_all x1, blocking collectives, local(): spread = lax.all_to_all(by_frame, 'frame', 0, 0, tiled=True)  24.7 us
    ppermute x2, waiting for transfers between devices, from_above(): lax.ppermute(value, 'tile', [(i, (i + 1) % tiles) for i in range(tiles)])  20.4 us
    ppermute x2, starting transfers between devices, next_frames(): lax.ppermute(value, 'frame', [(i, i + steps) for i in range(groups - step...  9.43 us
    ppermute x2, waiting for transfers between devices, earlier_frames(): return lax.ppermute(value, 'frame', [(i + 1, i) for i in range(groups - 1)])  8.37 us
    pallas_call x10, Pallas kernels, call(): pl.pallas_call(kernel, out_shape=out_shape, scratch_shapes=list(scratch),...  8.28 us
    ppermute x1, starting transfers between devices, from_below(): lax.ppermute(value, 'tile', [((i + 1) % tiles, i) for i in range(tiles)])  5.62 us
    all_to_all x1, starting transfers between devices, local(): lax.all_to_all(paired, 'tile', 0, 0, tiled=True, axis_index_groups=by_core)  4.18 us
    ppermute x2, starting transfers between devices, earlier_frames(): return lax.ppermute(value, 'frame', [(i + 1, i) for i in range(groups - 1)])  4.1 us
  transfers between devices with their start and end apart: 9, of which 8 were waited for; matrix products, arithmetic and copies ran while one was open for 2% of the time, Pallas kernels for 2%

profile of v8, /device:TPU:2, one launch (start us, length us, event | category | flops | bytes accessed | tf_op | source)
XLA Modules:
  0.0 101.4 jit_solution(5834905776023983408)
XLA Ops:
  0.6 0.9 multiply_convert_fusion.own_ref
  1.6 4.0 %collective-permute-start.1 = (bf16[2,4,32,128]{3,2,1,0:T(8,128)(2,1)S(1)}, bf16[2,4,32,128]{3,2,1,0:T(8,128)(2,1)S(1)}, u32[]{:S(2)}, u32[]{:S(2)}) collective-permute-start(bf16[2,4,32,128]{3,2,1,0:T(8,128)(2,1)S(1)} %multiply_convert_fusion.own_ref), channel_id=1, source_target_pairs={{0,64},{32,96},{64,128},{96,160},{128,192},{160,224},{192,256},{22... | collective-permute-start | bytes 196616 | tf_op jit(solution)/shard_map/ppermute | solution.py:283
  5.6 5.4 %collective-permute-start = (bf16[2,4,32,128]{3,2,1,0:T(8,128)(2,1)S(1)}, bf16[2,4,32,128]{3,2,1,0:T(8,128)(2,1)S(1)}, u32[]{:S(2)}, u32[]{:S(2)}) collective-permute-start(bf16[2,4,32,128]{3,2,1,0:T(8,128)(2,1)S(1)} %multiply_convert_fusion.own_ref), channel_id=1, source_target_pairs={{0,32},{32,64},{64,96},{96,128},{128,160},{160,192},{192,224},{224... | collective-permute-start | bytes 196616 | tf_op jit(solution)/shard_map/ppermute | solution.py:283
  11.0 0.8 slice.11
  11.8 0.0 collective-permute-done.1.earliest_ref
  11.8 1.1 %collective-permute-done.earlier_ref = bf16[2,4,32,128]{3,2,1,0:T(8,128)(2,1)S(1)} collective-permute-done((bf16[2,4,32,128]{3,2,1,0:T(8,128)(2,1)S(1)}, bf16[2,4,32,128]{3,2,1,0:T(8,128)(2,1)S(1)}, u32[]{:S(2)}, u32[]{:S(2)}) %collective-permute-start) | collective-permute-done | bytes 65568 | tf_op jit(solution)/shard_map/ppermute | solution.py:283
  12.9 0.0 copy-start
  13.0 0.0 copy-start.1
  13.0 5.6 %collective-permute-start.2 = (bf16[28,32,128]{2,1,0:T(8,128)(2,1)S(1)}, bf16[28,32,128]{2,1,0:T(8,128)(2,1)S(1)}, u32[]{:S(2)}, u32[]{:S(2)}) collective-permute-start(bf16[28,32,128]{2,1,0:T(8,128)(2,1)S(1)} %pad_maximum_fusion), channel_id=1, source_target_pairs={{1,0},{2,1},{3,2},{4,3},{5,4},{6,5},{7,6},{8,7},{9,8},{10,9},{11,1... | collective-permute-start | bytes 688136 | tf_op jit(solution)/shard_map/ppermute | solution.py:289
  18.6 1.6 %slice_bitcast_fusion = (bf16[27,128,128]{2,1,0:T(8,128)(2,1)S(1)}, bf16[27,128,128]{2,1,0:T(8,128)(2,1)S(1)}) fusion(bf16[2,27,128,128]{3,2,1,0:T(8,128)(2,1)} %param.7), kind=kLoop, calls=%fused_computation | loop fusion | bytes 3538944 | tf_op jit(solution)/shard_map/squeeze | solution.py:320
  20.2 1.9 %collective-permute-done.2.below_ref = bf16[28,32,128]{2,1,0:T(8,128)(2,1)S(1)} collective-permute-done((bf16[28,32,128]{2,1,0:T(8,128)(2,1)S(1)}, bf16[28,32,128]{2,1,0:T(8,128)(2,1)S(1)}, u32[]{:S(2)}, u32[]{:S(2)}) %collective-permute-start.2) | collective-permute-done | bytes 229408 | tf_op jit(solution)/shard_map/ppermute | solution.py:289
  22.1 0.0 copy-done
  22.1 0.0 copy-done.1
  22.1 2.5 %shard_map.68 = (bf16[6,4,32,128]{3,2,1,0:T(8,128)(2,1)S(1)}, f32[256,128]{1,0:T(8,128)S(1)}, bf16[4,2,32,128]{3,2,1,0:T(8,128)(2,1)S(1)}) custom-call(bf16[2,4,32,128]{3,2,1,0:T(8,128)(2,1)S(1)} %multiply_convert_fusion.own_ref, bf16[2,4,32,128]{3,2,1,0:T(8,128)(2,1)S(1)} %collective-permute-done.earlier_ref, ...), custom_call_target="tpu_custom_call" | custom-call | tf_op jit(solution)/shard_map/pallas_call | solution.py:18
  24.7 1.9 %collective-permute-start.3 = (bf16[4,2,32,128]{3,2,1,0:T(8,128)(2,1)S(1)}, bf16[4,2,32,128]{3,2,1,0:T(8,128)(2,1)S(1)}, u32[]{:S(2)}, u32[]{:S(2)}) collective-permute-start(bf16[4,2,32,128]{3,2,1,0:T(8,128)(2,1)S(1)} %get-tuple-element.11.own_ref.grad_ref), channel_id=1, source_target_pairs={{32,0},{64,32},{96,64},{128,96},{160,128},{192,160},{224,192},{256... | collective-permute-start | bytes 196616 | tf_op jit(solution)/shard_map/ppermute | solution.py:286
  26.6 4.3 %collective-permute-done.3.later_ref = bf16[4,2,32,128]{3,2,1,0:T(8,128)(2,1)S(1)} collective-permute-done((bf16[4,2,32,128]{3,2,1,0:T(8,128)(2,1)S(1)}, bf16[4,2,32,128]{3,2,1,0:T(8,128)(2,1)S(1)}, u32[]{:S(2)}, u32[]{:S(2)}) %collective-permute-start.3) | collective-permute-done | bytes 65568 | tf_op jit(solution)/shard_map/ppermute | solution.py:286
  30.9 1.9 %collective-permute-start.4 = (bf16[2,4,32,128]{3,2,1,0:T(8,128)(2,1)S(1)}, bf16[2,4,32,128]{3,2,1,0:T(8,128)(2,1)S(1)}, u32[]{:S(2)}, u32[]{:S(2)}) collective-permute-start(bf16[2,4,32,128]{3,2,1,0:T(8,128)(2,1)S(1)} %shard_map.69), channel_id=1, source_target_pairs={{0,1},{1,2},{2,3},{3,4},{4,5},{5,6},{6,7},{7,8},{8,9},{9,10},{10,1... | collective-permute-start | bytes 196616 | tf_op jit(solution)/shard_map/ppermute | solution.py:292
  32.8 0.7 shard_map.73
  33.6 5.0 %collective-permute-done.4.above_ref = bf16[2,4,32,128]{3,2,1,0:T(8,128)(2,1)S(1)} collective-permute-done((bf16[2,4,32,128]{3,2,1,0:T(8,128)(2,1)S(1)}, bf16[2,4,32,128]{3,2,1,0:T(8,128)(2,1)S(1)}, u32[]{:S(2)}, u32[]{:S(2)}) %collective-permute-start.4) | collective-permute-done | bytes 65568 | tf_op jit(solution)/shard_map/ppermute | solution.py:292
  38.6 0.8 shard_map.70.own_ref.grad_ref
  39.4 0.9 shard_map.74
  40.2 1.9 %collective-permute-start.7 = (bf16[16,54,4,128]{3,2,1,0:T(4,128)(2,1)S(1)}, bf16[16,54,4,128]{3,2,1,0:T(4,128)(2,1)S(1)}, u32[]{:S(2)}, u32[]{:S(2)}) collective-permute-start(bf16[16,54,4,128]{3,2,1,0:T(4,128)(2,1)S(1)} %get-tuple-element.18), channel_id=1, source_target_pairs={{0,1},{1,0},{2,3},{3,2},{4,5},{5,4},{6,7},{7,6},{8,9},{9,8},{10,11... | collective-permute-start | bytes 2654216 | tf_op jit(solution)/shard_map/ppermute | solution.py:295
  42.2 2.4 %collective-permute-done.7 = bf16[16,54,4,128]{3,2,1,0:T(4,128)(2,1)S(1)} collective-permute-done((bf16[16,54,4,128]{3,2,1,0:T(4,128)(2,1)S(1)}, bf16[16,54,4,128]{3,2,1,0:T(4,128)(2,1)S(1)}, u32[]{:S(2)}, u32[]{:S(2)}) %collective-permute-start.7) | collective-permute-done | bytes 884768 | tf_op jit(solution)/shard_map/ppermute | solution.py:295
  44.5 1.1 %shard_map.75 = bf16[16,216,128]{2,1,0:T(8,128)(2,1)} custom-call(bf16[16,216,128]{2,1,0:T(8,128)(2,1)S(1)} %bitcast.12, bf16[16,216,128]{2,1,0:T(8,128)(2,1)S(1)} %bitcast.13), custom_call_target="tpu_custom_call" | custom-call | tf_op jit(solution)/shard_map/pallas_call | solution.py:18
  45.7 4.2 %all-to-all-start = ((bf16[16,216,128]{2,1,0:T(8,128)(2,1)}), bf16[16,216,128]{2,1,0:T(8,128)(2,1)S(1)}, u32[]{:S(2)}, u32[]{:S(2)}) async-start(bf16[16,216,128]{2,1,0:T(8,128)(2,1)} %shard_map.75), calls=%async_computation | async-start | bytes 1769472 | tf_op jit(solution)/shard_map/all_to_all | solution.py:368
  49.9 2.2 %collective-permute-start.5 = (bf16[4,2,32,128]{3,2,1,0:T(8,128)(2,1)S(1)}, bf16[4,2,32,128]{3,2,1,0:T(8,128)(2,1)S(1)}, u32[]{:S(2)}, u32[]{:S(2)}) collective-permute-start(bf16[4,2,32,128]{3,2,1,0:T(8,128)(2,1)S(1)} %shard_map.70.own_ref.grad_ref), channel_id=1, source_target_pairs={{32,0},{64,32},{96,64},{128,96},{160,128},{192,160},{224,192},{256... | collective-permute-start | bytes 196616 | tf_op jit(solution)/shard_map/ppermute | solution.py:286
  52.1 4.1 %collective-permute-done.5.later_ref = bf16[4,2,32,128]{3,2,1,0:T(8,128)(2,1)S(1)} collective-permute-done((bf16[4,2,32,128]{3,2,1,0:T(8,128)(2,1)S(1)}, bf16[4,2,32,128]{3,2,1,0:T(8,128)(2,1)S(1)}, u32[]{:S(2)}, u32[]{:S(2)}) %collective-permute-start.5) | collective-permute-done | bytes 65568 | tf_op jit(solution)/shard_map/ppermute | solution.py:286
  56.1 1.9 %collective-permute-start.6 = (bf16[2,4,32,128]{3,2,1,0:T(8,128)(2,1)S(1)}, bf16[2,4,32,128]{3,2,1,0:T(8,128)(2,1)S(1)}, u32[]{:S(2)}, u32[]{:S(2)}) collective-permute-start(bf16[2,4,32,128]{3,2,1,0:T(8,128)(2,1)S(1)} %shard_map.71), channel_id=1, source_target_pairs={{0,1},{1,2},{2,3},{3,4},{4,5},{5,6},{6,7},{7,8},{8,9},{9,10},{10,1... | collective-permute-start | bytes 196616 | tf_op jit(solution)/shard_map/ppermute | solution.py:292
  58.0 15.4 %collective-permute-done.6.above_ref = bf16[2,4,32,128]{3,2,1,0:T(8,128)(2,1)S(1)} collective-permute-done((bf16[2,4,32,128]{3,2,1,0:T(8,128)(2,1)S(1)}, bf16[2,4,32,128]{3,2,1,0:T(8,128)(2,1)S(1)}, u32[]{:S(2)}, u32[]{:S(2)}) %collective-permute-start.6) | collective-permute-done | bytes 65568 | tf_op jit(solution)/shard_map/ppermute | solution.py:292
  73.4 1.3 %shard_map.72 = (bf16[2,4,32,128]{3,2,1,0:T(8,128)(2,1)}, f32[8,128]{1,0:T(8,128)S(1)}) custom-call(bf16[4,2,32,128]{3,2,1,0:T(8,128)(2,1)S(1)} %shard_map.70.own_ref.grad_ref, bf16[4,2,32,128]{3,2,1,0:T(8,128)(2,1)S(1)} %collective-permute-done.5.later_ref, bf16[2,4,32,128]{3,2,1,0:T(8,128)(2,1)S(1)} %collective-permute-done.6.above_ref, ...), custom_call_target="tpu_custom_call" | custom-call | tf_op jit(solution)/shard_map/pallas_call | solution.py:18
  74.7 1.0 all-to-all-done.refs_0_
  75.7 0.3 shard_map.76
  76.0 24.7 %all_to_all.10.refs_0_ = bf16[16,8,256]{2,1,0:T(8,128)(2,1)S(1)} all-to-all(bf16[16,8,256]{2,1,0:T(8,128)(2,1)S(1)} %shard_map.76), channel_id=1, replica_groups=mesh['frame'=16,'tile'=32] {'frame'}, dimensions={0} | all-to-all | bytes 131072 | tf_op jit(solution)/shard_map/all_to_all | solution.py:386
  100.7 0.7 shard_map.77
  (3 shorter events, 0.0 us)
Async XLA Ops:
  1.6 10.2 %collective-permute-start.1 = (bf16[2,4,32,128]{3,2,1,0:T(8,128)(2,1)S(1)}, bf16[2,4,32,128]{3,2,1,0:T(8,128)(2,1)S(1)}, u32[]{:S(2)}, u32[]{:S(2)}) collective-permute-start(bf16[2,4,32,128]{3,2,1,0:T(8,128)(2,1)S(1)} %multiply_convert_fusion.own_ref), channel_id=1, source_target_pairs={{0,64},{32,96},{64,128},{96,160},{128,192},{160,224},{192,256},{22... | collective-permute-start | bytes 196616 | tf_op jit(solution)/shard_map/ppermute | solution.py:283
  5.6 7.3 %collective-permute-start = (bf16[2,4,32,128]{3,2,1,0:T(8,128)(2,1)S(1)}, bf16[2,4,32,128]{3,2,1,0:T(8,128)(2,1)S(1)}, u32[]{:S(2)}, u32[]{:S(2)}) collective-permute-start(bf16[2,4,32,128]{3,2,1,0:T(8,128)(2,1)S(1)} %multiply_convert_fusion.own_ref), channel_id=1, source_target_pairs={{0,32},{32,64},{64,96},{96,128},{128,160},{160,192},{192,224},{224... | collective-permute-start | bytes 196616 | tf_op jit(solution)/shard_map/ppermute | solution.py:283
  12.9 9.2 %copy-start = (bf16[2,4,32,128]{3,2,1,0:T(8,128)(2,1)S(1)}, bf16[2,4,32,128]{3,2,1,0:T(8,128)(2,1)}, u32[]{:S(2)}) copy-start(bf16[2,4,32,128]{3,2,1,0:T(8,128)(2,1)} %top_ref.1) | copy-start | bytes 196612
  13.0 9.2 %copy-start.1 = (f32[2,128]{1,0:T(2,128)S(1)}, f32[2,128]{1,0:T(2,128)}, u32[]{:S(2)}) copy-start(f32[2,128]{1,0:T(2,128)} %gain_ref.3) | copy-start | bytes 3076
  13.0 9.1 %collective-permute-start.2 = (bf16[28,32,128]{2,1,0:T(8,128)(2,1)S(1)}, bf16[28,32,128]{2,1,0:T(8,128)(2,1)S(1)}, u32[]{:S(2)}, u32[]{:S(2)}) collective-permute-start(bf16[28,32,128]{2,1,0:T(8,128)(2,1)S(1)} %pad_maximum_fusion), channel_id=1, source_target_pairs={{1,0},{2,1},{3,2},{4,3},{5,4},{6,5},{7,6},{8,7},{9,8},{10,9},{11,1... | collective-permute-start | bytes 688136 | tf_op jit(solution)/shard_map/ppermute | solution.py:289
  24.7 6.2 %collective-permute-start.3 = (bf16[4,2,32,128]{3,2,1,0:T(8,128)(2,1)S(1)}, bf16[4,2,32,128]{3,2,1,0:T(8,128)(2,1)S(1)}, u32[]{:S(2)}, u32[]{:S(2)}) collective-permute-start(bf16[4,2,32,128]{3,2,1,0:T(8,128)(2,1)S(1)} %get-tuple-element.11.own_ref.grad_ref), channel_id=1, source_target_pairs={{32,0},{64,32},{96,64},{128,96},{160,128},{192,160},{224,192},{256... | collective-permute-start | bytes 196616 | tf_op jit(solution)/shard_map/ppermute | solution.py:286
  30.9 7.7 %collective-permute-start.4 = (bf16[2,4,32,128]{3,2,1,0:T(8,128)(2,1)S(1)}, bf16[2,4,32,128]{3,2,1,0:T(8,128)(2,1)S(1)}, u32[]{:S(2)}, u32[]{:S(2)}) collective-permute-start(bf16[2,4,32,128]{3,2,1,0:T(8,128)(2,1)S(1)} %shard_map.69), channel_id=1, source_target_pairs={{0,1},{1,2},{2,3},{3,4},{4,5},{5,6},{6,7},{7,8},{8,9},{9,10},{10,1... | collective-permute-start | bytes 196616 | tf_op jit(solution)/shard_map/ppermute | solution.py:292
  40.2 4.3 %collective-permute-start.7 = (bf16[16,54,4,128]{3,2,1,0:T(4,128)(2,1)S(1)}, bf16[16,54,4,128]{3,2,1,0:T(4,128)(2,1)S(1)}, u32[]{:S(2)}, u32[]{:S(2)}) collective-permute-start(bf16[16,54,4,128]{3,2,1,0:T(4,128)(2,1)S(1)} %get-tuple-element.18), channel_id=1, source_target_pairs={{0,1},{1,0},{2,3},{3,2},{4,5},{5,4},{6,7},{7,6},{8,9},{9,8},{10,11... | collective-permute-start | bytes 2654216 | tf_op jit(solution)/shard_map/ppermute | solution.py:295
  45.7 30.0 %all-to-all-start = ((bf16[16,216,128]{2,1,0:T(8,128)(2,1)}), bf16[16,216,128]{2,1,0:T(8,128)(2,1)S(1)}, u32[]{:S(2)}, u32[]{:S(2)}) async-start(bf16[16,216,128]{2,1,0:T(8,128)(2,1)} %shard_map.75), calls=%async_computation | async-start | bytes 1769472 | tf_op jit(solution)/shard_map/all_to_all | solution.py:368
  49.9 6.2 %collective-permute-start.5 = (bf16[4,2,32,128]{3,2,1,0:T(8,128)(2,1)S(1)}, bf16[4,2,32,128]{3,2,1,0:T(8,128)(2,1)S(1)}, u32[]{:S(2)}, u32[]{:S(2)}) collective-permute-start(bf16[4,2,32,128]{3,2,1,0:T(8,128)(2,1)S(1)} %shard_map.70.own_ref.grad_ref), channel_id=1, source_target_pairs={{32,0},{64,32},{96,64},{128,96},{160,128},{192,160},{224,192},{256... | collective-permute-start | bytes 196616 | tf_op jit(solution)/shard_map/ppermute | solution.py:286
  56.1 17.3 %collective-permute-start.6 = (bf16[2,4,32,128]{3,2,1,0:T(8,128)(2,1)S(1)}, bf16[2,4,32,128]{3,2,1,0:T(8,128)(2,1)S(1)}, u32[]{:S(2)}, u32[]{:S(2)}) collective-permute-start(bf16[2,4,32,128]{3,2,1,0:T(8,128)(2,1)S(1)} %shard_map.71), channel_id=1, source_target_pairs={{0,1},{1,2},{2,3},{3,4},{4,5},{5,6},{6,7},{7,8},{8,9},{9,10},{10,1... | collective-permute-start | bytes 196616 | tf_op jit(solution)/shard_map/ppermute | solution.py:292

commit v9 on v8

--- a/solution.py
+++ b/solution.py
@@ -100,57 +100,81 @@
     return lax.axis_index("tile") == lax.axis_size("tile") - 1
 
 
-def first_rows(parts, below_ref, total):
-    frames, rows = parts[0].shape[:2]
-    skipped = (3 - len(parts)) * frames
+def first_rows(own, below_ref, first_frame, total):
+    rows = own[0][0].shape[1]
     result = []
     for row in range(total):
         if row < rows:
-            result.append([part[frame, row] for part in parts for frame in range(frames)])
+            result.append([ref[frame, row] for ref, frame in own])
         else:
             result.append(
                 [
-                    below_ref[(skipped + frame) * rows + row - rows]
-                    for frame in range(len(parts) * frames)
+                    below_ref[(first_frame + index) * rows + row - rows]
+                    for index in range(len(own))
                 ]
             )
     return result
 
 
-def forward(
-    own_ref, earlier_ref, earliest_ref, below_ref, top_ref, first_kernel_ref, second_kernel_ref,
-    gain_ref, next_ref, pre_ref, grad_ref, wide_store, store,
+def core_step(
+    own_ref, earlier_ref, earliest_ref, later_ref, below_ref, above_ref, top_ref,
+    first_kernel_ref, second_kernel_ref, gain_ref, next_ref, second_grad_ref, first_grad_ref,
+    wide_store, next_store, store, wide_next, wide_grad, pre_ref,
 ):
     frames, rows, columns, _ = own_ref.shape
-    last = at_last_tile()
-    window = window_of(first_rows((earliest_ref, earlier_ref, own_ref), below_ref, 2 * rows))
-    wide, deep = 2 * rows - 2, 2 * frames
-    seams = {(rows - 2, 2): last, (rows - 1, 0): last}
-    store_columns(wide_store, window, (0, 1, 2), seams)
-    own_cells = frames * columns
-    for first in range(0, wide, 2):
-        pre_norm = product(wide_store, seams, (first, first + 1), deep, 1, first_kernel_ref)
+    first, last = lax.axis_index("tile") == 0, at_last_tile()
+    own = [
+        (ref, frame)
+        for ref in (earliest_ref, earlier_ref, own_ref, later_ref)
+        for frame in range(frames)
+    ]
+    deep = len(own)
+    window = [[above_ref[frame * 2 + row] for frame in range(deep)] for row in range(2)]
+    window += first_rows(own, below_ref, 0, 2 * rows)
+    seams = {(rows, 2): last, (rows + 1, 0): last, (0, 2): first, (1, 0): first}
+    store_columns(wide_store, window_of(window), (0, 1, 2), seams)
+    middle = deep - 2
+    for start in range(0, 2 * rows, 2):
+        pre_norm = product(wide_store, seams, (start, start + 1), middle, 1, first_kernel_ref)
         _, normed, sigma = silu_parts(pre_norm, gain_ref[0:1])
         value = (normed * sigma).astype(BF16)
-        for block in range(2 * deep):
-            row, frame = first + block // deep, block % deep
+        for block in range(2 * middle):
+            row, frame = start + block // middle, block % middle
             cells = slice(block * columns, (block + 1) * columns)
-            next_ref[row, frame] = value[cells]
-            if row < rows and frame >= frames:
-                start = row * own_cells + (frame - frames) * columns
-                pre_ref[start : start + columns] = pre_norm[cells]
-    seams = {(rows - 3, 2): last, (rows - 2, 0): last}
-    store_columns(store, window_of(block_rows(next_ref)), (0, 1, 2), seams)
-    pre_norm = product(store, seams, range(rows), frames, 1, second_kernel_ref)
-    spread = []
-    for row in range(rows):
-        for frame in range(frames):
-            if row < rows - 2:
-                spread.append(top_ref[frame, row + 2])
-            else:
-                spread.append(below_ref[3 * frames * rows + frame * 2 + row - rows + 2])
-    upstream = jnp.concatenate(spread, axis=0).astype(F32)
-    grad_ref[...] = pre_norm_gradient(pre_norm, gain_ref[1:2], upstream).reshape(grad_ref.shape)
+            wide_next[row, frame] = value[cells]
+            if row >= 2 and frame < 2 * frames:
+                next_ref[row - 2, frame] = value[cells]
+            if 2 <= row < rows + 2 and frames <= frame < 2 * frames:
+                place = ((row - 2) * frames + frame - frames) * columns
+                pre_ref[place : place + columns] = pre_norm[cells]
+    seams = {(rows - 1, 2): last, (rows, 0): last, (0, 0): first}
+    store_columns(next_store, window_of(block_rows(wide_next)), (0, 1, 2), seams)
+    spread = 2 * frames
+    for start in range(0, rows + 2, 2):
+        pre_norm = product(next_store, seams, (start, start + 1), spread, 1, second_kernel_ref)
+        upstream = []
+        for row in (start, start + 1):
+            for frame in range(spread):
+                if row >= rows:
+                    upstream.append(below_ref[deep * rows + frame * 2 + row - rows])
+                elif frame < frames:
+                    upstream.append(top_ref[frame, row])
+                else:
+                    upstream.append(later_ref[frame - frames, rows + row])
+        upstream = jnp.concatenate(upstream, axis=0).astype(F32)
+        grad = pre_norm_gradient(pre_norm, gain_ref[1:2], upstream)
+        for block in range(2 * spread):
+            row, frame = start + block // spread, block % spread
+            value = grad[block * columns : (block + 1) * columns]
+            wide_grad[row, frame] = value
+            if row >= 2 and frame < frames:
+                second_grad_ref[row - 2, frame] = value
+    seams = {(rows - 2, 2): last, (rows - 1, 0): last}
+    store_columns(store, window_of(block_rows(wide_grad)), (2, 1, 0), seams)
+    upstream = product(store, seams, range(rows), frames, -1, second_kernel_ref)
+    upstream = upstream.astype(BF16).astype(F32)
+    grad = pre_norm_gradient(pre_ref[...], gain_ref[0:1], upstream)
+    first_grad_ref[...] = grad.reshape(first_grad_ref.shape)
 
 
 def backward_rows(own_ref, later_ref, above_ref, frames):
@@ -164,18 +188,6 @@
             + [later_ref[row, frame] for frame in range(frames)]
         )
     return result
-
-
-def second_backward(
-    own_ref, later_ref, above_ref, kernel_ref, gain_ref, pre_ref, grad_ref, store
-):
-    rows, frames, _, _ = own_ref.shape
-    last = at_last_tile()
-    seams = {(rows - 2, 2): last, (rows - 1, 0): last}
-    window = window_of(backward_rows(own_ref, later_ref, above_ref, frames))
-    store_columns(store, window, (2, 1, 0), seams)
-    upstream = product(store, seams, range(rows), frames, -1, kernel_ref).astype(BF16).astype(F32)
-    grad_ref[...] = pre_norm_gradient(pre_ref[...], gain_ref[0:1], upstream).reshape(grad_ref.shape)
 
 
 def first_backward(own_ref, later_ref, above_ref, kernel_ref, out_ref, token_ref, store):
@@ -226,10 +238,29 @@
     rows = grad_ref.shape[0]
     last = at_last_tile()
     seams = {(rows - 2, 2): last, (rows - 1, 0): last}
-    window = window_of(first_rows((earlier_ref, own_ref), below_ref, rows + 2))
+    frames = own_ref.shape[0]
+    own = [(ref, frame) for ref in (earlier_ref, own_ref) for frame in range(frames)]
+    window = window_of(first_rows(own, below_ref, frames, rows + 2))
     store_columns(store, window, (0, 1, 2), seams)
     keep_ref[:, TAPS:], send_ref[:, TAPS:] = keep_second[...], send_second[...]
     split_gradient(store, seams, grad_ref, keep_ref, send_ref)
+
+
+def pack_inputs(
+    own_ref, earlier_ref, earliest_ref, later_ref, top_ref, below_ref, above_ref
+):
+    frames, rows = own_ref.shape[:2]
+    parts = (earliest_ref, earlier_ref, own_ref, later_ref)
+    for index, part in enumerate(parts):
+        for frame in range(frames):
+            place = index * frames + frame
+            below_ref[place * rows : (place + 1) * rows] = part[frame, :rows]
+            above_ref[place * 2 : (place + 1) * 2] = part[frame, rows - 2 : rows]
+    base = len(parts) * frames * rows
+    for frame in range(frames):
+        below_ref[base + frame * 2 : base + frame * 2 + 2] = top_ref[frame, :2]
+        place = base + (frames + frame) * 2
+        below_ref[place : place + 2] = later_ref[frame, rows : rows + 2]
 
 
 def pack_rows(own_ref, later_ref, out_ref):
@@ -295,31 +326,43 @@
         return lax.ppermute(value, "tile", [(i, i ^ 1) for i in range(tiles)])
 
     own_0 = (saved_codes.astype(F32) * saved_scales[..., None]).astype(BF16)
-    earlier_0, earliest_0 = next_frames(own_0, 1), next_frames(own_0, 2)
-    sent = jnp.concatenate(
-        [
-            earliest_0.reshape(frames * rows, *block),
-            earlier_0.reshape(frames * rows, *block),
-            own_0.reshape(frames * rows, *block),
-            cotangent[:, :2].reshape(frames * 2, *block),
-        ],
-        axis=0,
-    )
-    below = from_below(sent)
-    wide = 2 * rows - 2
-    grad_shape = shape_of(rows, frames, *block)
-    next_1, pre_0, grad_1 = call(
-        forward,
-        (shape_of(wide, 2 * frames, *block), shape_of(cells, channels, dtype=F32), grad_shape),
+    earliest_0, earlier_0 = next_frames(own_0, 2), next_frames(own_0, 1)
+    later = earlier_frames(jnp.concatenate([own_0, cotangent], axis=1))
+
+    count = 4 * frames
+    to_above, to_below = call(
+        pack_inputs,
+        (shape_of(count * rows + 4 * frames, *block), shape_of(2 * count, *block)),
         own_0,
         earlier_0,
         earliest_0,
+        later,
+        cotangent,
+    )
+    below, above = from_below(to_above), from_above(to_below)
+    wide, deep = 2 * rows, 3 * frames
+    grad_shape = shape_of(rows, frames, *block)
+    next_1, grad_1, grad_0 = call(
+        core_step,
+        (shape_of(wide - 2, 2 * frames, *block), grad_shape, grad_shape),
+        own_0,
+        earlier_0,
+        earliest_0,
+        later,
         below,
+        above,
         cotangent,
         kernels[0],
         kernels[1],
         norm_gains,
-        scratch=column_store(2 * rows, 3 * frames) + column_store(wide, 2 * frames),
+        scratch=column_store(wide + 4, 4 * frames)
+        + column_store(wide + 1, deep)
+        + column_store(rows + 2, 2 * frames)
+        + (
+            pltpu.VMEM((wide, deep, *block), BF16),
+            pltpu.VMEM((rows + 2, 2 * frames, *block), BF16),
+            pltpu.VMEM((cells, channels), F32),
+        ),
     )
 
     share = channels // tiles
@@ -332,23 +375,12 @@
         packed = call(pack_rows, shape_of(2, 2 * frames, *block), grad, later)
         return later, from_above(packed)
 
-    next_to = neighbours(grad_1)
     keep_1, send_1 = call(
         second_kernel_gradient,
         (part, part),
         next_1,
         grad_1,
-        scratch=column_store(wide, 2 * frames),
-    )
-    grad_0 = call(
-        second_backward,
-        grad_shape,
-        grad_1,
-        *next_to,
-        kernels[1],
-        norm_gains,
-        pre_0,
-        scratch=column_store(rows + 2, 2 * frames),
+        scratch=column_store(wide - 2, 2 * frames),
     )
     keep, send = call(
         first_kernel_gradient,

time: 102 us -> 98.8 us (0.969)
  waiting for transfers between devices: 35.2 us -> 30.9 us
  Pallas kernels: 8.28 us -> 11 us
  blocking collectives: 24.7 us -> 22.5 us
    ppermute x2, starting transfers between devices: 4.1 us -> 9.71 us  [earlier_frames(): return lax.ppermute(value, 'frame', [(i + 1, i) for i in range(groups - 1)])]
    ppermute x2, starting transfers between devices: 9.43 us -> 4.49 us  [next_frames(): lax.ppermute(value, 'frame', [(i, i + steps) for i in range(groups - step...]
    ppermute x2, waiting for transfers between devices: 8.37 us -> 4.28 us  [earlier_frames(): return lax.ppermute(value, 'frame', [(i + 1, i) for i in range(groups - 1)])]
    pallas_call x10 -> x9, Pallas kernels: 8.28 us -> 11 us  [call(): pl.pallas_call(kernel, out_shape=out_shape, scratch_shapes=list(scratch),...]
    all_to_all x1, blocking collectives: 24.7 us -> 22.5 us  [local(): spread = lax.all_to_all(by_frame, 'frame', 0, 0, tiled=True)]
    ppermute x1, waiting for transfers between devices: 1.92 us -> 0.01 us  [from_below(): lax.ppermute(value, 'tile', [((i + 1) % tiles, i) for i in range(tiles)])]
    ppermute x2, waiting for transfers between devices: 1.12 us -> 2.95 us  [next_frames(): lax.ppermute(value, 'frame', [(i, i + steps) for i in range(groups - step...]
    ppermute x1, starting transfers between devices: 5.62 us -> 4.14 us  [from_below(): lax.ppermute(value, 'tile', [((i + 1) % tiles, i) for i in range(tiles)])]
  transfers between devices with their start and end apart: 9 -> 9, of which waited for: 8 -> 6; matrix products, arithmetic and copies ran while one was open for 2% -> 2% of each run, Pallas kernels for 2% -> 1%
where the time goes in v9:
time: 98.8 us; the launch traced here: 98.2 us
  waiting for transfers between devices  30.9 us (31%)
  starting transfers between devices  28.8 us (29%)
  blocking collectives  22.5 us (23%)
  Pallas kernels  11 us (11%)
  local copies, waits for them, and re-layouts  2.44 us (2%)
  other arithmetic  1.8 us (2%)
    all_to_all x1, blocking collectives, local(): spread = lax.all_to_all(by_frame, 'frame', 0, 0, tiled=True)  22.5 us
    ppermute x2, waiting for transfers between devices, from_above(): lax.ppermute(value, 'tile', [(i, (i + 1) % tiles) for i in range(tiles)])  20.3 us
    pallas_call x9, Pallas kernels, call(): pl.pallas_call(kernel, out_shape=out_shape, scratch_shapes=list(scratch),...  11 us
    ppermute x2, starting transfers between devices, earlier_frames(): return lax.ppermute(value, 'frame', [(i + 1, i) for i in range(groups - 1)])  9.71 us
    all_to_all x1, starting transfers between devices, local(): lax.all_to_all(paired, 'tile', 0, 0, tiled=True, axis_index_groups=by_core)  4.67 us
    ppermute x2, starting transfers between devices, next_frames(): lax.ppermute(value, 'frame', [(i, i + steps) for i in range(groups - step...  4.49 us
    ppermute x2, waiting for transfers between devices, earlier_frames(): return lax.ppermute(value, 'frame', [(i + 1, i) for i in range(groups - 1)])  4.28 us
    ppermute x1, starting transfers between devices, from_below(): lax.ppermute(value, 'tile', [((i + 1) % tiles, i) for i in range(tiles)])  4.14 us
  transfers between devices with their start and end apart: 9, of which 6 were waited for; matrix products, arithmetic and copies ran while one was open for 2% of the time, Pallas kernels for 1%

profile of v9, /device:TPU:2, one launch (start us, length us, event | category | flops | bytes accessed | tf_op | source)
XLA Modules:
  0.0 98.2 jit_solution(17055237284144965754)
XLA Ops:
  0.6 0.9 multiply_convert_fusion.own_ref
  1.6 0.9 pad_maximum_fusion
  2.4 7.8 %collective-permute-start.2 = (bf16[2,8,32,128]{3,2,1,0:T(8,128)(2,1)S(1)}, bf16[2,8,32,128]{3,2,1,0:T(8,128)(2,1)S(1)}, u32[]{:S(2)}, u32[]{:S(2)}) collective-permute-start(bf16[2,8,32,128]{3,2,1,0:T(8,128)(2,1)S(1)} %pad_maximum_fusion), channel_id=1, source_target_pairs={{32,0},{64,32},{96,64},{128,96},{160,128},{192,160},{224,192},{256... | collective-permute-start | bytes 393224 | tf_op jit(solution)/shard_map/ppermute | solution.py:317
  10.2 1.3 %collective-permute-start.1 = (bf16[2,4,32,128]{3,2,1,0:T(8,128)(2,1)S(1)}, bf16[2,4,32,128]{3,2,1,0:T(8,128)(2,1)S(1)}, u32[]{:S(2)}, u32[]{:S(2)}) collective-permute-start(bf16[2,4,32,128]{3,2,1,0:T(8,128)(2,1)S(1)} %multiply_convert_fusion.own_ref), channel_id=1, source_target_pairs={{0,64},{32,96},{64,128},{96,160},{128,192},{160,224},{192,256},{22... | collective-permute-start | bytes 196616 | tf_op jit(solution)/shard_map/ppermute | solution.py:314
  11.5 3.2 %collective-permute-start = (bf16[2,4,32,128]{3,2,1,0:T(8,128)(2,1)S(1)}, bf16[2,4,32,128]{3,2,1,0:T(8,128)(2,1)S(1)}, u32[]{:S(2)}, u32[]{:S(2)}) collective-permute-start(bf16[2,4,32,128]{3,2,1,0:T(8,128)(2,1)S(1)} %multiply_convert_fusion.own_ref), channel_id=1, source_target_pairs={{0,32},{32,64},{64,96},{96,128},{128,160},{160,192},{192,224},{224... | collective-permute-start | bytes 196616 | tf_op jit(solution)/shard_map/ppermute | solution.py:314
  14.7 0.0 collective-permute-done.1.earliest_ref
  14.7 2.9 %collective-permute-done.earlier_ref = bf16[2,4,32,128]{3,2,1,0:T(8,128)(2,1)S(1)} collective-permute-done((bf16[2,4,32,128]{3,2,1,0:T(8,128)(2,1)S(1)}, bf16[2,4,32,128]{3,2,1,0:T(8,128)(2,1)S(1)}, u32[]{:S(2)}, u32[]{:S(2)}) %collective-permute-start) | collective-permute-done | bytes 65568 | tf_op jit(solution)/shard_map/ppermute | solution.py:314
  17.7 0.0 collective-permute-done.2.later_ref
  17.7 0.0 copy-start
  17.7 0.8 copy-done
  18.6 4.1 %collective-permute-start.3 = (bf16[40,32,128]{2,1,0:T(8,128)(2,1)S(1)}, bf16[40,32,128]{2,1,0:T(8,128)(2,1)S(1)}, u32[]{:S(2)}, u32[]{:S(2)}) collective-permute-start(bf16[40,32,128]{2,1,0:T(8,128)(2,1)S(1)} %get-tuple-element.13), channel_id=1, source_target_pairs={{1,0},{2,1},{3,2},{4,3},{5,4},{6,5},{7,6},{8,7},{9,8},{10,9},{11,1... | collective-permute-start | bytes 983048 | tf_op jit(solution)/shard_map/ppermute | solution.py:320
  22.7 0.0 copy-start.1
  22.7 1.9 %collective-permute-start.4 = (bf16[16,32,128]{2,1,0:T(8,128)(2,1)S(1)}, bf16[16,32,128]{2,1,0:T(8,128)(2,1)S(1)}, u32[]{:S(2)}, u32[]{:S(2)}) collective-permute-start(bf16[16,32,128]{2,1,0:T(8,128)(2,1)S(1)} %get-tuple-element.14), channel_id=1, source_target_pairs={{0,1},{1,2},{2,3},{3,4},{4,5},{5,6},{6,7},{7,8},{8,9},{9,10},{10,1... | collective-permute-start | bytes 393224 | tf_op jit(solution)/shard_map/ppermute | solution.py:323
  24.7 1.6 %slice_bitcast_fusion = (bf16[27,128,128]{2,1,0:T(8,128)(2,1)S(1)}, bf16[27,128,128]{2,1,0:T(8,128)(2,1)S(1)}) fusion(bf16[2,27,128,128]{3,2,1,0:T(8,128)(2,1)} %param.7), kind=kLoop, calls=%fused_computation | loop fusion | bytes 3538944 | tf_op jit(solution)/shard_map/squeeze | solution.py:356
  26.3 4.9 %collective-permute-done.4.above_ref = bf16[16,32,128]{2,1,0:T(8,128)(2,1)S(1)} collective-permute-done((bf16[16,32,128]{2,1,0:T(8,128)(2,1)S(1)}, bf16[16,32,128]{2,1,0:T(8,128)(2,1)S(1)}, u32[]{:S(2)}, u32[]{:S(2)}) %collective-permute-start.4) | collective-permute-done | bytes 131104 | tf_op jit(solution)/shard_map/ppermute | solution.py:323
  31.1 0.0 collective-permute-done.3.below_ref
  31.1 0.0 copy-done.1
  31.2 6.0 %shard_map.69 = (bf16[6,4,32,128]{3,2,1,0:T(8,128)(2,1)S(1)}, bf16[4,2,32,128]{3,2,1,0:T(8,128)(2,1)S(1)}, bf16[4,2,32,128]{3,2,1,0:T(8,128)(2,1)S(1)}) custom-call(bf16[2,4,32,128]{3,2,1,0:T(8,128)(2,1)S(1)} %multiply_convert_fusion.own_ref, bf16[2,4,32,128]{3,2,1,0:T(8,128)(2,1)S(1)} %collective-permute-done.earlier_ref, ...), custom_call_target="tpu_custom_call" | custom-call | tf_op jit(solution)/shard_map/pallas_call | solution.py:18
  37.2 0.7 shard_map.72
  37.9 0.9 shard_map.73
  38.8 1.9 %collective-permute-start.7 = (bf16[16,54,4,128]{3,2,1,0:T(4,128)(2,1)S(1)}, bf16[16,54,4,128]{3,2,1,0:T(4,128)(2,1)S(1)}, u32[]{:S(2)}, u32[]{:S(2)}) collective-permute-start(bf16[16,54,4,128]{3,2,1,0:T(4,128)(2,1)S(1)} %get-tuple-element.22), channel_id=1, source_target_pairs={{0,1},{1,0},{2,3},{3,2},{4,5},{5,4},{6,7},{7,6},{8,9},{9,8},{10,11... | collective-permute-start | bytes 2654216 | tf_op jit(solution)/shard_map/ppermute | solution.py:326
  40.7 2.4 %collective-permute-done.7 = bf16[16,54,4,128]{3,2,1,0:T(4,128)(2,1)S(1)} collective-permute-done((bf16[16,54,4,128]{3,2,1,0:T(4,128)(2,1)S(1)}, bf16[16,54,4,128]{3,2,1,0:T(4,128)(2,1)S(1)}, u32[]{:S(2)}, u32[]{:S(2)}) %collective-permute-start.7) | collective-permute-done | bytes 884768 | tf_op jit(solution)/shard_map/ppermute | solution.py:326
  43.1 1.1 %shard_map.74 = bf16[16,216,128]{2,1,0:T(8,128)(2,1)} custom-call(bf16[16,216,128]{2,1,0:T(8,128)(2,1)S(1)} %bitcast.7, bf16[16,216,128]{2,1,0:T(8,128)(2,1)S(1)} %bitcast.8), custom_call_target="tpu_custom_call" | custom-call | tf_op jit(solution)/shard_map/pallas_call | solution.py:18
  44.2 4.7 %all-to-all-start = ((bf16[16,216,128]{2,1,0:T(8,128)(2,1)}), bf16[16,216,128]{2,1,0:T(8,128)(2,1)S(1)}, u32[]{:S(2)}, u32[]{:S(2)}) async-start(bf16[16,216,128]{2,1,0:T(8,128)(2,1)} %shard_map.74), calls=%async_computation | async-start | bytes 1769472 | tf_op jit(solution)/shard_map/all_to_all | solution.py:400
  48.9 1.9 %collective-permute-start.5 = (bf16[4,2,32,128]{3,2,1,0:T(8,128)(2,1)S(1)}, bf16[4,2,32,128]{3,2,1,0:T(8,128)(2,1)S(1)}, u32[]{:S(2)}, u32[]{:S(2)}) collective-permute-start(bf16[4,2,32,128]{3,2,1,0:T(8,128)(2,1)S(1)} %get-tuple-element.15.own_ref.grad_ref), channel_id=1, source_target_pairs={{32,0},{64,32},{96,64},{128,96},{160,128},{192,160},{224,192},{256... | collective-permute-start | bytes 196616 | tf_op jit(solution)/shard_map/ppermute | solution.py:317
  50.8 4.3 %collective-permute-done.5.later_ref = bf16[4,2,32,128]{3,2,1,0:T(8,128)(2,1)S(1)} collective-permute-done((bf16[4,2,32,128]{3,2,1,0:T(8,128)(2,1)S(1)}, bf16[4,2,32,128]{3,2,1,0:T(8,128)(2,1)S(1)}, u32[]{:S(2)}, u32[]{:S(2)}) %collective-permute-start.5) | collective-permute-done | bytes 65568 | tf_op jit(solution)/shard_map/ppermute | solution.py:317
  55.1 1.9 %collective-permute-start.6 = (bf16[2,4,32,128]{3,2,1,0:T(8,128)(2,1)S(1)}, bf16[2,4,32,128]{3,2,1,0:T(8,128)(2,1)S(1)}, u32[]{:S(2)}, u32[]{:S(2)}) collective-permute-start(bf16[2,4,32,128]{3,2,1,0:T(8,128)(2,1)S(1)} %shard_map.70), channel_id=1, source_target_pairs={{0,1},{1,2},{2,3},{3,4},{4,5},{5,6},{6,7},{7,8},{8,9},{9,10},{10,1... | collective-permute-start | bytes 196616 | tf_op jit(solution)/shard_map/ppermute | solution.py:323
  57.0 15.4 %collective-permute-done.6.above_ref = bf16[2,4,32,128]{3,2,1,0:T(8,128)(2,1)S(1)} collective-permute-done((bf16[2,4,32,128]{3,2,1,0:T(8,128)(2,1)S(1)}, bf16[2,4,32,128]{3,2,1,0:T(8,128)(2,1)S(1)}, u32[]{:S(2)}, u32[]{:S(2)}) %collective-permute-start.6) | collective-permute-done | bytes 65568 | tf_op jit(solution)/shard_map/ppermute | solution.py:323
  72.5 1.3 %shard_map.71 = (bf16[2,4,32,128]{3,2,1,0:T(8,128)(2,1)}, f32[8,128]{1,0:T(8,128)S(1)}) custom-call(bf16[4,2,32,128]{3,2,1,0:T(8,128)(2,1)S(1)} %get-tuple-element.15.own_ref.grad_ref, bf16[4,2,32,128]{3,2,1,0:T(8,128)(2,1)S(1)} %collective-permute-done.5.later_ref, bf16[2,4,32,128]{3,2,1,0:T(8,128)(2,1)S(1)} %collective-permute-done.6.above_ref, ...), custom_call_target="tpu_custom_call" | custom-call | tf_op jit(solution)/shard_map/pallas_call | solution.py:18
  73.8 1.0 all-to-all-done.refs_0_
  74.7 0.3 shard_map.75
  75.0 22.5 %all_to_all.10.refs_0_ = bf16[16,8,256]{2,1,0:T(8,128)(2,1)S(1)} all-to-all(bf16[16,8,256]{2,1,0:T(8,128)(2,1)S(1)} %shard_map.75), channel_id=1, replica_groups=mesh['frame'=16,'tile'=32] {'frame'}, dimensions={0} | all-to-all | bytes 131072 | tf_op jit(solution)/shard_map/all_to_all | solution.py:418
  97.5 0.7 shard_map.76
  (2 shorter events, 0.1 us)
Async XLA Ops:
  2.4 15.3 %collective-permute-start.2 = (bf16[2,8,32,128]{3,2,1,0:T(8,128)(2,1)S(1)}, bf16[2,8,32,128]{3,2,1,0:T(8,128)(2,1)S(1)}, u32[]{:S(2)}, u32[]{:S(2)}) collective-permute-start(bf16[2,8,32,128]{3,2,1,0:T(8,128)(2,1)S(1)} %pad_maximum_fusion), channel_id=1, source_target_pairs={{32,0},{64,32},{96,64},{128,96},{160,128},{192,160},{224,192},{256... | collective-permute-start | bytes 393224 | tf_op jit(solution)/shard_map/ppermute | solution.py:317
  10.2 4.5 %collective-permute-start.1 = (bf16[2,4,32,128]{3,2,1,0:T(8,128)(2,1)S(1)}, bf16[2,4,32,128]{3,2,1,0:T(8,128)(2,1)S(1)}, u32[]{:S(2)}, u32[]{:S(2)}) collective-permute-start(bf16[2,4,32,128]{3,2,1,0:T(8,128)(2,1)S(1)} %multiply_convert_fusion.own_ref), channel_id=1, source_target_pairs={{0,64},{32,96},{64,128},{96,160},{128,192},{160,224},{192,256},{22... | collective-permute-start | bytes 196616 | tf_op jit(solution)/shard_map/ppermute | solution.py:314
  11.5 6.2 %collective-permute-start = (bf16[2,4,32,128]{3,2,1,0:T(8,128)(2,1)S(1)}, bf16[2,4,32,128]{3,2,1,0:T(8,128)(2,1)S(1)}, u32[]{:S(2)}, u32[]{:S(2)}) collective-permute-start(bf16[2,4,32,128]{3,2,1,0:T(8,128)(2,1)S(1)} %multiply_convert_fusion.own_ref), channel_id=1, source_target_pairs={{0,32},{32,64},{64,96},{96,128},{128,160},{160,192},{192,224},{224... | collective-permute-start | bytes 196616 | tf_op jit(solution)/shard_map/ppermute | solution.py:314
  17.7 0.8 copy-start
  18.6 12.6 %collective-permute-start.3 = (bf16[40,32,128]{2,1,0:T(8,128)(2,1)S(1)}, bf16[40,32,128]{2,1,0:T(8,128)(2,1)S(1)}, u32[]{:S(2)}, u32[]{:S(2)}) collective-permute-start(bf16[40,32,128]{2,1,0:T(8,128)(2,1)S(1)} %get-tuple-element.13), channel_id=1, source_target_pairs={{1,0},{2,1},{3,2},{4,3},{5,4},{6,5},{7,6},{8,7},{9,8},{10,9},{11,1... | collective-permute-start | bytes 983048 | tf_op jit(solution)/shard_map/ppermute | solution.py:320
  22.7 8.4 %copy-start.1 = (f32[2,128]{1,0:T(2,128)S(1)}, f32[2,128]{1,0:T(2,128)}, u32[]{:S(2)}) copy-start(f32[2,128]{1,0:T(2,128)} %gain_ref.1) | copy-start | bytes 3076
  22.7 8.4 %collective-permute-start.4 = (bf16[16,32,128]{2,1,0:T(8,128)(2,1)S(1)}, bf16[16,32,128]{2,1,0:T(8,128)(2,1)S(1)}, u32[]{:S(2)}, u32[]{:S(2)}) collective-permute-start(bf16[16,32,128]{2,1,0:T(8,128)(2,1)S(1)} %get-tuple-element.14), channel_id=1, source_target_pairs={{0,1},{1,2},{2,3},{3,4},{4,5},{5,6},{6,7},{7,8},{8,9},{9,10},{10,1... | collective-permute-start | bytes 393224 | tf_op jit(solution)/shard_map/ppermute | solution.py:323
  38.8 4.3 %collective-permute-start.7 = (bf16[16,54,4,128]{3,2,1,0:T(4,128)(2,1)S(1)}, bf16[16,54,4,128]{3,2,1,0:T(4,128)(2,1)S(1)}, u32[]{:S(2)}, u32[]{:S(2)}) collective-permute-start(bf16[16,54,4,128]{3,2,1,0:T(4,128)(2,1)S(1)} %get-tuple-element.22), channel_id=1, source_target_pairs={{0,1},{1,0},{2,3},{3,2},{4,5},{5,4},{6,7},{7,6},{8,9},{9,8},{10,11... | collective-permute-start | bytes 2654216 | tf_op jit(solution)/shard_map/ppermute | solution.py:326
  44.2 30.5 %all-to-all-start = ((bf16[16,216,128]{2,1,0:T(8,128)(2,1)}), bf16[16,216,128]{2,1,0:T(8,128)(2,1)S(1)}, u32[]{:S(2)}, u32[]{:S(2)}) async-start(bf16[16,216,128]{2,1,0:T(8,128)(2,1)} %shard_map.74), calls=%async_computation | async-start | bytes 1769472 | tf_op jit(solution)/shard_map/all_to_all | solution.py:400
  48.9 6.2 %collective-permute-start.5 = (bf16[4,2,32,128]{3,2,1,0:T(8,128)(2,1)S(1)}, bf16[4,2,32,128]{3,2,1,0:T(8,128)(2,1)S(1)}, u32[]{:S(2)}, u32[]{:S(2)}) collective-permute-start(bf16[4,2,32,128]{3,2,1,0:T(8,128)(2,1)S(1)} %get-tuple-element.15.own_ref.grad_ref), channel_id=1, source_target_pairs={{32,0},{64,32},{96,64},{128,96},{160,128},{192,160},{224,192},{256... | collective-permute-start | bytes 196616 | tf_op jit(solution)/shard_map/ppermute | solution.py:317
  55.1 17.3 %collective-permute-start.6 = (bf16[2,4,32,128]{3,2,1,0:T(8,128)(2,1)S(1)}, bf16[2,4,32,128]{3,2,1,0:T(8,128)(2,1)S(1)}, u32[]{:S(2)}, u32[]{:S(2)}) collective-permute-start(bf16[2,4,32,128]{3,2,1,0:T(8,128)(2,1)S(1)} %shard_map.70), channel_id=1, source_target_pairs={{0,1},{1,2},{2,3},{3,4},{4,5},{5,6},{6,7},{7,8},{8,9},{9,10},{10,1... | collective-permute-start | bytes 196616 | tf_op jit(solution)/shard_map/ppermute | solution.py:323

commit v10 on v9

--- a/solution.py
+++ b/solution.py
@@ -117,7 +117,7 @@
 
 
 def core_step(
-    own_ref, earlier_ref, earliest_ref, later_ref, below_ref, above_ref, top_ref,
+    own_ref, earlier_ref, earliest_ref, later_ref, below_ref, above_ref, joined_ref,
     first_kernel_ref, second_kernel_ref, gain_ref, next_ref, second_grad_ref, first_grad_ref,
     wide_store, next_store, store, wide_next, wide_grad, pre_ref,
 ):
@@ -158,7 +158,7 @@
                 if row >= rows:
                     upstream.append(below_ref[deep * rows + frame * 2 + row - rows])
                 elif frame < frames:
-                    upstream.append(top_ref[frame, row])
+                    upstream.append(joined_ref[frame, rows + row])
                 else:
                     upstream.append(later_ref[frame - frames, rows + row])
         upstream = jnp.concatenate(upstream, axis=0).astype(F32)
@@ -247,7 +247,7 @@
 
 
 def pack_inputs(
-    own_ref, earlier_ref, earliest_ref, later_ref, top_ref, below_ref, above_ref
+    own_ref, earlier_ref, earliest_ref, later_ref, joined_ref, below_ref, above_ref
 ):
     frames, rows = own_ref.shape[:2]
     parts = (earliest_ref, earlier_ref, own_ref, later_ref)
@@ -258,7 +258,7 @@
             above_ref[place * 2 : (place + 1) * 2] = part[frame, rows - 2 : rows]
     base = len(parts) * frames * rows
     for frame in range(frames):
-        below_ref[base + frame * 2 : base + frame * 2 + 2] = top_ref[frame, :2]
+        below_ref[base + frame * 2 : base + frame * 2 + 2] = joined_ref[frame, rows : rows + 2]
         place = base + (frames + frame) * 2
         below_ref[place : place + 2] = later_ref[frame, rows : rows + 2]
 
@@ -326,8 +326,10 @@
         return lax.ppermute(value, "tile", [(i, i ^ 1) for i in range(tiles)])
 
     own_0 = (saved_codes.astype(F32) * saved_scales[..., None]).astype(BF16)
-    earliest_0, earlier_0 = next_frames(own_0, 2), next_frames(own_0, 1)
-    later = earlier_frames(jnp.concatenate([own_0, cotangent], axis=1))
+    joined = jnp.concatenate([own_0, cotangent], axis=1)
+    earliest_0 = next_frames(own_0, 2)
+    earlier_0 = next_frames(own_0, 1)
+    later = earlier_frames(joined)
 
     count = 4 * frames
     to_above, to_below = call(
@@ -337,7 +339,7 @@
         earlier_0,
         earliest_0,
         later,
-        cotangent,
+        joined,
     )
     below, above = from_below(to_above), from_above(to_below)
     wide, deep = 2 * rows, 3 * frames
@@ -351,7 +353,7 @@
         later,
         below,
         above,
-        cotangent,
+        joined,
         kernels[0],
         kernels[1],
         norm_gains,

time: 98.8 us -> 97.9 us (level)
  no operation moved by 1% of the time
where the time goes in v10:
time: 97.9 us; the launch traced here: 97.4 us
  waiting for transfers between devices  30.9 us (32%)
  starting transfers between devices  28.8 us (29%)
  blocking collectives  22.5 us (23%)
  Pallas kernels  11.1 us (11%)
  other arithmetic  1.8 us (2%)
  local copies, waits for them, and re-layouts  1.6 us (2%)
    all_to_all x1, blocking collectives, local(): spread = lax.all_to_all(by_frame, 'frame', 0, 0, tiled=True)  22.5 us
    ppermute x2, waiting for transfers between devices, from_above(): lax.ppermute(value, 'tile', [(i, (i + 1) % tiles) for i in range(tiles)])  20.3 us
    pallas_call x9, Pallas kernels, call(): pl.pallas_call(kernel, out_shape=out_shape, scratch_shapes=list(scratch),...  11.1 us
    ppermute x2, starting transfers between devices, earlier_frames(): return lax.ppermute(value, 'frame', [(i + 1, i) for i in range(groups - 1)])  9.71 us
    all_to_all x1, starting transfers between devices, local(): lax.all_to_all(paired, 'tile', 0, 0, tiled=True, axis_index_groups=by_core)  4.68 us
    ppermute x2, starting transfers between devices, next_frames(): lax.ppermute(value, 'frame', [(i, i + steps) for i in range(groups - step...  4.49 us
    ppermute x2, waiting for transfers between devices, earlier_frames(): return lax.ppermute(value, 'frame', [(i + 1, i) for i in range(groups - 1)])  4.28 us
    ppermute x1, starting transfers between devices, from_below(): lax.ppermute(value, 'tile', [((i + 1) % tiles, i) for i in range(tiles)])  4.14 us
  transfers between devices with their start and end apart: 9, of which 6 were waited for; matrix products, arithmetic and copies ran while one was open for 2% of the time, Pallas kernels for 1%

profile of v10, /device:TPU:2, one launch (start us, length us, event | category | flops | bytes accessed | tf_op | source)
XLA Modules:
  0.0 97.4 jit_solution(16917478798525966912)
XLA Ops:
  0.6 0.9 multiply_convert_fusion.own_ref
  1.6 0.9 pad_maximum_fusion.joined_ref
  2.4 7.8 %collective-permute-start.2 = (bf16[2,8,32,128]{3,2,1,0:T(8,128)(2,1)S(1)}, bf16[2,8,32,128]{3,2,1,0:T(8,128)(2,1)S(1)}, u32[]{:S(2)}, u32[]{:S(2)}) collective-permute-start(bf16[2,8,32,128]{3,2,1,0:T(8,128)(2,1)S(1)} %pad_maximum_fusion.joined_ref), channel_id=1, source_target_pairs={{32,0},{64,32},{96,64},{128,96},{160,128},{192,160},{224,192},{256... | collective-permute-start | bytes 393224 | tf_op jit(solution)/shard_map/ppermute | solution.py:317
  10.2 1.3 %collective-permute-start.1 = (bf16[2,4,32,128]{3,2,1,0:T(8,128)(2,1)S(1)}, bf16[2,4,32,128]{3,2,1,0:T(8,128)(2,1)S(1)}, u32[]{:S(2)}, u32[]{:S(2)}) collective-permute-start(bf16[2,4,32,128]{3,2,1,0:T(8,128)(2,1)S(1)} %multiply_convert_fusion.own_ref), channel_id=1, source_target_pairs={{0,64},{32,96},{64,128},{96,160},{128,192},{160,224},{192,256},{22... | collective-permute-start | bytes 196616 | tf_op jit(solution)/shard_map/ppermute | solution.py:314
  11.5 3.2 %collective-permute-start = (bf16[2,4,32,128]{3,2,1,0:T(8,128)(2,1)S(1)}, bf16[2,4,32,128]{3,2,1,0:T(8,128)(2,1)S(1)}, u32[]{:S(2)}, u32[]{:S(2)}) collective-permute-start(bf16[2,4,32,128]{3,2,1,0:T(8,128)(2,1)S(1)} %multiply_convert_fusion.own_ref), channel_id=1, source_target_pairs={{0,32},{32,64},{64,96},{96,128},{128,160},{160,192},{192,224},{224... | collective-permute-start | bytes 196616 | tf_op jit(solution)/shard_map/ppermute | solution.py:314
  14.7 0.0 collective-permute-done.1.earliest_ref
  14.7 2.9 %collective-permute-done.earlier_ref = bf16[2,4,32,128]{3,2,1,0:T(8,128)(2,1)S(1)} collective-permute-done((bf16[2,4,32,128]{3,2,1,0:T(8,128)(2,1)S(1)}, bf16[2,4,32,128]{3,2,1,0:T(8,128)(2,1)S(1)}, u32[]{:S(2)}, u32[]{:S(2)}) %collective-permute-start) | collective-permute-done | bytes 65568 | tf_op jit(solution)/shard_map/ppermute | solution.py:314
  17.7 0.0 collective-permute-done.2.later_ref
  17.7 0.1 shard_map.68
  17.8 4.1 %collective-permute-start.3 = (bf16[40,32,128]{2,1,0:T(8,128)(2,1)S(1)}, bf16[40,32,128]{2,1,0:T(8,128)(2,1)S(1)}, u32[]{:S(2)}, u32[]{:S(2)}) collective-permute-start(bf16[40,32,128]{2,1,0:T(8,128)(2,1)S(1)} %get-tuple-element.13), channel_id=1, source_target_pairs={{1,0},{2,1},{3,2},{4,3},{5,4},{6,5},{7,6},{8,7},{9,8},{10,9},{11,1... | collective-permute-start | bytes 983048 | tf_op jit(solution)/shard_map/ppermute | solution.py:320
  21.9 0.0 copy-start
  21.9 1.9 %collective-permute-start.4 = (bf16[16,32,128]{2,1,0:T(8,128)(2,1)S(1)}, bf16[16,32,128]{2,1,0:T(8,128)(2,1)S(1)}, u32[]{:S(2)}, u32[]{:S(2)}) collective-permute-start(bf16[16,32,128]{2,1,0:T(8,128)(2,1)S(1)} %get-tuple-element.14), channel_id=1, source_target_pairs={{0,1},{1,2},{2,3},{3,4},{4,5},{5,6},{6,7},{7,8},{8,9},{9,10},{10,1... | collective-permute-start | bytes 393224 | tf_op jit(solution)/shard_map/ppermute | solution.py:323
  23.8 1.6 %slice_bitcast_fusion = (bf16[27,128,128]{2,1,0:T(8,128)(2,1)S(1)}, bf16[27,128,128]{2,1,0:T(8,128)(2,1)S(1)}) fusion(bf16[2,27,128,128]{3,2,1,0:T(8,128)(2,1)} %param.7), kind=kLoop, calls=%fused_computation | loop fusion | bytes 3538944 | tf_op jit(solution)/shard_map/squeeze | solution.py:358
  25.4 4.9 %collective-permute-done.4.above_ref = bf16[16,32,128]{2,1,0:T(8,128)(2,1)S(1)} collective-permute-done((bf16[16,32,128]{2,1,0:T(8,128)(2,1)S(1)}, bf16[16,32,128]{2,1,0:T(8,128)(2,1)S(1)}, u32[]{:S(2)}, u32[]{:S(2)}) %collective-permute-start.4) | collective-permute-done | bytes 131104 | tf_op jit(solution)/shard_map/ppermute | solution.py:323
  30.3 0.0 collective-permute-done.3.below_ref
  30.3 0.0 copy-done
  30.3 6.0 %shard_map.69 = (bf16[6,4,32,128]{3,2,1,0:T(8,128)(2,1)S(1)}, bf16[4,2,32,128]{3,2,1,0:T(8,128)(2,1)S(1)}, bf16[4,2,32,128]{3,2,1,0:T(8,128)(2,1)S(1)}) custom-call(bf16[2,4,32,128]{3,2,1,0:T(8,128)(2,1)S(1)} %multiply_convert_fusion.own_ref, bf16[2,4,32,128]{3,2,1,0:T(8,128)(2,1)S(1)} %collective-permute-done.earlier_ref, ...), custom_call_target="tpu_custom_call" | custom-call | tf_op jit(solution)/shard_map/pallas_call | solution.py:18
  36.3 0.7 shard_map.72
  37.1 0.9 shard_map.73
  37.9 1.9 %collective-permute-start.7 = (bf16[16,54,4,128]{3,2,1,0:T(4,128)(2,1)S(1)}, bf16[16,54,4,128]{3,2,1,0:T(4,128)(2,1)S(1)}, u32[]{:S(2)}, u32[]{:S(2)}) collective-permute-start(bf16[16,54,4,128]{3,2,1,0:T(4,128)(2,1)S(1)} %get-tuple-element.22), channel_id=1, source_target_pairs={{0,1},{1,0},{2,3},{3,2},{4,5},{5,4},{6,7},{7,6},{8,9},{9,8},{10,11... | collective-permute-start | bytes 2654216 | tf_op jit(solution)/shard_map/ppermute | solution.py:326
  39.9 2.4 %collective-permute-done.7 = bf16[16,54,4,128]{3,2,1,0:T(4,128)(2,1)S(1)} collective-permute-done((bf16[16,54,4,128]{3,2,1,0:T(4,128)(2,1)S(1)}, bf16[16,54,4,128]{3,2,1,0:T(4,128)(2,1)S(1)}, u32[]{:S(2)}, u32[]{:S(2)}) %collective-permute-start.7) | collective-permute-done | bytes 884768 | tf_op jit(solution)/shard_map/ppermute | solution.py:326
  42.3 1.1 %shard_map.74 = bf16[16,216,128]{2,1,0:T(8,128)(2,1)} custom-call(bf16[16,216,128]{2,1,0:T(8,128)(2,1)S(1)} %bitcast.7, bf16[16,216,128]{2,1,0:T(8,128)(2,1)S(1)} %bitcast.8), custom_call_target="tpu_custom_call" | custom-call | tf_op jit(solution)/shard_map/pallas_call | solution.py:18
  43.4 4.7 %all-to-all-start = ((bf16[16,216,128]{2,1,0:T(8,128)(2,1)}), bf16[16,216,128]{2,1,0:T(8,128)(2,1)S(1)}, u32[]{:S(2)}, u32[]{:S(2)}) async-start(bf16[16,216,128]{2,1,0:T(8,128)(2,1)} %shard_map.74), calls=%async_computation | async-start | bytes 1769472 | tf_op jit(solution)/shard_map/all_to_all | solution.py:402
  48.1 1.9 %collective-permute-start.5 = (bf16[4,2,32,128]{3,2,1,0:T(8,128)(2,1)S(1)}, bf16[4,2,32,128]{3,2,1,0:T(8,128)(2,1)S(1)}, u32[]{:S(2)}, u32[]{:S(2)}) collective-permute-start(bf16[4,2,32,128]{3,2,1,0:T(8,128)(2,1)S(1)} %get-tuple-element.15.own_ref.grad_ref), channel_id=1, source_target_pairs={{32,0},{64,32},{96,64},{128,96},{160,128},{192,160},{224,192},{256... | collective-permute-start | bytes 196616 | tf_op jit(solution)/shard_map/ppermute | solution.py:317
  50.0 4.3 %collective-permute-done.5.later_ref = bf16[4,2,32,128]{3,2,1,0:T(8,128)(2,1)S(1)} collective-permute-done((bf16[4,2,32,128]{3,2,1,0:T(8,128)(2,1)S(1)}, bf16[4,2,32,128]{3,2,1,0:T(8,128)(2,1)S(1)}, u32[]{:S(2)}, u32[]{:S(2)}) %collective-permute-start.5) | collective-permute-done | bytes 65568 | tf_op jit(solution)/shard_map/ppermute | solution.py:317
  54.3 1.9 %collective-permute-start.6 = (bf16[2,4,32,128]{3,2,1,0:T(8,128)(2,1)S(1)}, bf16[2,4,32,128]{3,2,1,0:T(8,128)(2,1)S(1)}, u32[]{:S(2)}, u32[]{:S(2)}) collective-permute-start(bf16[2,4,32,128]{3,2,1,0:T(8,128)(2,1)S(1)} %shard_map.70), channel_id=1, source_target_pairs={{0,1},{1,2},{2,3},{3,4},{4,5},{5,6},{6,7},{7,8},{8,9},{9,10},{10,1... | collective-permute-start | bytes 196616 | tf_op jit(solution)/shard_map/ppermute | solution.py:323
  56.2 15.4 %collective-permute-done.6.above_ref = bf16[2,4,32,128]{3,2,1,0:T(8,128)(2,1)S(1)} collective-permute-done((bf16[2,4,32,128]{3,2,1,0:T(8,128)(2,1)S(1)}, bf16[2,4,32,128]{3,2,1,0:T(8,128)(2,1)S(1)}, u32[]{:S(2)}, u32[]{:S(2)}) %collective-permute-start.6) | collective-permute-done | bytes 65568 | tf_op jit(solution)/shard_map/ppermute | solution.py:323
  71.6 1.3 %shard_map.71 = (bf16[2,4,32,128]{3,2,1,0:T(8,128)(2,1)}, f32[8,128]{1,0:T(8,128)S(1)}) custom-call(bf16[4,2,32,128]{3,2,1,0:T(8,128)(2,1)S(1)} %get-tuple-element.15.own_ref.grad_ref, bf16[4,2,32,128]{3,2,1,0:T(8,128)(2,1)S(1)} %collective-permute-done.5.later_ref, bf16[2,4,32,128]{3,2,1,0:T(8,128)(2,1)S(1)} %collective-permute-done.6.above_ref, ...), custom_call_target="tpu_custom_call" | custom-call | tf_op jit(solution)/shard_map/pallas_call | solution.py:18
  72.9 1.0 all-to-all-done.refs_0_
  73.9 0.3 shard_map.75
  74.2 22.5 %all_to_all.10.refs_0_ = bf16[16,8,256]{2,1,0:T(8,128)(2,1)S(1)} all-to-all(bf16[16,8,256]{2,1,0:T(8,128)(2,1)S(1)} %shard_map.75), channel_id=1, replica_groups=mesh['frame'=16,'tile'=32] {'frame'}, dimensions={0} | all-to-all | bytes 131072 | tf_op jit(solution)/shard_map/all_to_all | solution.py:420
  96.7 0.7 shard_map.76
  (1 shorter events, 0.0 us)
Async XLA Ops:
  2.4 15.3 %collective-permute-start.2 = (bf16[2,8,32,128]{3,2,1,0:T(8,128)(2,1)S(1)}, bf16[2,8,32,128]{3,2,1,0:T(8,128)(2,1)S(1)}, u32[]{:S(2)}, u32[]{:S(2)}) collective-permute-start(bf16[2,8,32,128]{3,2,1,0:T(8,128)(2,1)S(1)} %pad_maximum_fusion.joined_ref), channel_id=1, source_target_pairs={{32,0},{64,32},{96,64},{128,96},{160,128},{192,160},{224,192},{256... | collective-permute-start | bytes 393224 | tf_op jit(solution)/shard_map/ppermute | solution.py:317
  10.2 4.5 %collective-permute-start.1 = (bf16[2,4,32,128]{3,2,1,0:T(8,128)(2,1)S(1)}, bf16[2,4,32,128]{3,2,1,0:T(8,128)(2,1)S(1)}, u32[]{:S(2)}, u32[]{:S(2)}) collective-permute-start(bf16[2,4,32,128]{3,2,1,0:T(8,128)(2,1)S(1)} %multiply_convert_fusion.own_ref), channel_id=1, source_target_pairs={{0,64},{32,96},{64,128},{96,160},{128,192},{160,224},{192,256},{22... | collective-permute-start | bytes 196616 | tf_op jit(solution)/shard_map/ppermute | solution.py:314
  11.5 6.2 %collective-permute-start = (bf16[2,4,32,128]{3,2,1,0:T(8,128)(2,1)S(1)}, bf16[2,4,32,128]{3,2,1,0:T(8,128)(2,1)S(1)}, u32[]{:S(2)}, u32[]{:S(2)}) collective-permute-start(bf16[2,4,32,128]{3,2,1,0:T(8,128)(2,1)S(1)} %multiply_convert_fusion.own_ref), channel_id=1, source_target_pairs={{0,32},{32,64},{64,96},{96,128},{128,160},{160,192},{192,224},{224... | collective-permute-start | bytes 196616 | tf_op jit(solution)/shard_map/ppermute | solution.py:314
  17.8 12.6 %collective-permute-start.3 = (bf16[40,32,128]{2,1,0:T(8,128)(2,1)S(1)}, bf16[40,32,128]{2,1,0:T(8,128)(2,1)S(1)}, u32[]{:S(2)}, u32[]{:S(2)}) collective-permute-start(bf16[40,32,128]{2,1,0:T(8,128)(2,1)S(1)} %get-tuple-element.13), channel_id=1, source_target_pairs={{1,0},{2,1},{3,2},{4,3},{5,4},{6,5},{7,6},{8,7},{9,8},{10,9},{11,1... | collective-permute-start | bytes 983048 | tf_op jit(solution)/shard_map/ppermute | solution.py:320
  21.9 8.4 %copy-start = (f32[2,128]{1,0:T(2,128)S(1)}, f32[2,128]{1,0:T(2,128)}, u32[]{:S(2)}) copy-start(f32[2,128]{1,0:T(2,128)} %gain_ref.1) | copy-start | bytes 3076
  21.9 8.4 %collective-permute-start.4 = (bf16[16,32,128]{2,1,0:T(8,128)(2,1)S(1)}, bf16[16,32,128]{2,1,0:T(8,128)(2,1)S(1)}, u32[]{:S(2)}, u32[]{:S(2)}) collective-permute-start(bf16[16,32,128]{2,1,0:T(8,128)(2,1)S(1)} %get-tuple-element.14), channel_id=1, source_target_pairs={{0,1},{1,2},{2,3},{3,4},{4,5},{5,6},{6,7},{7,8},{8,9},{9,10},{10,1... | collective-permute-start | bytes 393224 | tf_op jit(solution)/shard_map/ppermute | solution.py:323
  37.9 4.3 %collective-permute-start.7 = (bf16[16,54,4,128]{3,2,1,0:T(4,128)(2,1)S(1)}, bf16[16,54,4,128]{3,2,1,0:T(4,128)(2,1)S(1)}, u32[]{:S(2)}, u32[]{:S(2)}) collective-permute-start(bf16[16,54,4,128]{3,2,1,0:T(4,128)(2,1)S(1)} %get-tuple-element.22), channel_id=1, source_target_pairs={{0,1},{1,0},{2,3},{3,2},{4,5},{5,4},{6,7},{7,6},{8,9},{9,8},{10,11... | collective-permute-start | bytes 2654216 | tf_op jit(solution)/shard_map/ppermute | solution.py:326
  43.4 30.5 %all-to-all-start = ((bf16[16,216,128]{2,1,0:T(8,128)(2,1)}), bf16[16,216,128]{2,1,0:T(8,128)(2,1)S(1)}, u32[]{:S(2)}, u32[]{:S(2)}) async-start(bf16[16,216,128]{2,1,0:T(8,128)(2,1)} %shard_map.74), calls=%async_computation | async-start | bytes 1769472 | tf_op jit(solution)/shard_map/all_to_all | solution.py:402
  48.1 6.2 %collective-permute-start.5 = (bf16[4,2,32,128]{3,2,1,0:T(8,128)(2,1)S(1)}, bf16[4,2,32,128]{3,2,1,0:T(8,128)(2,1)S(1)}, u32[]{:S(2)}, u32[]{:S(2)}) collective-permute-start(bf16[4,2,32,128]{3,2,1,0:T(8,128)(2,1)S(1)} %get-tuple-element.15.own_ref.grad_ref), channel_id=1, source_target_pairs={{32,0},{64,32},{96,64},{128,96},{160,128},{192,160},{224,192},{256... | collective-permute-start | bytes 196616 | tf_op jit(solution)/shard_map/ppermute | solution.py:317
  54.3 17.3 %collective-permute-start.6 = (bf16[2,4,32,128]{3,2,1,0:T(8,128)(2,1)S(1)}, bf16[2,4,32,128]{3,2,1,0:T(8,128)(2,1)S(1)}, u32[]{:S(2)}, u32[]{:S(2)}) collective-permute-start(bf16[2,4,32,128]{3,2,1,0:T(8,128)(2,1)S(1)} %shard_map.70), channel_id=1, source_target_pairs={{0,1},{1,2},{2,3},{3,4},{4,5},{5,6},{6,7},{7,8},{8,9},{9,10},{10,1... | collective-permute-start | bytes 196616 | tf_op jit(solution)/shard_map/ppermute | solution.py:323
